TPU v7x, 256 devices: a whole 4x4x8 slice. The times are simulated.
256 devices in a mesh: band: 16 (over x_hi, z), grid: 16 (over y, x_lo, core).
Axes of the slice: x: 4 (x_hi: 2, x_lo: 2; x = x_hi * 2 + x_lo), y: 4, z: 8, core: 2. Of those that a mesh axis runs over, the one named last changes fastest.
Arguments:
- partial_density: float32 [16, 128, 128, 128], P('band', 'grid'), may hold values from 0.01 to 1
- node_index: int32 [128, 128, 128], P('grid'), may hold values from 0 to 19
- node_weight: float32 [4, 128, 128, 128], P(None, 'grid'), may hold values from 0 to 1
- node_slope: float32 [4, 128, 128, 128], P(None, 'grid'), may hold values from -6 to 6
- kernel_table: float32 [20, 20, 114], replicated, may hold values from -0.8 to 0.8, as said below
Outputs:
- potential: float32 [128, 128, 128], P('grid')
Inputs may be any that keep to these rules, and one draw needn't show every extreme that they name: node_index(r) is the node at the lower end of the interval of q0 at r; nodes node_index - 1 to node_index + 2 carry the four weights. `kernel_table`: symmetric in its first two indices.
All inputs are finite; a program needn't handle non-finite values.
Results may differ from a plain program's by a relative error of at most 0.0003.
Values sent between devices are 32-bit elements; how exact they have to be, the bound alone decides.
No kernel may reach another device: no remote copies, remote signals or barrier semaphores. Data moves between devices by JAX's collectives and lax.ppermute only.
A program may use at most 64 MiB of HBM per device.

v0:
```python
import math

import jax
import jax.numpy as jnp
from jax import lax
from jax.sharding import PartitionSpec as P

N = 128


def in_blocks(x, dim, size):
    before, after = (x.shape[:dim], x.shape[dim + 1 :])
    return jnp.moveaxis(x.reshape(*before, size, -1, *after), dim, 0)


def summed_on_arrival(x, axis, dim):
    size = lax.axis_size(axis)
    parts = lax.all_to_all(in_blocks(x, dim, size), axis, 0, 0, tiled=True)
    return jnp.sum(parts, axis=0)


def filled_up(lines, size):
    spare = -len(lines) % size
    return jnp.pad(lines, [(0, spare)] + [(0, 0)] * (lines.ndim - 1))


def sent_to_all(x, axis):
    size = lax.axis_size(axis)
    return lax.all_to_all(jnp.broadcast_to(x[None], (size, *x.shape)), axis, 0, 0, tiled=True)


def in_order(parts, dim):
    parts = jnp.moveaxis(parts, 0, dim)
    dims = parts.shape
    return parts.reshape(*dims[:dim], dims[dim] * dims[dim + 1], *dims[dim + 2 :])


def collect(x, axis, dim):
    parts = sent_to_all(x, axis)
    return in_order(parts, dim)


def sum_by_parts(x, axes):
    lines = x.reshape(-1, x.shape[-1])
    padded = filled_up(lines, lax.axis_size(axes))
    whole = collect(summed_on_arrival(padded, axes, 0), axes, 0)
    return lax.slice_in_dim(whole, 0, len(lines)).reshape(x.shape)


def frequency_of(positions, length):
    return jnp.where(positions < length // 2, positions, positions - length)


def shell_split(square_norm):
    root_value = jnp.sqrt(square_norm.astype(jnp.float32))
    shell_idx = root_value.astype(jnp.int32)
    shell_idx = shell_idx - (shell_idx * shell_idx > square_norm).astype(jnp.int32)
    shell_idx = shell_idx + ((shell_idx + 1) * (shell_idx + 1) <= square_norm).astype(jnp.int32)
    fraction = root_value - shell_idx.astype(jnp.float32)
    return (shell_idx, fraction)


def node_fields(count_nodes, intervals, weights):
    node_ids = jnp.arange(count_nodes, dtype=jnp.int32)
    summed = jnp.zeros((count_nodes,) + intervals.shape, jnp.float32)
    for offset in range(4):
        matched = node_ids[:, None, None, None] == (intervals + (offset - 1))[None]
        summed = summed + jnp.where(matched, weights[offset][None], jnp.zeros((), jnp.float32))
    return summed


def phase_table(source_idx, target_idx, modulus):
    product_mod = source_idx[:, None] * target_idx[None, :] % modulus
    angles = product_mod.astype(jnp.float32) * (2.0 * math.pi / modulus)
    return (jnp.cos(angles), jnp.sin(angles))


def contract(pattern, operand, matrix):
    return jnp.einsum(pattern, operand, matrix, precision=lax.Precision.HIGHEST)


def mirrored(values, dim):
    return jnp.roll(jnp.flip(values, dim), 1, dim)


def forward_tables(positions, plane_ids, length):
    cosine, sine = phase_table(positions, plane_ids, length)
    alternating = jnp.where(positions % 2 == 0, 1.0, -1.0).astype(jnp.float32)
    sine = jnp.where(plane_ids[None, :] == 0, -alternating[:, None], sine)
    return (cosine, sine)


def shell_weights_of(square_norm, shell_count):
    shell_ids = jnp.arange(shell_count, dtype=jnp.int32)
    shell_idx, fraction = shell_split(square_norm)
    expand = (slice(None),) + (None,) * square_norm.ndim
    lower_hit = shell_ids[expand] == shell_idx[None]
    upper_hit = shell_ids[expand] == shell_idx[None] + 1
    return jnp.where(lower_hit, 1.0 - fraction[None], 0.0) + jnp.where(
        upper_hit, fraction[None], 0.0
    )


def per_device(partial_density, node_index, node_weight, node_slope, kernel_table):
    length = N
    half = length // 2
    count_nodes = kernel_table.shape[0]
    shell_count = kernel_table.shape[2]
    band_part = length // lax.axis_size("band")
    planes = half // lax.axis_size("band")
    grid_part = length // lax.axis_size("grid")
    band_at = lax.axis_index("band")
    grid_at = lax.axis_index("grid")
    full_range = jnp.arange(length, dtype=jnp.int32)
    half_range = jnp.arange(half, dtype=jnp.int32)
    own_planes = band_at * planes + jnp.arange(planes, dtype=jnp.int32)
    own_rows = grid_at * grid_part + jnp.arange(grid_part, dtype=jnp.int32)
    first_band = band_at == 0
    lower_rows = (full_range >= 1) & (full_range < half)
    upper_rows = full_range > half
    density = summed_on_arrival(partial_density[0], "band", 1)
    rows_index = lax.dynamic_slice_in_dim(node_index, band_at * band_part, band_part, 1)
    rows_weight = lax.dynamic_slice_in_dim(node_weight, band_at * band_part, band_part, 2)
    theta_fields = density[None] * node_fields(count_nodes, rows_index, rows_weight)
    cosine_z, sine_z = forward_tables(full_range, half_range, length)
    forward_real = contract("axyz,zk->axyk", theta_fields, cosine_z)
    forward_imag = -contract("axyz,zk->axyk", theta_fields, sine_z)
    columns = lax.all_to_all(
        jnp.stack([forward_real, forward_imag]), "band", split_axis=4, concat_axis=3, tiled=True
    )
    cosine_full, sine_full = phase_table(full_range, full_range, length)
    y_cos = contract("caxyp,yw->caxpw", columns, cosine_full)
    y_sin = contract("caxyp,yw->caxpw", columns, sine_full)
    ywave_real = y_cos[0] + y_sin[1]
    ywave_imag = y_cos[1] - y_sin[0]
    first_real = ywave_real[:, :, 0, :]
    first_imag = ywave_imag[:, :, 0, :]
    turned_real = mirrored(first_real, 2)
    turned_imag = mirrored(first_imag, 2)
    packed_real = jnp.where(
        lower_rows,
        0.5 * (first_real + turned_real),
        jnp.where(upper_rows, 0.5 * (turned_imag + first_imag), first_real),
    )
    packed_imag = jnp.where(
        lower_rows,
        0.5 * (first_imag - turned_imag),
        jnp.where(upper_rows, 0.5 * (first_real - turned_real), first_imag),
    )
    ywave_real = ywave_real.at[:, :, 0, :].set(jnp.where(first_band, packed_real, first_real))
    ywave_imag = ywave_imag.at[:, :, 0, :].set(jnp.where(first_band, packed_imag, first_imag))
    pencils = lax.all_to_all(
        jnp.stack([ywave_real, ywave_imag]), "grid", split_axis=4, concat_axis=2, tiled=True
    )
    x_cos = contract("caxpw,xv->capwv", pencils, cosine_full)
    x_sin = contract("caxpw,xv->capwv", pencils, sine_full)
    spec_real = x_cos[0] + x_sin[1]
    spec_imag = x_cos[1] - x_sin[0]
    freq_x = frequency_of(full_range, length)
    square_x = freq_x * freq_x
    freq_rows = frequency_of(own_rows, length)
    plane_square = own_planes * own_planes
    third_square = jnp.where(
        (own_planes[:, None] == 0) & (own_rows[None, :] > half), half * half, plane_square[:, None]
    )
    special_rows = ((own_rows == 0) | (own_rows == half)) & (own_planes[0] == 0)

    def mix_row(row_idx):
        row_real = lax.dynamic_index_in_dim(spec_real, row_idx, 2, keepdims=False)
        row_imag = lax.dynamic_index_in_dim(spec_imag, row_idx, 2, keepdims=False)
        freq_row = lax.dynamic_index_in_dim(freq_rows, row_idx, 0, keepdims=False)
        third_row = lax.dynamic_index_in_dim(third_square, row_idx, 1, keepdims=False)
        square_norm = third_row[:, None] + square_x[None, :] + freq_row * freq_row
        kernel = contract("abs,spx->abpx", kernel_table, shell_weights_of(square_norm, shell_count))
        out_real = contract("abpx,apx->bpx", kernel, row_real)
        out_imag = contract("abpx,apx->bpx", kernel, row_imag)
        other_norm = square_x + freq_row * freq_row + half * half
        kernel_other = contract(
            "abs,sx->abx", kernel_table, shell_weights_of(other_norm, shell_count)
        )
        flag = lax.dynamic_index_in_dim(special_rows, row_idx, 0, keepdims=False).astype(
            jnp.float32
        )
        spread = 0.5 * flag * (kernel[:, :, 0, :] - kernel_other)
        base_real = row_real[:, 0, :]
        base_imag = row_imag[:, 0, :]
        delta_real = mirrored(base_real, 1) - base_real
        delta_imag = -mirrored(base_imag, 1) - base_imag
        out_real = out_real.at[:, 0, :].add(contract("abx,ax->bx", spread, delta_real))
        out_imag = out_imag.at[:, 0, :].add(contract("abx,ax->bx", spread, delta_imag))
        return jnp.stack([out_real, out_imag])

    mixed = lax.map(mix_row, jnp.arange(grid_part, dtype=jnp.int32))
    i_cos = contract("wcbpx,xv->wcbpv", mixed, cosine_full)
    i_sin = contract("wcbpx,xv->wcbpv", mixed, sine_full)
    inverse_real = i_cos[:, 0] - i_sin[:, 1]
    inverse_imag = i_cos[:, 1] + i_sin[:, 0]
    returned = lax.all_to_all(
        jnp.stack([inverse_real, inverse_imag], axis=1),
        "grid",
        split_axis=4,
        concat_axis=0,
        tiled=True,
    )
    lower_col = lower_rows[:, None, None]
    upper_col = upper_rows[:, None, None]
    back_real = returned[:, 0, :, 0, :]
    back_imag = returned[:, 1, :, 0, :]
    flip_real = mirrored(back_real, 0)
    flip_imag = mirrored(back_imag, 0)
    joined_real = jnp.where(
        lower_col, back_real - flip_imag, jnp.where(upper_col, flip_real + back_imag, back_real)
    )
    joined_imag = jnp.where(
        lower_col, back_imag + flip_real, jnp.where(upper_col, back_real - flip_imag, back_imag)
    )
    returned = returned.at[:, 0, :, 0, :].set(jnp.where(first_band, joined_real, back_real))
    returned = returned.at[:, 1, :, 0, :].set(jnp.where(first_band, joined_imag, back_imag))
    b_cos = contract("wcbpx,wy->cbpxy", returned, cosine_full)
    b_sin = contract("wcbpx,wy->cbpxy", returned, sine_full)
    slab_real = b_cos[0] - b_sin[1]
    slab_imag = b_cos[1] + b_sin[0]
    cosine_own, sine_own = phase_table(own_planes, full_range, length)
    alternating = jnp.where(full_range % 2 == 0, 1.0, -1.0).astype(jnp.float32)
    cosine_back = jnp.where(own_planes[:, None] == 0, 1.0, 2.0 * cosine_own)
    sine_back = jnp.where(own_planes[:, None] == 0, -alternating[None, :], 2.0 * sine_own)
    scale_factor = 1.0 / float(length) ** 3
    field_parts = (
        contract("bpxy,pz->bxyz", slab_real, cosine_back)
        - contract("bpxy,pz->bxyz", slab_imag, sine_back)
    ) * scale_factor
    slopes = node_fields(count_nodes, node_index, node_slope)
    partial_potential = jnp.sum(field_parts * slopes, axis=0)
    return sum_by_parts(partial_potential, "band")


def solution(mesh):
    placed = (
        P("band", "grid", None, None),
        P("grid", None, None),
        P(None, "grid", None, None),
        P(None, "grid", None, None),
        P(),
    )
    return jax.shard_map(
        per_device, mesh=mesh, in_specs=placed, out_specs=P("grid", None, None), check_vma=False
    )
```

profile of v0, /device:TPU:2, one launch (start us, length us, event | category | flops | bytes accessed | tf_op | source)
XLA Modules:
  0.0 350.1 jit_solution(8504545347986841677)
XLA Ops:
  0.0 1.9 copy.148
  1.9 10.1 %all-to-all-start = ((f32[16,8,8,128]{3,2,1,0:T(8,128)}), f32[16,8,8,128]{3,2,1,0:T(8,128)S(1)}, u32[]{:S(2)}, u32[]{:S(2)}) async-start(f32[16,8,8,128]{3,2,1,0:T(8,128)} %copy.148), calls=%async_computation | async-start | bytes 1048576 | tf_op jit(solution)/shard_map/all_to_all | solution.py:18
  12.1 0.8 broadcast_add_fusion.7
  12.8 0.8 dynamic-slice_bitcast_fusion.3
  13.7 15.5 %all-to-all-done = f32[16,8,8,128]{3,2,1,0:T(8,128)S(1)} async-done(((f32[16,8,8,128]{3,2,1,0:T(8,128)}), f32[16,8,8,128]{3,2,1,0:T(8,128)S(1)}, u32[]{:S(2)}, u32[]{:S(2)}) %all-to-all-start) | async-done | bytes 524320 | tf_op jit(solution)/shard_map/all_to_all | solution.py:18
  29.2 1.0 convolution_bitcast_fusion.1
  30.2 1.0 fusion.45
  31.3 4.6 %copy.149 = f32[2,20,8,8,64]{1,3,2,0,4:T(8,128)} copy(f32[2,20,8,8,64]{4,3,2,1,0:T(8,128)S(1)} %pad_maximum_fusion) | data formatting | bytes 1310720 | tf_op jit(solution)/shard_map/stack | solution.py:129
  36.0 6.5 %reshape.675 = f32[16,1,10240]{2,1,0:T(1,128)} reshape(f32[64,2,8,8,20]{4,3,2,1,0:T(8,128)} %bitcast.336) | data formatting | bytes 1310720
  42.5 4.8 %all-to-all-start.1 = ((f32[16,1,10240]{2,1,0:T(1,128)}), f32[16,1,10240]{2,1,0:T(1,128)S(1)}, u32[]{:S(2)}, u32[]{:S(2)}) async-start(f32[16,1,10240]{2,1,0:T(1,128)} %reshape.675), calls=%async_computation.1 | async-start | bytes 1310720 | tf_op jit(solution)/shard_map/all_to_all | solution.py:128
  47.3 19.6 %all-to-all-done.1 = f32[16,1,10240]{2,1,0:T(1,128)S(1)} async-done(((f32[16,1,10240]{2,1,0:T(1,128)}), f32[16,1,10240]{2,1,0:T(1,128)S(1)}, u32[]{:S(2)}, u32[]{:S(2)}) %all-to-all-start.1) | async-done | bytes 655392 | tf_op jit(solution)/shard_map/all_to_all | solution.py:128
  67.4 2.1 reduce.21
  69.5 6.2 %reshape.676 = f32[64,2,8,8,20]{4,3,2,1,0:T(8,128)} reshape(f32[16,10240]{1,0:T(8,128)S(1)} %reduce.21) | data formatting | bytes 1310720
  75.7 8.7 %fusion.39 = f32[2,20,8,4,128]{4,1,3,2,0:T(8,128)S(1)} fusion(f32[2,20,8,16,8,4]{1,4,2,0,5,3:T(8,128)} %bitcast.327), kind=kOutput, calls=%fused_computation.79 | convolution fusion | flops 251887616 | bytes 1310720 | tf_op jit(solution)/shard_map/caxyp,yw->caxpw/dot_general | solution.py:79
  84.4 6.7 %fusion.41 = f32[2,20,8,4,128]{4,1,3,2,0:T(8,128)S(1)} fusion(f32[2,20,8,16,8,4]{1,4,2,0,5,3:T(8,128)S(1)} %bitcast.328), kind=kOutput, calls=%fused_computation.81 | convolution fusion | flops 251887616 | bytes 1310720 | tf_op jit(solution)/shard_map/caxyp,yw->caxpw/dot_general | solution.py:79
  92.0 4.9 %copy.161 = f32[2,20,8,4,128]{1,2,3,0,4:T(8,128)} copy(f32[2,20,8,4,128]{4,1,3,2,0:T(8,128)S(1)} %pad_maximum_fusion.1) | data formatting | bytes 1310720 | tf_op jit(solution)/shard_map/stack | solution.py:153
  96.9 6.5 %reshape.677 = f32[16,1,10240]{2,1,0:T(1,128)} reshape(f32[128,2,4,8,20]{4,3,2,1,0:T(8,128)} %bitcast.334) | data formatting | bytes 1310720
  103.4 5.9 %all-to-all-start.2 = ((f32[16,1,10240]{2,1,0:T(1,128)}), f32[16,1,10240]{2,1,0:T(1,128)S(1)}, u32[]{:S(2)}, u32[]{:S(2)}) async-start(f32[16,1,10240]{2,1,0:T(1,128)} %reshape.677), calls=%async_computation.2 | async-start | bytes 1310720 | tf_op jit(solution)/shard_map/all_to_all | solution.py:152
  109.5 10.9 %all-to-all-done.2 = f32[16,1,10240]{2,1,0:T(1,128)S(1)} async-done(((f32[16,1,10240]{2,1,0:T(1,128)}), f32[16,1,10240]{2,1,0:T(1,128)S(1)}, u32[]{:S(2)}, u32[]{:S(2)}) %all-to-all-start.2) | async-done | bytes 655392 | tf_op jit(solution)/shard_map/all_to_all | solution.py:152
  120.4 2.1 reduce.22
  122.5 6.2 %reshape.678 = f32[128,2,4,8,20]{4,3,2,1,0:T(8,128)} reshape(f32[16,10240]{1,0:T(8,128)S(1)} %reduce.22) | data formatting | bytes 1310720
  128.7 7.9 %copy.163 = f32[2,20,16,8,4,8]{1,5,4,3,2,0:T(8,128)} copy(f32[2,20,16,8,4,8]{1,3,4,0,5,2:T(8,128)} %bitcast.337) | data formatting | bytes 1310720 | tf_op jit(solution)/shard_map/all_to_all | solution.py:152
  136.7 4.0 %copy.164 = f32[2,20,128,4,8]{2,4,3,1,0:T(8,128)S(1)} copy(f32[2,20,128,4,8]{1,4,3,2,0:T(8,128)} %bitcast.338) | data formatting | bytes 1310720 | tf_op jit(solution)/shard_map/all_to_all | solution.py:152
  140.7 0.9 fusion.93
  141.6 0.9 fusion.99
  142.7 67.2 %while.20 = (s32[]{:T(128)}, f32[8,2,20,4,128]{4,3,2,1,0:T(4,128)S(1)}, s32[8]{0:T(128)S(1)}, f32[20,4,8,128]{3,2,1,0:T(8,128)S(1)}, s32[4,8]{0,1:T(8,128)S(1)},...) while((s32[]{:T(128)}, ...), condition=%wide.region_2.3_spmd.clone.clone, body=%wide.region_1.2_spmd.clone.clone.sunk | while | flops 351732736 | bytes 2762182 | solution.py:193
  147.6 1.1 multiply_reduce_fusion.7
  149.2 0.6 dynamic_slice.77
  155.9 1.1 multiply_reduce_fusion.7
  157.6 0.6 dynamic_slice.77
  164.3 1.1 multiply_reduce_fusion.7
  166.0 0.6 dynamic_slice.77
  172.7 1.1 multiply_reduce_fusion.7
  174.4 0.6 dynamic_slice.77
  181.1 1.1 multiply_reduce_fusion.7
  182.8 0.6 dynamic_slice.77
  189.4 1.1 multiply_reduce_fusion.7
  191.1 0.6 dynamic_slice.77
  197.8 1.1 multiply_reduce_fusion.7
  199.5 0.6 dynamic_slice.77
  206.2 1.1 multiply_reduce_fusion.7
  207.9 0.6 dynamic_slice.77
  209.9 1.0 fusion.46
  210.9 1.0 fusion.48
  212.1 3.5 copy.168
  215.5 7.5 %reshape.679 = f32[16,1,10240]{2,1,0:T(1,128)} reshape(f32[128,8,2,4,20]{4,3,2,1,0:T(4,128)} %bitcast.335) | data formatting | bytes 1310720
  223.0 5.0 %all-to-all-start.3 = ((f32[16,1,10240]{2,1,0:T(1,128)}), f32[16,1,10240]{2,1,0:T(1,128)S(1)}, u32[]{:S(2)}, u32[]{:S(2)}) async-start(f32[16,1,10240]{2,1,0:T(1,128)} %reshape.679), calls=%async_computation.3 | async-start | bytes 1310720 | tf_op jit(solution)/shard_map/all_to_all | solution.py:198
  228.0 1.2 broadcast_add_fusion.4
  229.2 1.4 slice_bitcast_fusion.6
  230.6 8.4 %all-to-all-done.3 = f32[16,1,10240]{2,1,0:T(1,128)S(1)} async-done(((f32[16,1,10240]{2,1,0:T(1,128)}), f32[16,1,10240]{2,1,0:T(1,128)S(1)}, u32[]{:S(2)}, u32[]{:S(2)}) %all-to-all-start.3) | async-done | bytes 655392 | tf_op jit(solution)/shard_map/all_to_all | solution.py:198
  239.0 2.1 reduce.23
  241.1 7.2 %reshape.680 = f32[128,8,2,4,20]{4,3,2,1,0:T(4,128)} reshape(f32[16,10240]{1,0:T(8,128)S(1)} %reduce.23) | data formatting | bytes 1310720
  248.3 4.6 %copy.262 = f32[8,2,20,4,128]{2,4,3,1,0:T(8,128)S(1)} copy(f32[8,2,20,4,128]{2,3,1,0,4:T(4,128)} %bitcast.339) | data formatting | bytes 1310720 | tf_op jit(solution)/shard_map/all_to_all | solution.py:198
  253.7 1.9 copy.294
  255.9 2.2 select_dynamic-update-slice_fusion.1
  258.1 1.2 select_dynamic-update-slice_fusion
  259.4 4.2 %copy.173 = f32[128,2,20,4,8]{0,4,3,2,1:T(8,128)S(1)} copy(f32[128,2,20,4,8]{2,4,3,1,0:T(8,128)} %select_dynamic-update-slice_fusion) | data formatting | bytes 1310720 | tf_op jit(solution)/shard_map/scatter | solution.py:218
  263.6 0.9 fusion.90
  264.5 0.9 fusion.96
  265.6 16.9 %fusion.55 = f32[20,8,128,128]{3,2,1,0:T(8,128)S(1)} fusion(f32[20,4,8,128]{3,2,1,0:T(8,128)S(1)} %get-tuple-element.302, s32[4]{0:T(128)S(1)} %get-tuple-element.319, pred[4]{0:T(512)(128)(4,1)S(1)} %broadcast_compare_fusion), kind=kOutput, calls=%fused_computation.126 | convolution fusion | flops 125837312 | bytes 10813460 | tf_op jit(solution)/shard_map/bpxy,pz->bxyz/dot_general | solution.py:79
  282.6 23.0 %multiply_reduce_fusion.4 = f32[8,128,128]{2,1,0:T(8,128)S(1)} fusion(f32[20,8,128,128]{3,2,1,0:T(8,128)S(1)} %fusion.55, f32[8,128,128]{2,1,0:T(8,128)S(1)} %copy-done.10, s32[8,128,128]{2,1,0:T(8,128)S(1)} %copy-done.6, f32[8,128,128]{2,1,0:T(8,128)S(1)} %copy-done.11, s32[8,128,128]{2,1,0:T(8,128)S(1)} %copy-done.7, f32[8,128,128]{2,1,0:T(8,128)S(1)} %copy-done.9, ...), kind=kOutput, calls=%fused_computation.74 | convolution fusion | flops 165027840 | bytes 15532564 | tf_op jit(solution)/shard_map/bpxy,pz->bxyz/dot_general | solution.py:79
  305.7 21.6 %all_to_all.69 = f32[16,64,128]{2,1,0:T(8,128)S(1)} all-to-all(f32[16,64,128]{2,1,0:T(8,128)S(1)} %bitcast.359), channel_id=1, replica_groups=mesh['band'=16,'grid'=16] {'band'}, dimensions={0} | all-to-all | bytes 1048576 | tf_op jit(solution)/shard_map/all_to_all | solution.py:18
  327.3 21.8 %all_to_all.70 = f32[16,64,128]{2,1,0:T(8,128)S(1)} all-to-all(f32[16,64,128]{2,1,0:T(8,128)S(1)} %broadcast_in_dim.329), channel_id=1, replica_groups=mesh['band'=16,'grid'=16] {'band'}, dimensions={0} | all-to-all | bytes 1048576 | tf_op jit(solution)/shard_map/all_to_all | solution.py:29
  349.1 0.8 copy.297
  (312 shorter events, 24.5 us)
Async XLA Ops:
  1.9 27.3 %all-to-all-start = ((f32[16,8,8,128]{3,2,1,0:T(8,128)}), f32[16,8,8,128]{3,2,1,0:T(8,128)S(1)}, u32[]{:S(2)}, u32[]{:S(2)}) async-start(f32[16,8,8,128]{3,2,1,0:T(8,128)} %copy.148), calls=%async_computation | async-start | bytes 1048576 | tf_op jit(solution)/shard_map/all_to_all | solution.py:18
  42.5 24.4 %all-to-all-start.1 = ((f32[16,1,10240]{2,1,0:T(1,128)}), f32[16,1,10240]{2,1,0:T(1,128)S(1)}, u32[]{:S(2)}, u32[]{:S(2)}) async-start(f32[16,1,10240]{2,1,0:T(1,128)} %reshape.675), calls=%async_computation.1 | async-start | bytes 1310720 | tf_op jit(solution)/shard_map/all_to_all | solution.py:128
  75.7 8.7 %copy-start = (f32[64,2,8,8,20]{4,3,2,1,0:T(8,128)S(1)}, f32[64,2,8,8,20]{4,3,2,1,0:T(8,128)}, u32[]{:S(2)}) copy-start(f32[64,2,8,8,20]{4,3,2,1,0:T(8,128)} %reshape.676) | copy-start | bytes 1966084
  103.4 17.0 %all-to-all-start.2 = ((f32[16,1,10240]{2,1,0:T(1,128)}), f32[16,1,10240]{2,1,0:T(1,128)S(1)}, u32[]{:S(2)}, u32[]{:S(2)}) async-start(f32[16,1,10240]{2,1,0:T(1,128)} %reshape.677), calls=%async_computation.2 | async-start | bytes 1310720 | tf_op jit(solution)/shard_map/all_to_all | solution.py:152
  136.7 5.9 %copy-start.1 = (f32[20,20,114]{2,1,0:T(8,128)S(1)}, f32[20,20,114]{2,1,0:T(8,128)}, u32[]{:S(2)}) copy-start(f32[20,20,114]{2,1,0:T(8,128)} %param.23) | copy-start | bytes 547204
  215.5 12.4 %copy-start.3 = (s32[8,128,128]{2,1,0:T(8,128)S(1)}, s32[8,128,128]{2,1,0:T(8,128)}, u32[]{:S(2)}) copy-start(s32[8,128,128]{2,1,0:T(8,128)} %param.20) | copy-start | bytes 1572868
  215.5 13.7 %copy-start.2 = (f32[4,8,128,128]{3,2,1,0:T(8,128)S(1)}, f32[4,8,128,128]{3,2,1,0:T(8,128)}, u32[]{:S(2)}) copy-start(f32[4,8,128,128]{3,2,1,0:T(8,128)} %param.22) | copy-start | bytes 6291460
  223.0 16.0 %all-to-all-start.3 = ((f32[16,1,10240]{2,1,0:T(1,128)}), f32[16,1,10240]{2,1,0:T(1,128)S(1)}, u32[]{:S(2)}, u32[]{:S(2)}) async-start(f32[16,1,10240]{2,1,0:T(1,128)} %reshape.679), calls=%async_computation.3 | async-start | bytes 1310720 | tf_op jit(solution)/shard_map/all_to_all | solution.py:198
  265.5 17.0 %copy-start.4 = (s32[8,128,128]{2,1,0:T(8,128)S(1)}, s32[8,128,128]{2,1,0:T(8,128)}, u32[]{:S(2)}) copy-start(s32[8,128,128]{2,1,0:T(8,128)} %param.20) | copy-start | bytes 1572868
  265.5 17.0 %copy-start.5 = (s32[8,128,128]{2,1,0:T(8,128)S(1)}, s32[8,128,128]{2,1,0:T(8,128)}, u32[]{:S(2)}) copy-start(s32[8,128,128]{2,1,0:T(8,128)} %get-tuple-element.310) | copy-start | bytes 1572868
  265.6 17.0 %copy-start.6 = (s32[8,128,128]{2,1,0:T(8,128)S(1)}, s32[8,128,128]{2,1,0:T(8,128)}, u32[]{:S(2)}) copy-start(s32[8,128,128]{2,1,0:T(8,128)} %get-tuple-element.311) | copy-start | bytes 1572868
  265.6 17.0 %copy-start.7 = (s32[8,128,128]{2,1,0:T(8,128)S(1)}, s32[8,128,128]{2,1,0:T(8,128)}, u32[]{:S(2)}) copy-start(s32[8,128,128]{2,1,0:T(8,128)} %get-tuple-element.312) | copy-start | bytes 1572868
  265.6 17.0 %copy-start.8 = (f32[8,128,128]{2,1,0:T(8,128)S(1)}, f32[8,128,128]{2,1,0:T(8,128)}, u32[]{:S(2)}) copy-start(f32[8,128,128]{2,1,0:T(8,128)} %get-tuple-element.291) | copy-start | bytes 1572868
  265.6 17.0 %copy-start.9 = (f32[8,128,128]{2,1,0:T(8,128)S(1)}, f32[8,128,128]{2,1,0:T(8,128)}, u32[]{:S(2)}) copy-start(f32[8,128,128]{2,1,0:T(8,128)} %get-tuple-element.292) | copy-start | bytes 1572868
  265.6 17.0 %copy-start.10 = (f32[8,128,128]{2,1,0:T(8,128)S(1)}, f32[8,128,128]{2,1,0:T(8,128)}, u32[]{:S(2)}) copy-start(f32[8,128,128]{2,1,0:T(8,128)} %get-tuple-element.293) | copy-start | bytes 1572868
  265.6 17.0 %copy-start.11 = (f32[8,128,128]{2,1,0:T(8,128)S(1)}, f32[8,128,128]{2,1,0:T(8,128)}, u32[]{:S(2)}) copy-start(f32[8,128,128]{2,1,0:T(8,128)} %get-tuple-element.294) | copy-start | bytes 1572868
where the time goes:
time: 357 us; the launch traced here: 350 us
  local copies, waits for them, and re-layouts  102 us (29%)
  matrix products  75 us (21%)
  waiting for transfers between devices  54.5 us (15%)
  blocking collectives  43.4 us (12%)
  loops' own time  31.9 us (9%)
  starting transfers between devices  25.8 us (7%)
  other arithmetic  16.6 us (5%)
    dot_general x28, matrix products, contract(): return jnp.einsum(pattern, operand, matrix, precision=lax.Precision.HIGHEST)  75 us
    unnamed x33, local copies, waits for them, and re-layouts  42.9 us
    another operation x1, loops' own time, per_device(): mixed = lax.map(mix_row, jnp.arange(grid_part, dtype=jnp.int32))  31.9 us
    all_to_all x1, blocking collectives, sent_to_all(): lax.all_to_all(jnp.broadcast_to(x[None], (size, *x.shape)), axis, 0, 0, t...  21.8 us
    all_to_all x1, blocking collectives, summed_on_arrival(): parts = lax.all_to_all(in_blocks(x, dim, size), axis, 0, 0, tiled=True)  21.6 us
    all_to_all x1, waiting for transfers between devices, per_device(): lax.all_to_all(jnp.stack([forward_real, forward_imag]), 'band', split_axi...  19.6 us
    all_to_all x1, waiting for transfers between devices, summed_on_arrival(): parts = lax.all_to_all(in_blocks(x, dim, size), axis, 0, 0, tiled=True)  15.5 us
    all_to_all x2, local copies, waits for them, and re-layouts, per_device(): lax.all_to_all(jnp.stack([ywave_real, ywave_imag]), 'grid', split_axis=4,...  11.9 us
  transfers between devices with their start and end apart: 4, of which 4 were waited for; matrix products, arithmetic and copies ran while one was open for 1% of the time, Pallas kernels for 0%

commit v1 on v0

v1 whole, which is shorter than its diff:
```python
import jax
import jax.numpy as jnp
import numpy as np
from jax import lax
from jax.experimental import pallas as pl
from jax.experimental.pallas import tpu as pltpu
from jax.sharding import PartitionSpec as P

N = 128
NA = 20
HALF_NA = 10
PAIRS = NA * (NA + 1) // 2
PAIR_ROWS = 216
POINTS = 64
ROWS = 5


def cas_table():
    idx = np.arange(N)
    angle = 2.0 * np.pi * ((idx[:, None] * idx[None, :]) % N) / N
    return np.cos(angle) + np.sin(angle)


def split_constant(table):
    high = jnp.asarray(table, jnp.float32).astype(jnp.bfloat16)
    low = (jnp.asarray(table, jnp.float32) - high.astype(jnp.float32)).astype(jnp.bfloat16)
    return jnp.stack([high, low])


def split_value(value):
    high = value.astype(jnp.bfloat16)
    low = (value - high.astype(jnp.float32)).astype(jnp.bfloat16)
    return high, low


def product(left, right, dims=((1,), (0,))):
    dot = lambda a, b: lax.dot_general(a, b, (dims, ((), ())), preferred_element_type=jnp.float32)
    return dot(left[0], right[0]) + (dot(left[0], right[1]) + dot(left[1], right[0]))


def node_sum(rel, fields, node):
    out = jnp.zeros_like(fields[0])
    for offset in range(4):
        out = jnp.where(rel == node - (offset - 1), fields[offset], out)
    return out


def frequency(positions):
    return jnp.where(positions < N // 2, positions, positions - N)


def phi_kernel(place_ref, table_ref, out_ref, flat_ref, shell_ref, fraction_ref, stage_ref):
    flat_ref[...] = jnp.zeros_like(flat_ref)
    start = 0
    for node in range(NA):
        count = NA - node
        flat_ref[start : start + count, 0 : table_ref.shape[2]] = table_ref[node, node:NA, :]
        start += count
    table = split_value(flat_ref[...])
    freq_y = frequency(place_ref[0])
    point = lax.broadcasted_iota(jnp.int32, (POINTS, N), 0)
    freq_z = frequency(point + place_ref[1] * POINTS)
    freq_x = frequency(lax.broadcasted_iota(jnp.int32, (POINTS, N), 1))
    square = freq_x * freq_x + freq_z * freq_z + freq_y * freq_y
    root = jnp.sqrt(square.astype(jnp.float32))
    shell = root.astype(jnp.int32)
    shell = shell - (shell * shell > square).astype(jnp.int32)
    shell = shell + ((shell + 1) * (shell + 1) <= square).astype(jnp.int32)
    shell_ref[...] = shell
    fraction_ref[...] = root - shell.astype(jnp.float32)
    row = lax.broadcasted_iota(jnp.int32, (N, N), 0)

    def weights(at):
        low = shell_ref[pl.ds(at, 1), :]
        part = fraction_ref[pl.ds(at, 1), :]
        return jnp.where(row == low, 1.0 - part, jnp.where(row == low + 1, part, 0.0))

    def group(step, carry):
        for pair in range(4):
            first = step * 8 + pair * 2
            both = jnp.concatenate([weights(first), weights(first + 1)], axis=1)
            value = product(table, split_value(both))
            stage_ref[pair * 2 * PAIR_ROWS : (pair * 2 + 1) * PAIR_ROWS, :] = value[:, :N]
            stage_ref[(pair * 2 + 1) * PAIR_ROWS : (pair * 2 + 2) * PAIR_ROWS, :] = value[:, N:]
        for item in range(PAIRS):
            out_ref[item, pl.ds(step * 8, 8), :] = stage_ref[pl.ds(item, 8, stride=PAIR_ROWS), :]
        return carry

    lax.fori_loop(0, POINTS // 8, group, 0)


def forward_kernel(place_ref, own_ref, other_ref, index_ref, weight_ref, cas_ref, out_ref):
    parity = place_ref[1]
    own, other = own_ref[...], other_ref[...]
    first = parity == 0
    density = jnp.concatenate([jnp.where(first, own, other), jnp.where(first, other, own)], axis=0)
    rel = index_ref[0] - parity * HALF_NA
    fields = [density * weight_ref[offset, 0] for offset in range(4)]
    cas = (cas_ref[0], cas_ref[1])
    lane = lax.broadcasted_iota(jnp.int32, (N, N), 1)
    for pair in range(ROWS):
        waves = []
        for node in (2 * pair, 2 * pair + 1):
            along_z = product(split_value(node_sum(rel, fields, node)), cas)
            waves.append(product(cas, split_value(along_z)))
        even, odd = waves
        out_ref[pl.ds(pair, N, stride=2 * ROWS), :] = jnp.where(
            lane < POINTS, even, pltpu.roll(odd, POINTS, 1)
        )
        out_ref[pl.ds(ROWS + pair, N, stride=2 * ROWS), :] = jnp.where(
            lane < POINTS, pltpu.roll(even, POINTS, 1), odd
        )


def mix_kernel(data_ref, cas_ref, phi_ref, out_ref, spec_ref, mixed_ref):
    cas = (cas_ref[0], cas_ref[1])

    def lines(half, pair, at):
        return pl.ds((at * 2 + half) * 16 * ROWS + pair, 16, stride=ROWS)

    for half in range(2):
        for pair in range(ROWS):
            block = jnp.concatenate([data_ref[lines(half, pair, at), :] for at in range(8)], axis=0)
            start = (half * ROWS + pair) * N
            spec_ref[start : start + N, :] = product(split_value(block.T), cas)

    def group(step, carry):
        spec = [spec_ref[pl.ds(node * POINTS + step * 8, 8), :] for node in range(NA)]
        total = [None] * NA
        item = 0
        for a in range(NA):
            for b in range(a, NA):
                phi = phi_ref[item, pl.ds(step * 8, 8), :]
                item += 1
                term = phi * spec[a]
                total[b] = term if total[b] is None else total[b] + term
                if a != b:
                    term = phi * spec[b]
                    total[a] = term if total[a] is None else total[a] + term
        for b in range(NA):
            mixed_ref[pl.ds(b * POINTS + step * 8, 8), :] = total[b]
        return carry

    lax.fori_loop(0, POINTS // 8, group, 0)
    for half in range(2):
        for pair in range(ROWS):
            start = (half * ROWS + pair) * N
            block = product(cas, split_value(mixed_ref[start : start + N, :]), ((1,), (1,)))
            for at in range(8):
                out_ref[lines(half, pair, at), :] = block[at * 16 : at * 16 + 16]


def inverse_kernel(place_ref, data_ref, index_ref, slope_ref, cas_ref, keep_ref, send_ref, sum_ref):
    parity = place_ref[1]
    rel = index_ref[0] - parity * HALF_NA
    slopes = [slope_ref[offset, 0] for offset in range(4)]
    cas = (cas_ref[0], cas_ref[1])
    lane = lax.broadcasted_iota(jnp.int32, (N, N), 1)
    total = jnp.zeros((N, N), jnp.float32)
    for pair in range(ROWS):
        lower = data_ref[pl.ds(pair, N, stride=2 * ROWS), :]
        upper = data_ref[pl.ds(ROWS + pair, N, stride=2 * ROWS), :]
        even = jnp.where(lane < POINTS, lower, pltpu.roll(upper, POINTS, 1))
        odd = jnp.where(lane < POINTS, pltpu.roll(lower, POINTS, 1), upper)
        for node, wave in ((2 * pair, even), (2 * pair + 1, odd)):
            along_y = product(cas, split_value(wave))
            field = product(split_value(along_y), cas)
            total = total + field * node_sum(rel, slopes, node)
    sum_ref[...] = total * (1.0 / float(N) ** 3)
    keep_ref[...] = sum_ref[pl.ds(parity * 64, 64), :]
    send_ref[...] = sum_ref[pl.ds(64 - parity * 64, 64), :]


def vmem():
    return pl.BlockSpec(memory_space=pltpu.VMEM)


def per_device(partial_density, node_index, node_weight, node_slope, kernel_table):
    band_at = lax.axis_index("band")
    grid_at = lax.axis_index("grid")
    table = cas_table()
    cas = split_constant(table)
    x_order = np.arange(N).reshape(16, 8).T.reshape(-1)
    cas_x = split_constant(table[x_order])
    plane = jnp.stack([band_at // 2, band_at % 2]).astype(jnp.int32)
    wave = jnp.stack([band_at * 8 + grid_at // 2, grid_at % 2]).astype(jnp.int32)
    partner = [(i, i ^ 1) for i in range(16)]
    axes = ("band", "grid")
    f32 = jnp.float32

    phi = pl.pallas_call(
        phi_kernel,
        out_shape=jax.ShapeDtypeStruct((PAIRS, POINTS, N), f32),
        in_specs=[pl.BlockSpec(memory_space=pltpu.SMEM), vmem()],
        out_specs=vmem(),
        scratch_shapes=[
            pltpu.VMEM((PAIR_ROWS, N), f32),
            pltpu.VMEM((POINTS, N), jnp.int32),
            pltpu.VMEM((POINTS, N), f32),
            pltpu.VMEM((8 * PAIR_ROWS, N), f32),
        ],
        compiler_params=pltpu.CompilerParams(vmem_limit_bytes=16 << 20),
        cost_estimate=pl.CostEstimate(flops=4 * 10**9, bytes_accessed=8 << 20, transcendentals=0),
        name="phi",
    )(wave, kernel_table)

    parts = lax.all_to_all(
        partial_density.reshape(16, 64, N), "band", 0, 0, tiled=True
    )
    own = jnp.sum(parts, axis=0)
    other = lax.ppermute(own, "band", partner)

    def plane_of(at, place):
        return (place[0], 0, 0)

    def planes_of(at, place):
        return (0, place[0], 0, 0)

    def whole(rank):
        return lambda at, place: (0,) * rank

    lines = pl.pallas_call(
        forward_kernel,
        out_shape=jax.ShapeDtypeStruct((256 * ROWS, N), f32),
        grid_spec=pltpu.PrefetchScalarGridSpec(
            num_scalar_prefetch=1,
            grid=(1,),
            in_specs=[
                pl.BlockSpec((64, N), whole(2)),
                pl.BlockSpec((64, N), whole(2)),
                pl.BlockSpec((1, N, N), plane_of),
                pl.BlockSpec((4, 1, N, N), planes_of),
                pl.BlockSpec((2, N, N), whole(3)),
            ],
            out_specs=pl.BlockSpec((256 * ROWS, N), whole(2)),
        ),
        compiler_params=pltpu.CompilerParams(vmem_limit_bytes=16 << 20),
        name="forward",
    )(plane, own, other, node_index, node_weight, cas)
    lines = lax.all_to_all(lines.reshape(256, 1, ROWS * N), axes, 0, 0, tiled=True)
    lines = lines.reshape(256 * ROWS, N)
    lines = pl.pallas_call(
        mix_kernel,
        out_shape=jax.ShapeDtypeStruct((256 * ROWS, N), f32),
        in_specs=[vmem(), vmem(), vmem()],
        out_specs=vmem(),
        scratch_shapes=[pltpu.VMEM((NA * POINTS, N), f32), pltpu.VMEM((NA * POINTS, N), f32)],
        compiler_params=pltpu.CompilerParams(vmem_limit_bytes=24 << 20),
        name="mix",
    )(lines, cas_x, phi)
    lines = lax.all_to_all(lines.reshape(256, 1, ROWS * N), axes, 0, 0, tiled=True)
    lines = lines.reshape(256 * ROWS, N)
    keep, send = pl.pallas_call(
        inverse_kernel,
        out_shape=[jax.ShapeDtypeStruct((64, N), f32), jax.ShapeDtypeStruct((64, N), f32)],
        grid_spec=pltpu.PrefetchScalarGridSpec(
            num_scalar_prefetch=1,
            grid=(1,),
            in_specs=[
                pl.BlockSpec((256 * ROWS, N), whole(2)),
                pl.BlockSpec((1, N, N), plane_of),
                pl.BlockSpec((4, 1, N, N), planes_of),
                pl.BlockSpec((2, N, N), whole(3)),
            ],
            out_specs=[pl.BlockSpec((64, N), whole(2)), pl.BlockSpec((64, N), whole(2))],
            scratch_shapes=[pltpu.VMEM((N, N), f32)],
        ),
        compiler_params=pltpu.CompilerParams(vmem_limit_bytes=16 << 20),
        name="inverse",
    )(plane, lines, node_index, node_slope, cas)
    share = keep + lax.ppermute(send, "band", partner)
    gathered = lax.all_to_all(
        jnp.broadcast_to(share[None], (16, 64, N)), "band", 0, 0, tiled=True
    )
    return gathered.reshape(8, N, N)


def solution(mesh):
    placed = (
        P("band", "grid", None, None),
        P("grid", None, None),
        P(None, "grid", None, None),
        P(None, "grid", None, None),
        P(),
    )
    return jax.shard_map(
        per_device, mesh=mesh, in_specs=placed, out_specs=P("grid", None, None), check_vma=False
    )
```

time: 357 us -> 130 us (0.36); the launches traced: 350 us -> 129 us
  local copies, waits for them, and re-layouts: 102 us -> 10.1 us
  matrix products: 75 us -> 0 us
  loops' own time: 31.9 us -> 0 us
  waiting for transfers between devices: 54.5 us -> 36.2 us
  other arithmetic: 16.6 us -> 0.19 us
  Pallas kernels: 0 us -> 12.1 us
  blocking collectives: 43.4 us -> 48.9 us
  starting transfers between devices: 25.8 us -> 21.3 us
    dot_general x28 -> x0, matrix products: 75 us -> none  [contract(): return jnp.einsum(pattern, operand, matrix, precision=lax.Precision.HIGHEST)]
    unnamed x33 -> x21, local copies, waits for them, and re-layouts: 42.9 us -> 10.1 us
    another operation x1 -> x0, loops' own time: 31.9 us -> none  [per_device(): mixed = lax.map(mix_row, jnp.arange(grid_part, dtype=jnp.int32))]
    all_to_all x4 -> x2, waiting for transfers between devices: 54.5 us -> 30.3 us  [the longest x1 17.1 us: per_device(): lax.all_to_all(partial_density.reshape(16, 64, N), 'band', 0, 0, tiled=True)]
    all_to_all x5 -> x0, local copies, waits for them, and re-layouts: 17.6 us -> none  [the longest x2 11.9 us: per_device(): lax.all_to_all(jnp.stack([ywave_real, ywave_imag]), 'grid', split_axis=4,...]
    dynamic_slice x32 -> x0, local copies, waits for them, and re-layouts: 15.5 us -> none  [the longest x8 5 us: mix_row(): lax.dynamic_index_in_dim(special_rows, row_idx, 0, keepdims=False)]
    another operation x3 -> x0, local copies, waits for them, and re-layouts: 13 us -> none  [the longest x1 4.91 us: per_device(): jnp.stack([ywave_real, ywave_imag])]
    pallas_call x0 -> x4, Pallas kernels: none -> 12.1 us  [the longest x1 5.95 us: per_device(): pl.pallas_call(phi_kernel, out_shape=jax.ShapeDtypeStruct((PAIRS, POINTS,...]
  transfers between devices with their start and end apart: 4 -> 4, of which waited for: 4 -> 4; matrix products, arithmetic and copies ran while one was open for 1% -> 0% of each run, Pallas kernels for 0% -> 5%
where the time goes in v1:
time: 130 us; the launch traced here: 129 us
  blocking collectives  48.9 us (38%)
  waiting for transfers between devices  36.2 us (28%)
  starting transfers between devices  21.3 us (16%)
  Pallas kernels  12.1 us (9%)
  local copies, waits for them, and re-layouts  10.1 us (8%)
    all_to_all x1, blocking collectives, per_device(): lax.all_to_all(lines.reshape(256, 1, ROWS * N), axes, 0, 0, tiled=True)  29 us
    all_to_all x1, blocking collectives, per_device(): lax.all_to_all(jnp.broadcast_to(share[None], (16, 64, N)), 'band', 0, 0,...  20 us
    all_to_all x1, waiting for transfers between devices, per_device(): lax.all_to_all(partial_density.reshape(16, 64, N), 'band', 0, 0, tiled=True)  17.1 us
    all_to_all x1, waiting for transfers between devices, per_device(): lax.all_to_all(lines.reshape(256, 1, ROWS * N), axes, 0, 0, tiled=True)  13.1 us
    all_to_all x1, starting transfers between devices, per_device(): lax.all_to_all(partial_density.reshape(16, 64, N), 'band', 0, 0, tiled=True)  10.1 us
    unnamed x21, local copies, waits for them, and re-layouts  10.1 us
    all_to_all x1, starting transfers between devices, per_device(): lax.all_to_all(lines.reshape(256, 1, ROWS * N), axes, 0, 0, tiled=True)  9.13 us
    pallas_call x1, Pallas kernels, per_device(): pl.pallas_call(phi_kernel, out_shape=jax.ShapeDtypeStruct((PAIRS, POINTS,...  5.95 us
  transfers between devices with their start and end apart: 4, of which 4 were waited for; matrix products, arithmetic and copies ran while one was open for 0% of the time, Pallas kernels for 5%

profile of v1, /device:TPU:2, one launch (start us, length us, event | category | flops | bytes accessed | tf_op | source)
XLA Modules:
  0.0 129.0 jit_solution(13647664740690520041)
XLA Ops:
  0.0 10.1 %all-to-all-start = ((f32[16,64,128]{2,1,0:T(8,128)}), f32[16,64,128]{2,1,0:T(8,128)S(1)}, u32[]{:S(2)}, u32[]{:S(2)}) async-start(f32[16,64,128]{2,1,0:T(8,128)} %bitcast.14), calls=%async_computation | async-start | bytes 1048576 | tf_op jit(solution)/shard_map/all_to_all | solution.py:207
  10.2 17.1 %all-to-all-done = f32[16,64,128]{2,1,0:T(8,128)S(1)} async-done(((f32[16,64,128]{2,1,0:T(8,128)}), f32[16,64,128]{2,1,0:T(8,128)S(1)}, u32[]{:S(2)}, u32[]{:S(2)}) %all-to-all-start) | async-done | bytes 524320 | tf_op jit(solution)/shard_map/all_to_all | solution.py:207
  27.3 1.2 collective-permute-start
  28.5 0.1 pad_add_fusion.place_ref
  28.6 2.8 %collective-permute-done.other_ref = f32[64,128]{1,0:T(8,128)S(1)} collective-permute-done((f32[64,128]{1,0:T(8,128)S(1)}, f32[64,128]{1,0:T(8,128)S(1)}, u32[]{:S(2)}, u32[]{:S(2)}) %collective-permute-start) | collective-permute-done | bytes 32800 | tf_op jit(solution)/shard_map/ppermute | solution.py:211
  31.3 0.0 copy-start.2
  31.4 1.6 %copy-done.2 = f32[4,8,128,128]{3,2,1,0:T(8,128)S(1)} copy-done((f32[4,8,128,128]{3,2,1,0:T(8,128)S(1)}, f32[4,8,128,128]{3,2,1,0:T(8,128)}, u32[]{:S(2)}) %copy-start.2) | copy-done | bytes 2097176
  32.9 0.0 copy-start.4
  32.9 1.0 copy-done.4
  34.0 0.0 copy-start.6
  34.0 0.8 copy-done.6
  34.8 0.0 copy-start.9
  34.8 2.3 %forward.1 = f32[1280,128]{1,0:T(8,128)} custom-call(s32[2]{0:T(128)S(1)} %pad_add_fusion.place_ref, f32[64,128]{1,0:T(8,128)S(1)} %reduce_sum.9.own_ref, f32[64,128]{1,0:T(8,128)S(1)} %collective-permute-done.other_ref, s32[8,128,128]{2,1,0:T(8,128)S(1)} %copy-done.4, f32[4,8,128,128]{3,2,1,0:T(8,128)S(1)} %copy-done.2, bf16[2,128,128]{2,1,0:T(8,128)(2,1)S(1)} %copy-done.6), custom_call_target="tpu_custom_call" | custom-call | tf_op jit(solution)/shard_map/forward/pallas_call | solution.py:222
  37.1 9.1 %all-to-all-start.1 = ((f32[256,1,640]{2,1,0:T(1,128)}), f32[256,1,640]{2,1,0:T(1,128)S(1)}, u32[]{:S(2)}, u32[]{:S(2)}) async-start(f32[256,1,640]{2,1,0:T(1,128)} %bitcast.3), calls=%async_computation.1 | async-start | bytes 1310720 | tf_op jit(solution)/shard_map/all_to_all | solution.py:240
  46.3 0.1 pad_add_fusion.1.place_ref
  46.4 0.0 copy-done.9
  46.4 0.0 copy-start.8
  46.4 6.0 %phi.1.phi_ref = f32[210,64,128]{2,1,0:T(8,128)S(1)} custom-call(s32[2]{0:T(128)S(1)} %pad_add_fusion.1.place_ref, f32[20,20,114]{2,1,0:T(8,128)S(1)} %copy-done.9), custom_call_target="tpu_custom_call" | custom-call | flops 4000000000 | bytes 8388608 | tf_op jit(solution)/shard_map/phi/pallas_call | solution.py:191
  52.3 0.0 copy-start
  52.3 2.9 %copy-done = f32[210,64,128]{2,1,0:T(8,128)} copy-done((f32[210,64,128]{2,1,0:T(8,128)}, f32[210,64,128]{2,1,0:T(8,128)S(1)}, u32[]{:S(2)}) %copy-start) | copy-done | bytes 6881304
  55.2 13.1 %all-to-all-done.1 = f32[256,1,640]{2,1,0:T(1,128)S(1)} async-done(((f32[256,1,640]{2,1,0:T(1,128)}), f32[256,1,640]{2,1,0:T(1,128)S(1)}, u32[]{:S(2)}, u32[]{:S(2)}) %all-to-all-start.1) | async-done | bytes 655392 | tf_op jit(solution)/shard_map/all_to_all | solution.py:240
  68.3 0.0 copy-done.8
  68.3 0.0 copy-start.1
  68.3 3.0 %copy-done.1 = f32[210,64,128]{2,1,0:T(8,128)S(1)} copy-done((f32[210,64,128]{2,1,0:T(8,128)S(1)}, f32[210,64,128]{2,1,0:T(8,128)}, u32[]{:S(2)}) %copy-start.1) | copy-done | bytes 6881304
  71.3 0.0 copy-start.3
  71.3 0.0 copy-start.5
  71.3 0.0 copy-start.7
  71.3 2.4 %mix.1 = f32[1280,128]{1,0:T(8,128)S(1)} custom-call(f32[1280,128]{1,0:T(8,128)S(1)} %bitcast.10, bf16[2,128,128]{2,1,0:T(8,128)(2,1)S(1)} %copy-done.8, f32[210,64,128]{2,1,0:T(8,128)S(1)} %copy-done.1), custom_call_target="tpu_custom_call" | custom-call | tf_op jit(solution)/shard_map/mix/pallas_call | solution.py:242
  73.7 29.0 %all_to_all.20 = f32[256,1,640]{2,1,0:T(1,128)S(1)} all-to-all(f32[256,1,640]{2,1,0:T(1,128)S(1)} %bitcast.11), channel_id=1, replica_groups=mesh['band'=16,'grid'=16] {'band','grid'}, dimensions={0} | all-to-all | bytes 1310720 | tf_op jit(solution)/shard_map/all_to_all | solution.py:251
  102.7 0.0 copy-done.3
  102.7 0.0 copy-done.5
  102.7 0.0 copy-done.7
  102.7 1.5 %inverse.1 = (f32[64,128]{1,0:T(8,128)S(1)}, f32[64,128]{1,0:T(8,128)S(1)}) custom-call(s32[2]{0:T(128)S(1)} %pad_add_fusion.place_ref, f32[1280,128]{1,0:T(8,128)S(1)} %bitcast.12, s32[8,128,128]{2,1,0:T(8,128)S(1)} %copy-done.5, f32[4,8,128,128]{3,2,1,0:T(8,128)S(1)} %copy-done.3, bf16[2,128,128]{2,1,0:T(8,128)(2,1)S(1)} %copy-done.7), custom_call_target="tpu_custom_call" | custom-call | tf_op jit(solution)/shard_map/inverse/pallas_call | solution.py:253
  104.1 0.8 collective-permute-start.1
  105.0 3.2 %collective-permute-done.1 = f32[64,128]{1,0:T(8,128)S(1)} collective-permute-done((f32[64,128]{1,0:T(8,128)S(1)}, f32[64,128]{1,0:T(8,128)S(1)}, u32[]{:S(2)}, u32[]{:S(2)}) %collective-permute-start.1) | collective-permute-done | bytes 32800 | tf_op jit(solution)/shard_map/ppermute | solution.py:271
  108.2 20.0 %all_to_all.21 = f32[16,64,128]{2,1,0:T(8,128)S(1)} all-to-all(f32[16,64,128]{2,1,0:T(8,128)S(1)} %broadcast_in_dim.2), channel_id=1, replica_groups=mesh['band'=16,'grid'=16] {'band'}, dimensions={0} | all-to-all | bytes 1048576 | tf_op jit(solution)/shard_map/all_to_all | solution.py:272
  128.2 0.8 copy.13
  (3 shorter events, 0.1 us)
Async XLA Ops:
  0.0 27.3 %all-to-all-start = ((f32[16,64,128]{2,1,0:T(8,128)}), f32[16,64,128]{2,1,0:T(8,128)S(1)}, u32[]{:S(2)}, u32[]{:S(2)}) async-start(f32[16,64,128]{2,1,0:T(8,128)} %bitcast.14), calls=%async_computation | async-start | bytes 1048576 | tf_op jit(solution)/shard_map/all_to_all | solution.py:207
  27.3 4.0 %collective-permute-start = (f32[64,128]{1,0:T(8,128)S(1)}, f32[64,128]{1,0:T(8,128)S(1)}, u32[]{:S(2)}, u32[]{:S(2)}) collective-permute-start(f32[64,128]{1,0:T(8,128)S(1)} %reduce_sum.9.own_ref), channel_id=1, source_target_pairs={{0,16},{16,0},{32,48},{48,32},{64,80},{80,64},{96,112},{112,96},{1... | collective-permute-start | bytes 98312 | tf_op jit(solution)/shard_map/ppermute | solution.py:211
  31.3 1.6 %copy-start.2 = (f32[4,8,128,128]{3,2,1,0:T(8,128)S(1)}, f32[4,8,128,128]{3,2,1,0:T(8,128)}, u32[]{:S(2)}) copy-start(f32[4,8,128,128]{3,2,1,0:T(8,128)} %weight_ref.1) | copy-start | bytes 6291460
  32.9 1.0 copy-start.4
  34.0 0.8 copy-start.6
  34.8 11.5 %copy-start.9 = (f32[20,20,114]{2,1,0:T(8,128)S(1)}, f32[20,20,114]{2,1,0:T(8,128)}, u32[]{:S(2)}) copy-start(f32[20,20,114]{2,1,0:T(8,128)} %table_ref.1) | copy-start | bytes 547204
  37.1 31.2 %all-to-all-start.1 = ((f32[256,1,640]{2,1,0:T(1,128)}), f32[256,1,640]{2,1,0:T(1,128)S(1)}, u32[]{:S(2)}, u32[]{:S(2)}) async-start(f32[256,1,640]{2,1,0:T(1,128)} %bitcast.3), calls=%async_computation.1 | async-start | bytes 1310720 | tf_op jit(solution)/shard_map/all_to_all | solution.py:240
  46.4 22.0 %copy-start.8 = (bf16[2,128,128]{2,1,0:T(8,128)(2,1)S(1)}, bf16[2,128,128]{2,1,0:T(8,128)(2,1)}, u32[]{:S(2)}) copy-start(bf16[2,128,128]{2,1,0:T(8,128)(2,1)} %constant.69.cas_ref) | copy-start | bytes 196612
  52.3 2.9 %copy-start = (f32[210,64,128]{2,1,0:T(8,128)}, f32[210,64,128]{2,1,0:T(8,128)S(1)}, u32[]{:S(2)}) copy-start(f32[210,64,128]{2,1,0:T(8,128)S(1)} %phi.1.phi_ref) | copy-start | bytes 20643844
  68.3 3.0 %copy-start.1 = (f32[210,64,128]{2,1,0:T(8,128)S(1)}, f32[210,64,128]{2,1,0:T(8,128)}, u32[]{:S(2)}) copy-start(f32[210,64,128]{2,1,0:T(8,128)} %copy-done) | copy-start | bytes 20643844
  71.3 31.4 %copy-start.3 = (f32[4,8,128,128]{3,2,1,0:T(8,128)S(1)}, f32[4,8,128,128]{3,2,1,0:T(8,128)}, u32[]{:S(2)}) copy-start(f32[4,8,128,128]{3,2,1,0:T(8,128)} %slope_ref.1) | copy-start | bytes 6291460
  71.3 31.4 %copy-start.5 = (s32[8,128,128]{2,1,0:T(8,128)S(1)}, s32[8,128,128]{2,1,0:T(8,128)}, u32[]{:S(2)}) copy-start(s32[8,128,128]{2,1,0:T(8,128)} %index_ref.3) | copy-start | bytes 1572868
  71.3 31.4 %copy-start.7 = (bf16[2,128,128]{2,1,0:T(8,128)(2,1)S(1)}, bf16[2,128,128]{2,1,0:T(8,128)(2,1)}, u32[]{:S(2)}) copy-start(bf16[2,128,128]{2,1,0:T(8,128)(2,1)} %constant.62.cas_ref) | copy-start | bytes 196612
  104.1 4.0 %collective-permute-start.1 = (f32[64,128]{1,0:T(8,128)S(1)}, f32[64,128]{1,0:T(8,128)S(1)}, u32[]{:S(2)}, u32[]{:S(2)}) collective-permute-start(f32[64,128]{1,0:T(8,128)S(1)} %get-tuple-element.8), channel_id=1, source_target_pairs={{0,16},{16,0},{32,48},{48,32},{64,80},{80,64},{96,112},{112,96},{1... | collective-permute-start | bytes 98312 | tf_op jit(solution)/shard_map/ppermute | solution.py:271

commit v2 on v1

--- a/solution.py
+++ b/solution.py
@@ -13,6 +13,7 @@
 PAIR_ROWS = 216
 POINTS = 64
 ROWS = 5
+GROUPS = POINTS // 8
 
 
 def cas_table():
@@ -49,7 +50,7 @@
     return jnp.where(positions < N // 2, positions, positions - N)
 
 
-def phi_kernel(place_ref, table_ref, out_ref, flat_ref, shell_ref, fraction_ref, stage_ref):
+def phi_kernel(place_ref, table_ref, out_ref, flat_ref, shell_ref, fraction_ref, stage_ref, group_ref, sems):
     flat_ref[...] = jnp.zeros_like(flat_ref)
     start = 0
     for node in range(NA):
@@ -75,6 +76,10 @@
         part = fraction_ref[pl.ds(at, 1), :]
         return jnp.where(row == low, 1.0 - part, jnp.where(row == low + 1, part, 0.0))
 
+    def put(step):
+        slot = step % 2
+        return pltpu.make_async_copy(group_ref.at[slot], out_ref.at[step], sems.at[slot])
+
     def group(step, carry):
         for pair in range(4):
             first = step * 8 + pair * 2
@@ -82,26 +87,67 @@
             value = product(table, split_value(both))
             stage_ref[pair * 2 * PAIR_ROWS : (pair * 2 + 1) * PAIR_ROWS, :] = value[:, :N]
             stage_ref[(pair * 2 + 1) * PAIR_ROWS : (pair * 2 + 2) * PAIR_ROWS, :] = value[:, N:]
+
+        @pl.when(step >= 2)
+        def _():
+            put(step - 2).wait()
+
         for item in range(PAIRS):
-            out_ref[item, pl.ds(step * 8, 8), :] = stage_ref[pl.ds(item, 8, stride=PAIR_ROWS), :]
+            group_ref[step % 2, item] = stage_ref[pl.ds(item, 8, stride=PAIR_ROWS), :]
+        put(step).start()
         return carry
 
-    lax.fori_loop(0, POINTS // 8, group, 0)
-
-
-def forward_kernel(place_ref, own_ref, other_ref, index_ref, weight_ref, cas_ref, out_ref):
-    parity = place_ref[1]
+    lax.fori_loop(0, GROUPS, group, 0)
+    put(GROUPS - 2).wait()
+    put(GROUPS - 1).wait()
+
+
+def fields_kernel(
+    place_ref, index_ref, weight_ref, slope_ref, theta_out, slope_out,
+    index_buf, weight_buf, slope_buf, sems,
+):
+    plane = place_ref[0]
+    copies = [
+        pltpu.make_async_copy(index_ref.at[plane], index_buf, sems.at[0]),
+        pltpu.make_async_copy(weight_ref.at[:, plane], weight_buf, sems.at[1]),
+        pltpu.make_async_copy(slope_ref.at[:, plane], slope_buf, sems.at[2]),
+    ]
+    for copy in copies:
+        copy.start()
+    for copy in copies:
+        copy.wait()
+    rel = index_buf[...] - place_ref[1] * HALF_NA
+    for buf, out_ref in ((weight_buf, theta_out), (slope_buf, slope_out)):
+        fields = [buf[offset] for offset in range(4)]
+        for node in range(HALF_NA):
+            out_ref[node] = node_sum(rel, fields, node)
+
+
+def load_kernel(own_ref, phi_far, theta_far, cas_far, phi_ref, theta_ref, cas_ref, phi_sems, sems):
+    copies = [
+        pltpu.make_async_copy(theta_far, theta_ref, sems.at[0]),
+        pltpu.make_async_copy(cas_far, cas_ref, sems.at[1]),
+    ]
+    copies += [
+        pltpu.make_async_copy(phi_far.at[step], phi_ref.at[step], phi_sems.at[step])
+        for step in range(GROUPS)
+    ]
+    for copy in copies:
+        copy.start()
+    for copy in copies:
+        copy.wait()
+
+
+def forward_kernel(place_ref, own_ref, other_ref, coefficient_ref, cas_ref, out_ref):
     own, other = own_ref[...], other_ref[...]
-    first = parity == 0
+    first = place_ref[1] == 0
     density = jnp.concatenate([jnp.where(first, own, other), jnp.where(first, other, own)], axis=0)
-    rel = index_ref[0] - parity * HALF_NA
-    fields = [density * weight_ref[offset, 0] for offset in range(4)]
     cas = (cas_ref[0], cas_ref[1])
     lane = lax.broadcasted_iota(jnp.int32, (N, N), 1)
     for pair in range(ROWS):
         waves = []
         for node in (2 * pair, 2 * pair + 1):
-            along_z = product(split_value(node_sum(rel, fields, node)), cas)
+            along_z = product(split_value(density * coefficient_ref[node]), cas)
             waves.append(product(cas, split_value(along_z)))
         even, odd = waves
         out_ref[pl.ds(pair, N, stride=2 * ROWS), :] = jnp.where(
@@ -130,7 +176,7 @@
         item = 0
         for a in range(NA):
             for b in range(a, NA):
-                phi = phi_ref[item, pl.ds(step * 8, 8), :]
+                phi = phi_ref[step, item]
                 item += 1
                 term = phi * spec[a]
                 total[b] = term if total[b] is None else total[b] + term
@@ -141,7 +187,7 @@
             mixed_ref[pl.ds(b * POINTS + step * 8, 8), :] = total[b]
         return carry
 
-    lax.fori_loop(0, POINTS // 8, group, 0)
+    lax.fori_loop(0, GROUPS, group, 0)
     for half in range(2):
         for pair in range(ROWS):
             start = (half * ROWS + pair) * N
@@ -150,10 +196,8 @@
                 out_ref[lines(half, pair, at), :] = block[at * 16 : at * 16 + 16]
 
 
-def inverse_kernel(place_ref, data_ref, index_ref, slope_ref, cas_ref, keep_ref, send_ref, sum_ref):
+def inverse_kernel(place_ref, data_ref, coefficient_ref, cas_ref, keep_ref, send_ref, sum_ref):
     parity = place_ref[1]
-    rel = index_ref[0] - parity * HALF_NA
-    slopes = [slope_ref[offset, 0] for offset in range(4)]
     cas = (cas_ref[0], cas_ref[1])
     lane = lax.broadcasted_iota(jnp.int32, (N, N), 1)
     total = jnp.zeros((N, N), jnp.float32)
@@ -165,7 +209,7 @@
         for node, wave in ((2 * pair, even), (2 * pair + 1, odd)):
             along_y = product(cas, split_value(wave))
             field = product(split_value(along_y), cas)
-            total = total + field * node_sum(rel, slopes, node)
+            total = total + field * coefficient_ref[node]
     sum_ref[...] = total * (1.0 / float(N) ** 3)
     keep_ref[...] = sum_ref[pl.ds(parity * 64, 64), :]
     send_ref[...] = sum_ref[pl.ds(64 - parity * 64, 64), :]
@@ -173,6 +217,18 @@
 
 def vmem():
     return pl.BlockSpec(memory_space=pltpu.VMEM)
+
+
+def scalars():
+    return pl.BlockSpec(memory_space=pltpu.SMEM)
+
+
+def anywhere():
+    return pl.BlockSpec(memory_space=pl.ANY)
+
+
+def far(value):
+    return pltpu.with_memory_space_constraint(value, pltpu.HBM)
 
 
 def per_device(partial_density, node_index, node_weight, node_slope, kernel_table):
@@ -188,55 +244,65 @@
     axes = ("band", "grid")
     f32 = jnp.float32
 
-    phi = pl.pallas_call(
+    phi_far = pl.pallas_call(
         phi_kernel,
-        out_shape=jax.ShapeDtypeStruct((PAIRS, POINTS, N), f32),
-        in_specs=[pl.BlockSpec(memory_space=pltpu.SMEM), vmem()],
-        out_specs=vmem(),
+        out_shape=pltpu.HBM((GROUPS, PAIRS, 8, N), f32),
+        in_specs=[scalars(), vmem()],
+        out_specs=anywhere(),
         scratch_shapes=[
             pltpu.VMEM((PAIR_ROWS, N), f32),
             pltpu.VMEM((POINTS, N), jnp.int32),
             pltpu.VMEM((POINTS, N), f32),
             pltpu.VMEM((8 * PAIR_ROWS, N), f32),
+            pltpu.VMEM((2, PAIRS, 8, N), f32),
+            pltpu.SemaphoreType.DMA((2,)),
         ],
-        compiler_params=pltpu.CompilerParams(vmem_limit_bytes=16 << 20),
+        compiler_params=pltpu.CompilerParams(vmem_limit_bytes=8 << 20),
         cost_estimate=pl.CostEstimate(flops=4 * 10**9, bytes_accessed=8 << 20, transcendentals=0),
         name="phi",
     )(wave, kernel_table)
 
-    parts = lax.all_to_all(
-        partial_density.reshape(16, 64, N), "band", 0, 0, tiled=True
-    )
+    theta, slope = pl.pallas_call(
+        fields_kernel,
+        out_shape=[pltpu.HBM((HALF_NA, N, N), f32)] * 2,
+        in_specs=[scalars()] + [anywhere()] * 3,
+        out_specs=[vmem()] * 2,
+        scratch_shapes=[
+            pltpu.VMEM((N, N), jnp.int32),
+            pltpu.VMEM((4, N, N), f32),
+            pltpu.VMEM((4, N, N), f32),
+            pltpu.SemaphoreType.DMA((3,)),
+        ],
+        compiler_params=pltpu.CompilerParams(vmem_limit_bytes=4 << 20),
+        cost_estimate=pl.CostEstimate(flops=10**8, bytes_accessed=2 << 20, transcendentals=0),
+        name="fields",
+    )(plane, far(node_index), far(node_weight), far(node_slope))
+    parts = lax.all_to_all(partial_density.reshape(16, 64, N), "band", 0, 0, tiled=True)
     own = jnp.sum(parts, axis=0)
+    own, phi_far, slope, theta_far = lax.optimization_barrier((own, phi_far, slope, theta))
     other = lax.ppermute(own, "band", partner)
-
-    def plane_of(at, place):
-        return (place[0], 0, 0)
-
-    def planes_of(at, place):
-        return (0, place[0], 0, 0)
-
-    def whole(rank):
-        return lambda at, place: (0,) * rank
-
+    phi, theta, cas_near = pl.pallas_call(
+        load_kernel,
+        out_shape=[
+            pltpu.VMEM(phi_far.shape, f32),
+            pltpu.VMEM(theta_far.shape, f32),
+            pltpu.VMEM(cas.shape, cas.dtype),
+        ],
+        in_specs=[anywhere()] * 4,
+        out_specs=[vmem()] * 3,
+        scratch_shapes=[pltpu.SemaphoreType.DMA((GROUPS,)), pltpu.SemaphoreType.DMA((2,))],
+        compiler_params=pltpu.CompilerParams(vmem_limit_bytes=2 << 20),
+        cost_estimate=pl.CostEstimate(flops=10**9, bytes_accessed=8 << 20, transcendentals=0),
+        name="load",
+    )(own, far(phi_far), far(theta_far), far(cas))
     lines = pl.pallas_call(
         forward_kernel,
         out_shape=jax.ShapeDtypeStruct((256 * ROWS, N), f32),
-        grid_spec=pltpu.PrefetchScalarGridSpec(
-            num_scalar_prefetch=1,
-            grid=(1,),
-            in_specs=[
-                pl.BlockSpec((64, N), whole(2)),
-                pl.BlockSpec((64, N), whole(2)),
-                pl.BlockSpec((1, N, N), plane_of),
-                pl.BlockSpec((4, 1, N, N), planes_of),
-                pl.BlockSpec((2, N, N), whole(3)),
-            ],
-            out_specs=pl.BlockSpec((256 * ROWS, N), whole(2)),
-        ),
-        compiler_params=pltpu.CompilerParams(vmem_limit_bytes=16 << 20),
+        in_specs=[pl.BlockSpec(memory_space=pltpu.SMEM)] + [vmem()] * 4,
+        out_specs=vmem(),
+        compiler_params=pltpu.CompilerParams(vmem_limit_bytes=12 << 20),
         name="forward",
-    )(plane, own, other, node_index, node_weight, cas)
+    )(plane, own, other, theta, cas_near)
     lines = lax.all_to_all(lines.reshape(256, 1, ROWS * N), axes, 0, 0, tiled=True)
     lines = lines.reshape(256 * ROWS, N)
     lines = pl.pallas_call(
@@ -253,21 +319,12 @@
     keep, send = pl.pallas_call(
         inverse_kernel,
         out_shape=[jax.ShapeDtypeStruct((64, N), f32), jax.ShapeDtypeStruct((64, N), f32)],
-        grid_spec=pltpu.PrefetchScalarGridSpec(
-            num_scalar_prefetch=1,
-            grid=(1,),
-            in_specs=[
-                pl.BlockSpec((256 * ROWS, N), whole(2)),
-                pl.BlockSpec((1, N, N), plane_of),
-                pl.BlockSpec((4, 1, N, N), planes_of),
-                pl.BlockSpec((2, N, N), whole(3)),
-            ],
-            out_specs=[pl.BlockSpec((64, N), whole(2)), pl.BlockSpec((64, N), whole(2))],
-            scratch_shapes=[pltpu.VMEM((N, N), f32)],
-        ),
-        compiler_params=pltpu.CompilerParams(vmem_limit_bytes=16 << 20),
+        in_specs=[pl.BlockSpec(memory_space=pltpu.SMEM)] + [vmem()] * 3,
+        out_specs=[vmem(), vmem()],
+        scratch_shapes=[pltpu.VMEM((N, N), f32)],
+        compiler_params=pltpu.CompilerParams(vmem_limit_bytes=12 << 20),
         name="inverse",
-    )(plane, lines, node_index, node_slope, cas)
+    )(plane, lines, slope, cas)
     share = keep + lax.ppermute(send, "band", partner)
     gathered = lax.all_to_all(
         jnp.broadcast_to(share[None], (16, 64, N)), "band", 0, 0, tiled=True

time: 130 us -> 122 us (0.938)
  blocking collectives: 48.9 us -> 80 us
  waiting for transfers between devices: 36.2 us -> 9.03 us
  starting transfers between devices: 21.3 us -> 12.1 us
  local copies, waits for them, and re-layouts: 10.1 us -> 1.8 us
  Pallas kernels: 12.1 us -> 18.5 us
    all_to_all x1 -> x2, blocking collectives: 29 us -> 60 us  [per_device(): lax.all_to_all(lines.reshape(256, 1, ROWS * N), axes, 0, 0, tiled=True)]
    all_to_all x1 -> x0, waiting for transfers between devices: 13.1 us -> none  [per_device(): lax.all_to_all(lines.reshape(256, 1, ROWS * N), axes, 0, 0, tiled=True)]
    all_to_all x1, waiting for transfers between devices: 17.1 us -> 5.88 us  [per_device(): lax.all_to_all(partial_density.reshape(16, 64, N), 'band', 0, 0, tiled=True)]
    all_to_all x1 -> x0, starting transfers between devices: 9.13 us -> none  [per_device(): lax.all_to_all(lines.reshape(256, 1, ROWS * N), axes, 0, 0, tiled=True)]
    unnamed x21 -> x9, local copies, waits for them, and re-layouts: 10.1 us -> 1.76 us
    pallas_call x1 -> x3, Pallas kernels: 5.95 us -> 13.4 us  [the longest x1 7.26 us: per_device(): pl.pallas_call(phi_kernel, out_shape=pltpu.HBM((GROUPS, PAIRS, 8, N), f32...]
    ppermute x1, waiting for transfers between devices: 2.77 us -> 0.01 us  [per_device(): other = lax.ppermute(own, 'band', partner)]
  transfers between devices with their start and end apart: 4 -> 3, of which waited for: 4 -> 2; matrix products, arithmetic and copies ran while one was open for 0% -> 0% of each run, Pallas kernels for 5% -> 11%
where the time goes in v2:
time: 122 us
  blocking collectives  80 us (66%)
  Pallas kernels  18.5 us (15%)
  starting transfers between devices  12.1 us (10%)
  waiting for transfers between devices  9.03 us (7%)
  local copies, waits for them, and re-layouts  1.8 us (1%)
    all_to_all x2, blocking collectives, per_device(): lax.all_to_all(lines.reshape(256, 1, ROWS * N), axes, 0, 0, tiled=True)  60 us
    all_to_all x1, blocking collectives, per_device(): lax.all_to_all(jnp.broadcast_to(share[None], (16, 64, N)), 'band', 0, 0,...  20 us
    all_to_all x1, starting transfers between devices, per_device(): lax.all_to_all(partial_density.reshape(16, 64, N), 'band', 0, 0, tiled=True)  10.1 us
    pallas_call x1, Pallas kernels, per_device(): pl.pallas_call(phi_kernel, out_shape=pltpu.HBM((GROUPS, PAIRS, 8, N), f32...  7.26 us
    all_to_all x1, waiting for transfers between devices, per_device(): lax.all_to_all(partial_density.reshape(16, 64, N), 'band', 0, 0, tiled=True)  5.88 us
    pallas_call x1, Pallas kernels, per_device(): pl.pallas_call(load_kernel, out_shape=[pltpu.VMEM(phi_far.shape, f32), pl...  3.25 us
    ppermute x1, waiting for transfers between devices, per_device(): share = keep + lax.ppermute(send, 'band', partner)  3.16 us
    pallas_call x1, Pallas kernels, per_device(): pl.pallas_call(fields_kernel, out_shape=[pltpu.HBM((HALF_NA, N, N), f32)]...  2.87 us
  transfers between devices with their start and end apart: 3, of which 2 were waited for; matrix products, arithmetic and copies ran while one was open for 0% of the time, Pallas kernels for 11%

profile of v2, /device:TPU:2, one launch (start us, length us, event | category | flops | bytes accessed | tf_op | source)
XLA Modules:
  0.0 121.8 jit_solution(15366938112278952039)
XLA Ops:
  0.0 10.1 %all-to-all-start = ((f32[16,64,128]{2,1,0:T(8,128)}), f32[16,64,128]{2,1,0:T(8,128)S(1)}, u32[]{:S(2)}, u32[]{:S(2)}) async-start(f32[16,64,128]{2,1,0:T(8,128)} %bitcast.15), calls=%async_computation | async-start | bytes 1048576 | tf_op jit(solution)/shard_map/all_to_all | solution.py:280
  10.2 0.1 pad_add_fusion.place_ref
  10.3 2.9 %fields.1 = (f32[10,128,128]{2,1,0:T(8,128)}, f32[10,128,128]{2,1,0:T(8,128)}) custom-call(s32[2]{0:T(128)S(1)} %pad_add_fusion.place_ref, s32[8,128,128]{2,1,0:T(8,128)} %index_ref.1, f32[4,8,128,128]{3,2,1,0:T(8,128)} %weight_ref.1, f32[4,8,128,128]{3,2,1,0:T(8,128)} %slope_ref.1), custom_call_target="tpu_custom_call" | custom-call | flops 100000000 | bytes 2097152 | tf_op jit(solution)/shard_map/fields/pallas_call | solution.py:265
  13.1 0.1 pad_add_fusion.1.place_ref
  13.2 0.0 copy-start.3
  13.2 0.9 copy-done.3
  14.2 7.3 %phi.1.phi_far = f32[8,210,8,128]{3,2,1,0:T(8,128)} custom-call(s32[2]{0:T(128)S(1)} %pad_add_fusion.1.place_ref, f32[20,20,114]{2,1,0:T(8,128)S(1)} %copy-done.3), custom_call_target="tpu_custom_call" | custom-call | flops 4000000000 | bytes 8388608 | tf_op jit(solution)/shard_map/phi/pallas_call | solution.py:247
  21.4 0.0 copy-start.2
  21.4 5.9 %all-to-all-done = f32[16,64,128]{2,1,0:T(8,128)S(1)} async-done(((f32[16,64,128]{2,1,0:T(8,128)}), f32[16,64,128]{2,1,0:T(8,128)S(1)}, u32[]{:S(2)}, u32[]{:S(2)}) %all-to-all-start) | async-done | bytes 524320 | tf_op jit(solution)/shard_map/all_to_all | solution.py:280
  27.3 1.2 collective-permute-start
  28.5 3.3 %load.1 = (f32[8,210,8,128]{3,2,1,0:T(8,128)S(1)}, f32[10,128,128]{2,1,0:T(8,128)S(1)}, bf16[2,128,128]{2,1,0:T(8,128)(2,1)S(1)}) custom-call(f32[64,128]{1,0:T(8,128)S(1)} %reduce_sum.9.own_ref, f32[8,210,8,128]{3,2,1,0:T(8,128)} %phi.1.phi_far, f32[10,128,128]{2,1,0:T(8,128)} %get-tuple-element.20.theta_far, bf16[2,128,128]{2,1,0:T(8,128)(2,1)} %constant.62.cas_far.cas_ref), custom_call_target="tpu_custom_call" | custom-call | flops 1000000000 | bytes 8388608 | tf_op jit(solution)/shard_map/load/pallas_call | solution.py:284
  31.8 0.0 copy-start
  31.8 0.0 copy-start.1
  31.8 0.0 collective-permute-done.other_ref
  31.8 1.4 %forward.1 = f32[1280,128]{1,0:T(8,128)S(1)} custom-call(s32[2]{0:T(128)S(1)} %pad_add_fusion.place_ref, f32[64,128]{1,0:T(8,128)S(1)} %reduce_sum.9.own_ref, f32[64,128]{1,0:T(8,128)S(1)} %collective-permute-done.other_ref, f32[10,128,128]{2,1,0:T(8,128)S(1)} %get-tuple-element.21.coefficient_ref, bf16[2,128,128]{2,1,0:T(8,128)(2,1)S(1)} %get-tuple-element.22.cas_ref), custom_call_target="tpu_custom_call" | custom-call | tf_op jit(solution)/shard_map/forward/pallas_call | solution.py:298
  33.2 31.1 %all_to_all.20 = f32[256,1,640]{2,1,0:T(1,128)S(1)} all-to-all(f32[256,1,640]{2,1,0:T(1,128)S(1)} %bitcast.13), channel_id=1, replica_groups=mesh['band'=16,'grid'=16] {'band','grid'}, dimensions={0} | all-to-all | bytes 1310720 | tf_op jit(solution)/shard_map/all_to_all | solution.py:306
  64.3 0.0 copy-done.2
  64.3 2.2 %mix.1 = f32[1280,128]{1,0:T(8,128)S(1)} custom-call(f32[1280,128]{1,0:T(8,128)S(1)} %bitcast.10, bf16[2,128,128]{2,1,0:T(8,128)(2,1)S(1)} %copy-done.2, f32[8,210,8,128]{3,2,1,0:T(8,128)S(1)} %get-tuple-element.23.phi_ref), custom_call_target="tpu_custom_call" | custom-call | tf_op jit(solution)/shard_map/mix/pallas_call | solution.py:308
  66.5 29.0 %all_to_all.21 = f32[256,1,640]{2,1,0:T(1,128)S(1)} all-to-all(f32[256,1,640]{2,1,0:T(1,128)S(1)} %bitcast.11), channel_id=1, replica_groups=mesh['band'=16,'grid'=16] {'band','grid'}, dimensions={0} | all-to-all | bytes 1310720 | tf_op jit(solution)/shard_map/all_to_all | solution.py:317
  95.5 0.0 copy-done
  95.5 0.0 copy-done.1
  95.5 1.4 %inverse.1 = (f32[64,128]{1,0:T(8,128)S(1)}, f32[64,128]{1,0:T(8,128)S(1)}) custom-call(s32[2]{0:T(128)S(1)} %pad_add_fusion.place_ref, f32[1280,128]{1,0:T(8,128)S(1)} %bitcast.12, f32[10,128,128]{2,1,0:T(8,128)S(1)} %copy-done, bf16[2,128,128]{2,1,0:T(8,128)(2,1)S(1)} %copy-done.1), custom_call_target="tpu_custom_call" | custom-call | tf_op jit(solution)/shard_map/inverse/pallas_call | solution.py:319
  96.9 0.8 collective-permute-start.1
  97.8 3.2 %collective-permute-done.1 = f32[64,128]{1,0:T(8,128)S(1)} collective-permute-done((f32[64,128]{1,0:T(8,128)S(1)}, f32[64,128]{1,0:T(8,128)S(1)}, u32[]{:S(2)}, u32[]{:S(2)}) %collective-permute-start.1) | collective-permute-done | bytes 32800 | tf_op jit(solution)/shard_map/ppermute | solution.py:328
  101.0 20.0 %all_to_all.22 = f32[16,64,128]{2,1,0:T(8,128)S(1)} all-to-all(f32[16,64,128]{2,1,0:T(8,128)S(1)} %broadcast_in_dim.2), channel_id=1, replica_groups=mesh['band'=16,'grid'=16] {'band'}, dimensions={0} | all-to-all | bytes 1048576 | tf_op jit(solution)/shard_map/all_to_all | solution.py:329
  121.0 0.8 copy.13
  (3 shorter events, 0.1 us)
Async XLA Ops:
  0.0 27.3 %all-to-all-start = ((f32[16,64,128]{2,1,0:T(8,128)}), f32[16,64,128]{2,1,0:T(8,128)S(1)}, u32[]{:S(2)}, u32[]{:S(2)}) async-start(f32[16,64,128]{2,1,0:T(8,128)} %bitcast.15), calls=%async_computation | async-start | bytes 1048576 | tf_op jit(solution)/shard_map/all_to_all | solution.py:280
  13.2 0.9 copy-start.3
  21.4 42.9 %copy-start.2 = (bf16[2,128,128]{2,1,0:T(8,128)(2,1)S(1)}, bf16[2,128,128]{2,1,0:T(8,128)(2,1)}, u32[]{:S(2)}) copy-start(bf16[2,128,128]{2,1,0:T(8,128)(2,1)} %constant.69.cas_ref) | copy-start | bytes 196612
  27.3 4.4 %collective-permute-start = (f32[64,128]{1,0:T(8,128)S(1)}, f32[64,128]{1,0:T(8,128)S(1)}, u32[]{:S(2)}, u32[]{:S(2)}) collective-permute-start(f32[64,128]{1,0:T(8,128)S(1)} %reduce_sum.9.own_ref), channel_id=1, source_target_pairs={{0,16},{16,0},{32,48},{48,32},{64,80},{80,64},{96,112},{112,96},{1... | collective-permute-start | bytes 98312 | tf_op jit(solution)/shard_map/ppermute | solution.py:283
  31.8 63.7 %copy-start = (f32[10,128,128]{2,1,0:T(8,128)S(1)}, f32[10,128,128]{2,1,0:T(8,128)}, u32[]{:S(2)}) copy-start(f32[10,128,128]{2,1,0:T(8,128)} %get-tuple-element.24.coefficient_ref) | copy-start | bytes 1966084
  31.8 63.7 %copy-start.1 = (bf16[2,128,128]{2,1,0:T(8,128)(2,1)S(1)}, bf16[2,128,128]{2,1,0:T(8,128)(2,1)}, u32[]{:S(2)}) copy-start(bf16[2,128,128]{2,1,0:T(8,128)(2,1)} %constant.62.cas_far.cas_ref) | copy-start | bytes 196612
  96.9 4.0 %collective-permute-start.1 = (f32[64,128]{1,0:T(8,128)S(1)}, f32[64,128]{1,0:T(8,128)S(1)}, u32[]{:S(2)}, u32[]{:S(2)}) collective-permute-start(f32[64,128]{1,0:T(8,128)S(1)} %get-tuple-element.26), channel_id=1, source_target_pairs={{0,16},{16,0},{32,48},{48,32},{64,80},{80,64},{96,112},{112,96},{1... | collective-permute-start | bytes 98312 | tf_op jit(solution)/shard_map/ppermute | solution.py:328

commit v3 on v2

--- a/solution.py
+++ b/solution.py
@@ -14,6 +14,7 @@
 POINTS = 64
 ROWS = 5
 GROUPS = POINTS // 8
+NEAR = 7
 
 
 def cas_table():
@@ -25,7 +26,8 @@
 def split_constant(table):
     high = jnp.asarray(table, jnp.float32).astype(jnp.bfloat16)
     low = (jnp.asarray(table, jnp.float32) - high.astype(jnp.float32)).astype(jnp.bfloat16)
-    return jnp.stack([high, low])
+    row = jnp.concatenate([high, low], axis=1)
+    return jnp.concatenate([row, row], axis=0)
 
 
 def split_value(value):
@@ -37,6 +39,30 @@
 def product(left, right, dims=((1,), (0,))):
     dot = lambda a, b: lax.dot_general(a, b, (dims, ((), ())), preferred_element_type=jnp.float32)
     return dot(left[0], right[0]) + (dot(left[0], right[1]) + dot(left[1], right[0]))
+
+
+def halves_added(value):
+    return value[:, :N] + value[:, N:]
+
+
+def rows_times(value, wide):
+    parts = jnp.concatenate(split_value(value), axis=1)
+    return halves_added(jnp.dot(parts, wide, preferred_element_type=jnp.float32))
+
+
+def times_block(wide, value):
+    parts = jnp.concatenate(split_value(value), axis=1)
+    parts = jnp.concatenate([parts, parts], axis=0)
+    return halves_added(jnp.dot(wide[:N], parts, preferred_element_type=jnp.float32))
+
+
+def times_block_turned(wide, value):
+    parts = jnp.concatenate(split_value(value), axis=0)
+    parts = jnp.concatenate([parts, parts], axis=1)
+    dims = (((1,), (1,)), ((), ()))
+    return halves_added(
+        lax.dot_general(wide[:N], parts, dims, preferred_element_type=jnp.float32)
+    )
 
 
 def node_sum(rel, fields, node):
@@ -50,7 +76,7 @@
     return jnp.where(positions < N // 2, positions, positions - N)
 
 
-def phi_kernel(place_ref, table_ref, out_ref, flat_ref, shell_ref, fraction_ref, stage_ref, group_ref, sems):
+def phi_kernel(table_ref, out_ref, flat_ref, shell_ref, fraction_ref, stage_ref, group_ref, sems):
     flat_ref[...] = jnp.zeros_like(flat_ref)
     start = 0
     for node in range(NA):
@@ -58,9 +84,10 @@
         flat_ref[start : start + count, 0 : table_ref.shape[2]] = table_ref[node, node:NA, :]
         start += count
     table = split_value(flat_ref[...])
-    freq_y = frequency(place_ref[0])
+    band_at, grid_at = lax.axis_index("band"), lax.axis_index("grid")
+    freq_y = frequency(band_at * 8 + grid_at // 2)
     point = lax.broadcasted_iota(jnp.int32, (POINTS, N), 0)
-    freq_z = frequency(point + place_ref[1] * POINTS)
+    freq_z = frequency(point + grid_at % 2 * POINTS)
     freq_x = frequency(lax.broadcasted_iota(jnp.int32, (POINTS, N), 1))
     square = freq_x * freq_x + freq_z * freq_z + freq_y * freq_y
     root = jnp.sqrt(square.astype(jnp.float32))
@@ -103,10 +130,11 @@
 
 
 def fields_kernel(
-    place_ref, index_ref, weight_ref, slope_ref, theta_out, slope_out,
+    index_ref, weight_ref, slope_ref, theta_out, slope_out,
     index_buf, weight_buf, slope_buf, sems,
 ):
-    plane = place_ref[0]
+    band_at = lax.axis_index("band")
+    plane = band_at // 2
     copies = [
         pltpu.make_async_copy(index_ref.at[plane], index_buf, sems.at[0]),
         pltpu.make_async_copy(weight_ref.at[:, plane], weight_buf, sems.at[1]),
@@ -116,7 +144,7 @@
         copy.start()
     for copy in copies:
         copy.wait()
-    rel = index_buf[...] - place_ref[1] * HALF_NA
+    rel = index_buf[...] - band_at % 2 * HALF_NA
     for buf, out_ref in ((weight_buf, theta_out), (slope_buf, slope_out)):
         fields = [buf[offset] for offset in range(4)]
         for node in range(HALF_NA):
@@ -130,7 +158,7 @@
     ]
     copies += [
         pltpu.make_async_copy(phi_far.at[step], phi_ref.at[step], phi_sems.at[step])
-        for step in range(GROUPS)
+        for step in range(NEAR)
     ]
     for copy in copies:
         copy.start()
@@ -138,17 +166,18 @@
         copy.wait()
 
 
-def forward_kernel(place_ref, own_ref, other_ref, coefficient_ref, cas_ref, out_ref):
+def forward_kernel(own_ref, other_ref, coefficient_ref, cas_ref, out_ref):
     own, other = own_ref[...], other_ref[...]
-    first = place_ref[1] == 0
+    first = lax.axis_index("band") % 2 == 0
     density = jnp.concatenate([jnp.where(first, own, other), jnp.where(first, other, own)], axis=0)
-    cas = (cas_ref[0], cas_ref[1])
+    cas = cas_ref[...]
     lane = lax.broadcasted_iota(jnp.int32, (N, N), 1)
+    theta = density[None] * coefficient_ref[...]
+    along_z = rows_times(theta.reshape(HALF_NA * N, N), cas)
     for pair in range(ROWS):
         waves = []
         for node in (2 * pair, 2 * pair + 1):
-            along_z = product(split_value(density * coefficient_ref[node]), cas)
-            waves.append(product(cas, split_value(along_z)))
+            waves.append(times_block(cas, along_z[node * N : (node + 1) * N]))
         even, odd = waves
         out_ref[pl.ds(pair, N, stride=2 * ROWS), :] = jnp.where(
             lane < POINTS, even, pltpu.roll(odd, POINTS, 1)
@@ -158,8 +187,14 @@
         )
 
 
-def mix_kernel(data_ref, cas_ref, phi_ref, out_ref, spec_ref, mixed_ref):
-    cas = (cas_ref[0], cas_ref[1])
+def mix_kernel(data_ref, cas_ref, phi_ref, far_ref, out_ref, spec_ref, mixed_ref, late_ref, sems):
+    cas = cas_ref[...]
+    late = [
+        pltpu.make_async_copy(far_ref.at[NEAR + step], late_ref.at[step], sems.at[step])
+        for step in range(GROUPS - NEAR)
+    ]
+    for copy in late:
+        copy.start()
 
     def lines(half, pair, at):
         return pl.ds((at * 2 + half) * 16 * ROWS + pair, 16, stride=ROWS)
@@ -168,15 +203,15 @@
         for pair in range(ROWS):
             block = jnp.concatenate([data_ref[lines(half, pair, at), :] for at in range(8)], axis=0)
             start = (half * ROWS + pair) * N
-            spec_ref[start : start + N, :] = product(split_value(block.T), cas)
-
-    def group(step, carry):
+            spec_ref[start : start + N, :] = rows_times(block.T, cas)
+
+    def group(step, phi_at):
         spec = [spec_ref[pl.ds(node * POINTS + step * 8, 8), :] for node in range(NA)]
         total = [None] * NA
         item = 0
         for a in range(NA):
             for b in range(a, NA):
-                phi = phi_ref[step, item]
+                phi = phi_at[item]
                 item += 1
                 term = phi * spec[a]
                 total[b] = term if total[b] is None else total[b] + term
@@ -185,31 +220,45 @@
                     total[a] = term if total[a] is None else total[a] + term
         for b in range(NA):
             mixed_ref[pl.ds(b * POINTS + step * 8, 8), :] = total[b]
+
+    def near(step, carry):
+        group(step, phi_ref.at[step])
         return carry
 
-    lax.fori_loop(0, GROUPS, group, 0)
+    def far(step, carry):
+        group(NEAR + step, late_ref.at[step])
+        return carry
+
+    lax.fori_loop(0, NEAR, near, 0)
+    for copy in late:
+        copy.wait()
+    lax.fori_loop(0, GROUPS - NEAR, far, 0)
     for half in range(2):
         for pair in range(ROWS):
             start = (half * ROWS + pair) * N
-            block = product(cas, split_value(mixed_ref[start : start + N, :]), ((1,), (1,)))
+            block = times_block_turned(cas, mixed_ref[start : start + N, :])
             for at in range(8):
                 out_ref[lines(half, pair, at), :] = block[at * 16 : at * 16 + 16]
 
 
-def inverse_kernel(place_ref, data_ref, coefficient_ref, cas_ref, keep_ref, send_ref, sum_ref):
-    parity = place_ref[1]
-    cas = (cas_ref[0], cas_ref[1])
+def inverse_kernel(data_ref, coefficient_ref, cas_ref, keep_ref, send_ref, sum_ref):
+    parity = lax.axis_index("band") % 2
+    cas = cas_ref[...]
     lane = lax.broadcasted_iota(jnp.int32, (N, N), 1)
-    total = jnp.zeros((N, N), jnp.float32)
+    along_y = []
     for pair in range(ROWS):
         lower = data_ref[pl.ds(pair, N, stride=2 * ROWS), :]
         upper = data_ref[pl.ds(ROWS + pair, N, stride=2 * ROWS), :]
-        even = jnp.where(lane < POINTS, lower, pltpu.roll(upper, POINTS, 1))
-        odd = jnp.where(lane < POINTS, pltpu.roll(lower, POINTS, 1), upper)
-        for node, wave in ((2 * pair, even), (2 * pair + 1, odd)):
-            along_y = product(cas, split_value(wave))
-            field = product(split_value(along_y), cas)
-            total = total + field * coefficient_ref[node]
+        along_y.append(
+            times_block(cas, jnp.where(lane < POINTS, lower, pltpu.roll(upper, POINTS, 1)))
+        )
+        along_y.append(
+            times_block(cas, jnp.where(lane < POINTS, pltpu.roll(lower, POINTS, 1), upper))
+        )
+    fields = rows_times(jnp.concatenate(along_y, axis=0), cas)
+    total = fields[:N] * coefficient_ref[0]
+    for node in range(1, HALF_NA):
+        total = total + fields[node * N : (node + 1) * N] * coefficient_ref[node]
     sum_ref[...] = total * (1.0 / float(N) ** 3)
     keep_ref[...] = sum_ref[pl.ds(parity * 64, 64), :]
     send_ref[...] = sum_ref[pl.ds(64 - parity * 64, 64), :]
@@ -219,10 +268,6 @@
     return pl.BlockSpec(memory_space=pltpu.VMEM)
 
 
-def scalars():
-    return pl.BlockSpec(memory_space=pltpu.SMEM)
-
-
 def anywhere():
     return pl.BlockSpec(memory_space=pl.ANY)
 
@@ -232,14 +277,10 @@
 
 
 def per_device(partial_density, node_index, node_weight, node_slope, kernel_table):
-    band_at = lax.axis_index("band")
-    grid_at = lax.axis_index("grid")
     table = cas_table()
     cas = split_constant(table)
     x_order = np.arange(N).reshape(16, 8).T.reshape(-1)
     cas_x = split_constant(table[x_order])
-    plane = jnp.stack([band_at // 2, band_at % 2]).astype(jnp.int32)
-    wave = jnp.stack([band_at * 8 + grid_at // 2, grid_at % 2]).astype(jnp.int32)
     partner = [(i, i ^ 1) for i in range(16)]
     axes = ("band", "grid")
     f32 = jnp.float32
@@ -247,7 +288,7 @@
     phi_far = pl.pallas_call(
         phi_kernel,
         out_shape=pltpu.HBM((GROUPS, PAIRS, 8, N), f32),
-        in_specs=[scalars(), vmem()],
+        in_specs=[vmem()],
         out_specs=anywhere(),
         scratch_shapes=[
             pltpu.VMEM((PAIR_ROWS, N), f32),
@@ -260,12 +301,12 @@
         compiler_params=pltpu.CompilerParams(vmem_limit_bytes=8 << 20),
         cost_estimate=pl.CostEstimate(flops=4 * 10**9, bytes_accessed=8 << 20, transcendentals=0),
         name="phi",
-    )(wave, kernel_table)
+    )(kernel_table)
 
     theta, slope = pl.pallas_call(
         fields_kernel,
         out_shape=[pltpu.HBM((HALF_NA, N, N), f32)] * 2,
-        in_specs=[scalars()] + [anywhere()] * 3,
+        in_specs=[anywhere()] * 3,
         out_specs=[vmem()] * 2,
         scratch_shapes=[
             pltpu.VMEM((N, N), jnp.int32),
@@ -276,7 +317,7 @@
         compiler_params=pltpu.CompilerParams(vmem_limit_bytes=4 << 20),
         cost_estimate=pl.CostEstimate(flops=10**8, bytes_accessed=2 << 20, transcendentals=0),
         name="fields",
-    )(plane, far(node_index), far(node_weight), far(node_slope))
+    )(far(node_index), far(node_weight), far(node_slope))
     parts = lax.all_to_all(partial_density.reshape(16, 64, N), "band", 0, 0, tiled=True)
     own = jnp.sum(parts, axis=0)
     own, phi_far, slope, theta_far = lax.optimization_barrier((own, phi_far, slope, theta))
@@ -284,13 +325,13 @@
     phi, theta, cas_near = pl.pallas_call(
         load_kernel,
         out_shape=[
-            pltpu.VMEM(phi_far.shape, f32),
+            pltpu.VMEM((NEAR, PAIRS, 8, N), f32),
             pltpu.VMEM(theta_far.shape, f32),
             pltpu.VMEM(cas.shape, cas.dtype),
         ],
         in_specs=[anywhere()] * 4,
         out_specs=[vmem()] * 3,
-        scratch_shapes=[pltpu.SemaphoreType.DMA((GROUPS,)), pltpu.SemaphoreType.DMA((2,))],
+        scratch_shapes=[pltpu.SemaphoreType.DMA((NEAR,)), pltpu.SemaphoreType.DMA((2,))],
         compiler_params=pltpu.CompilerParams(vmem_limit_bytes=2 << 20),
         cost_estimate=pl.CostEstimate(flops=10**9, bytes_accessed=8 << 20, transcendentals=0),
         name="load",
@@ -298,33 +339,38 @@
     lines = pl.pallas_call(
         forward_kernel,
         out_shape=jax.ShapeDtypeStruct((256 * ROWS, N), f32),
-        in_specs=[pl.BlockSpec(memory_space=pltpu.SMEM)] + [vmem()] * 4,
+        in_specs=[vmem()] * 4,
         out_specs=vmem(),
         compiler_params=pltpu.CompilerParams(vmem_limit_bytes=12 << 20),
         name="forward",
-    )(plane, own, other, theta, cas_near)
+    )(own, other, theta, cas_near)
     lines = lax.all_to_all(lines.reshape(256, 1, ROWS * N), axes, 0, 0, tiled=True)
     lines = lines.reshape(256 * ROWS, N)
     lines = pl.pallas_call(
         mix_kernel,
         out_shape=jax.ShapeDtypeStruct((256 * ROWS, N), f32),
-        in_specs=[vmem(), vmem(), vmem()],
+        in_specs=[vmem(), vmem(), vmem(), anywhere()],
         out_specs=vmem(),
-        scratch_shapes=[pltpu.VMEM((NA * POINTS, N), f32), pltpu.VMEM((NA * POINTS, N), f32)],
+        scratch_shapes=[
+            pltpu.VMEM((NA * POINTS, N), f32),
+            pltpu.VMEM((NA * POINTS, N), f32),
+            pltpu.VMEM((GROUPS - NEAR, PAIRS, 8, N), f32),
+            pltpu.SemaphoreType.DMA((GROUPS - NEAR,)),
+        ],
         compiler_params=pltpu.CompilerParams(vmem_limit_bytes=24 << 20),
         name="mix",
-    )(lines, cas_x, phi)
+    )(lines, cas_x, phi, far(phi_far))
     lines = lax.all_to_all(lines.reshape(256, 1, ROWS * N), axes, 0, 0, tiled=True)
     lines = lines.reshape(256 * ROWS, N)
     keep, send = pl.pallas_call(
         inverse_kernel,
         out_shape=[jax.ShapeDtypeStruct((64, N), f32), jax.ShapeDtypeStruct((64, N), f32)],
-        in_specs=[pl.BlockSpec(memory_space=pltpu.SMEM)] + [vmem()] * 3,
+        in_specs=[vmem()] * 3,
         out_specs=[vmem(), vmem()],
         scratch_shapes=[pltpu.VMEM((N, N), f32)],
         compiler_params=pltpu.CompilerParams(vmem_limit_bytes=12 << 20),
         name="inverse",
-    )(plane, lines, slope, cas)
+    )(lines, slope, cas)
     share = keep + lax.ppermute(send, "band", partner)
     gathered = lax.all_to_all(
         jnp.broadcast_to(share[None], (16, 64, N)), "band", 0, 0, tiled=True

time: 122 us -> 120 us (0.984)
  Pallas kernels: 18.5 us -> 15.5 us
  waiting for transfers between devices: 9.03 us -> 10.3 us
    all_to_all x1, waiting for transfers between devices: 5.88 us -> 7.13 us  [per_device(): lax.all_to_all(partial_density.reshape(16, 64, N), 'band', 0, 0, tiled=True)]
  transfers between devices with their start and end apart: 3 -> 3, of which waited for: 2 -> 2; matrix products, arithmetic and copies ran while one was open for 0% -> 0% of each run, Pallas kernels for 11% -> 10%
where the time goes in v3:
time: 120 us
  blocking collectives  80 us (67%)
  Pallas kernels  15.5 us (13%)
  starting transfers between devices  12.1 us (10%)
  waiting for transfers between devices  10.3 us (9%)
  local copies, waits for them, and re-layouts  1.79 us (1%)
    all_to_all x2, blocking collectives, per_device(): lax.all_to_all(lines.reshape(256, 1, ROWS * N), axes, 0, 0, tiled=True)  60 us
    all_to_all x1, blocking collectives, per_device(): lax.all_to_all(jnp.broadcast_to(share[None], (16, 64, N)), 'band', 0, 0,...  20 us
    all_to_all x1, starting transfers between devices, per_device(): lax.all_to_all(partial_density.reshape(16, 64, N), 'band', 0, 0, tiled=True)  10.1 us
    all_to_all x1, waiting for transfers between devices, per_device(): lax.all_to_all(partial_density.reshape(16, 64, N), 'band', 0, 0, tiled=True)  7.13 us
    pallas_call x1, Pallas kernels, per_device(): pl.pallas_call(phi_kernel, out_shape=pltpu.HBM((GROUPS, PAIRS, 8, N), f32...  6.72 us
    ppermute x1, waiting for transfers between devices, per_device(): share = keep + lax.ppermute(send, 'band', partner)  3.15 us
    pallas_call x1, Pallas kernels, per_device(): pl.pallas_call(load_kernel, out_shape=[pltpu.VMEM((NEAR, PAIRS, 8, N), f3...  3.02 us
  transfers between devices with their start and end apart: 3, of which 2 were waited for; matrix products, arithmetic and copies ran while one was open for 0% of the time, Pallas kernels for 10%

profile of v3, /device:TPU:2, one launch (start us, length us, event | category | flops | bytes accessed | tf_op | source)
XLA Modules:
  0.0 119.8 jit_solution(8109334522148854955)
XLA Ops:
  0.0 10.1 %all-to-all-start = ((f32[16,64,128]{2,1,0:T(8,128)}), f32[16,64,128]{2,1,0:T(8,128)S(1)}, u32[]{:S(2)}, u32[]{:S(2)}) async-start(f32[16,64,128]{2,1,0:T(8,128)} %bitcast.11), calls=%async_computation | async-start | bytes 1048576 | tf_op jit(solution)/shard_map/all_to_all | solution.py:321
  10.1 2.3 %fields.1 = (f32[10,128,128]{2,1,0:T(8,128)}, f32[10,128,128]{2,1,0:T(8,128)}) custom-call(s32[8,128,128]{2,1,0:T(8,128)} %index_ref.1, f32[4,8,128,128]{3,2,1,0:T(8,128)} %weight_ref.1, f32[4,8,128,128]{3,2,1,0:T(8,128)} %slope_ref.1), custom_call_target="tpu_custom_call" | custom-call | flops 100000000 | bytes 2097152 | tf_op jit(solution)/shard_map/fields/pallas_call | solution.py:306
  12.5 0.0 copy-start.3
  12.5 0.9 copy-done.3
  13.4 6.7 %phi.1.phi_far.far_ref = f32[8,210,8,128]{3,2,1,0:T(8,128)} custom-call(f32[20,20,114]{2,1,0:T(8,128)S(1)} %copy-done.3), custom_call_target="tpu_custom_call" | custom-call | flops 4000000000 | bytes 8388608 | tf_op jit(solution)/shard_map/phi/pallas_call | solution.py:288
  20.2 0.0 copy-start.2
  20.2 7.1 %all-to-all-done = f32[16,64,128]{2,1,0:T(8,128)S(1)} async-done(((f32[16,64,128]{2,1,0:T(8,128)}), f32[16,64,128]{2,1,0:T(8,128)S(1)}, u32[]{:S(2)}, u32[]{:S(2)}) %all-to-all-start) | async-done | bytes 524320 | tf_op jit(solution)/shard_map/all_to_all | solution.py:321
  27.3 1.2 collective-permute-start
  28.5 3.0 %load.1 = (f32[7,210,8,128]{3,2,1,0:T(8,128)S(1)}, f32[10,128,128]{2,1,0:T(8,128)S(1)}, bf16[256,256]{1,0:T(8,128)(2,1)S(1)}) custom-call(f32[64,128]{1,0:T(8,128)S(1)} %reduce_sum.9.own_ref, f32[8,210,8,128]{3,2,1,0:T(8,128)} %phi.1.phi_far.far_ref, f32[10,128,128]{2,1,0:T(8,128)} %get-tuple-element.20.theta_far, bf16[256,256]{1,0:T(8,128)(2,1)} %constant.17.cas_far.cas_ref), custom_call_target="tpu_custom_call" | custom-call | flops 1000000000 | bytes 8388608 | tf_op jit(solution)/shard_map/load/pallas_call | solution.py:325
  31.5 0.0 collective-permute-done.other_ref
  31.5 0.7 forward.1
  32.3 31.1 %all_to_all.20 = f32[256,1,640]{2,1,0:T(1,128)S(1)} all-to-all(f32[256,1,640]{2,1,0:T(1,128)S(1)} %bitcast.7), channel_id=1, replica_groups=mesh['band'=16,'grid'=16] {'band','grid'}, dimensions={0} | all-to-all | bytes 1310720 | tf_op jit(solution)/shard_map/all_to_all | solution.py:347
  63.3 0.0 copy-done.2
  63.3 0.0 copy-start
  63.3 0.0 copy-start.1
  63.4 2.0 %mix.1 = f32[1280,128]{1,0:T(8,128)S(1)} custom-call(f32[1280,128]{1,0:T(8,128)S(1)} %bitcast.8, bf16[256,256]{1,0:T(8,128)(2,1)S(1)} %copy-done.2, f32[7,210,8,128]{3,2,1,0:T(8,128)S(1)} %get-tuple-element.23.phi_ref, f32[8,210,8,128]{3,2,1,0:T(8,128)} %phi.1.phi_far.far_ref), custom_call_target="tpu_custom_call" | custom-call | tf_op jit(solution)/shard_map/mix/pallas_call | solution.py:349
  65.4 28.9 %all_to_all.21 = f32[256,1,640]{2,1,0:T(1,128)S(1)} all-to-all(f32[256,1,640]{2,1,0:T(1,128)S(1)} %bitcast.9), channel_id=1, replica_groups=mesh['band'=16,'grid'=16] {'band','grid'}, dimensions={0} | all-to-all | bytes 1310720 | tf_op jit(solution)/shard_map/all_to_all | solution.py:363
  94.3 0.0 copy-done
  94.3 0.0 copy-done.1
  94.3 0.6 inverse.1
  95.0 0.9 collective-permute-start.1
  95.8 3.1 %collective-permute-done.1 = f32[64,128]{1,0:T(8,128)S(1)} collective-permute-done((f32[64,128]{1,0:T(8,128)S(1)}, f32[64,128]{1,0:T(8,128)S(1)}, u32[]{:S(2)}, u32[]{:S(2)}) %collective-permute-start.1) | collective-permute-done | bytes 32800 | tf_op jit(solution)/shard_map/ppermute | solution.py:374
  99.0 20.0 %all_to_all.22 = f32[16,64,128]{2,1,0:T(8,128)S(1)} all-to-all(f32[16,64,128]{2,1,0:T(8,128)S(1)} %broadcast_in_dim.2), channel_id=1, replica_groups=mesh['band'=16,'grid'=16] {'band'}, dimensions={0} | all-to-all | bytes 1048576 | tf_op jit(solution)/shard_map/all_to_all | solution.py:375
  119.0 0.8 copy.13
  (3 shorter events, 0.1 us)
Async XLA Ops:
  0.0 27.3 %all-to-all-start = ((f32[16,64,128]{2,1,0:T(8,128)}), f32[16,64,128]{2,1,0:T(8,128)S(1)}, u32[]{:S(2)}, u32[]{:S(2)}) async-start(f32[16,64,128]{2,1,0:T(8,128)} %bitcast.11), calls=%async_computation | async-start | bytes 1048576 | tf_op jit(solution)/shard_map/all_to_all | solution.py:321
  12.5 0.9 copy-start.3
  20.2 43.2 %copy-start.2 = (bf16[256,256]{1,0:T(8,128)(2,1)S(1)}, bf16[256,256]{1,0:T(8,128)(2,1)}, u32[]{:S(2)}) copy-start(bf16[256,256]{1,0:T(8,128)(2,1)} %constant.23.cas_ref) | copy-start | bytes 393220
  27.3 4.2 %collective-permute-start = (f32[64,128]{1,0:T(8,128)S(1)}, f32[64,128]{1,0:T(8,128)S(1)}, u32[]{:S(2)}, u32[]{:S(2)}) collective-permute-start(f32[64,128]{1,0:T(8,128)S(1)} %reduce_sum.9.own_ref), channel_id=1, source_target_pairs={{0,16},{16,0},{32,48},{48,32},{64,80},{80,64},{96,112},{112,96},{1... | collective-permute-start | bytes 98312 | tf_op jit(solution)/shard_map/ppermute | solution.py:324
  63.3 31.0 %copy-start = (f32[10,128,128]{2,1,0:T(8,128)S(1)}, f32[10,128,128]{2,1,0:T(8,128)}, u32[]{:S(2)}) copy-start(f32[10,128,128]{2,1,0:T(8,128)} %get-tuple-element.24.coefficient_ref) | copy-start | bytes 1966084
  63.3 31.0 %copy-start.1 = (bf16[256,256]{1,0:T(8,128)(2,1)S(1)}, bf16[256,256]{1,0:T(8,128)(2,1)}, u32[]{:S(2)}) copy-start(bf16[256,256]{1,0:T(8,128)(2,1)} %constant.17.cas_far.cas_ref) | copy-start | bytes 393220
  95.0 4.0 %collective-permute-start.1 = (f32[64,128]{1,0:T(8,128)S(1)}, f32[64,128]{1,0:T(8,128)S(1)}, u32[]{:S(2)}, u32[]{:S(2)}) collective-permute-start(f32[64,128]{1,0:T(8,128)S(1)} %get-tuple-element.26), channel_id=1, source_target_pairs={{0,16},{16,0},{32,48},{48,32},{64,80},{80,64},{96,112},{112,96},{1... | collective-permute-start | bytes 98312 | tf_op jit(solution)/shard_map/ppermute | solution.py:374

commit v4 on v3

--- a/solution.py
+++ b/solution.py
@@ -23,10 +23,34 @@
     return np.cos(angle) + np.sin(angle)
 
 
-def split_constant(table):
+def wave_order():
+    sets = np.arange(32)
+    other = np.where(sets == 0, 32, 64 - sets)
+    return np.concatenate([sets, sets + 64, other, other + 64])
+
+
+def half_table():
+    idx = np.arange(64)
+    order = wave_order().reshape(4, 32)[[0, 2]].reshape(-1)
+    angle = 2.0 * np.pi * ((idx[:, None] * order[None, :]) % 64) / 64
+    return np.cos(angle) + np.sin(angle)
+
+
+def twist_table():
+    angle = np.pi * np.arange(32) / 64
+    factors = np.stack([np.cos(angle), np.sin(angle), np.sin(angle), -np.cos(angle)], axis=1)
+    factors[0] = (1.0, 0.0, 0.0, 1.0)
+    return jnp.asarray(np.repeat(factors.reshape(-1, 1), N, axis=1), jnp.float32)
+
+
+def split_row(table):
     high = jnp.asarray(table, jnp.float32).astype(jnp.bfloat16)
     low = (jnp.asarray(table, jnp.float32) - high.astype(jnp.float32)).astype(jnp.bfloat16)
-    row = jnp.concatenate([high, low], axis=1)
+    return jnp.concatenate([high, low], axis=1)
+
+
+def split_constant(table):
+    row = split_row(table)
     return jnp.concatenate([row, row], axis=0)
 
 
@@ -50,10 +74,10 @@
     return halves_added(jnp.dot(parts, wide, preferred_element_type=jnp.float32))
 
 
-def times_block(wide, value):
+def times_block(row, value):
     parts = jnp.concatenate(split_value(value), axis=1)
     parts = jnp.concatenate([parts, parts], axis=0)
-    return halves_added(jnp.dot(wide[:N], parts, preferred_element_type=jnp.float32))
+    return halves_added(jnp.dot(row, parts, preferred_element_type=jnp.float32))
 
 
 def times_block_turned(wide, value):
@@ -63,6 +87,19 @@
     return halves_added(
         lax.dot_general(wide[:N], parts, dims, preferred_element_type=jnp.float32)
     )
+
+
+def turned_groups(items):
+    items = list(items)
+    group = lax.broadcasted_iota(jnp.int32, items[0].shape, 1) // 16
+    for bit in (1, 2, 4):
+        upper = group // bit % 2 == 1
+        for at in range(8):
+            if at & bit == 0:
+                first, second = items[at], items[at | bit]
+                items[at] = jnp.where(upper, pltpu.roll(second, bit * 16, 1), first)
+                items[at | bit] = jnp.where(upper, second, pltpu.roll(first, N - bit * 16, 1))
+    return items
 
 
 def node_sum(rel, fields, node):
@@ -85,9 +122,12 @@
         start += count
     table = split_value(flat_ref[...])
     band_at, grid_at = lax.axis_index("band"), lax.axis_index("grid")
-    freq_y = frequency(band_at * 8 + grid_at // 2)
+    wave_set = band_at * 2 + grid_at // 8
     point = lax.broadcasted_iota(jnp.int32, (POINTS, N), 0)
-    freq_z = frequency(point + grid_at % 2 * POINTS)
+    slot = point // 16
+    other = jnp.where(wave_set == 0, 32, 64 - wave_set)
+    freq_y = frequency(jnp.where(slot < 2, wave_set, other) + slot % 2 * 64)
+    freq_z = frequency(point % 16 + grid_at % 8 * 16)
     freq_x = frequency(lax.broadcasted_iota(jnp.int32, (POINTS, N), 1))
     square = freq_x * freq_x + freq_z * freq_z + freq_y * freq_y
     root = jnp.sqrt(square.astype(jnp.float32))
@@ -144,18 +184,20 @@
         copy.start()
     for copy in copies:
         copy.wait()
-    rel = index_buf[...] - band_at % 2 * HALF_NA
-    for buf, out_ref in ((weight_buf, theta_out), (slope_buf, slope_out)):
-        fields = [buf[offset] for offset in range(4)]
-        for node in range(HALF_NA):
-            out_ref[node] = node_sum(rel, fields, node)
-
-
-def load_kernel(own_ref, phi_far, theta_far, cas_far, phi_ref, theta_ref, cas_ref, phi_sems, sems):
-    copies = [
-        pltpu.make_async_copy(theta_far, theta_ref, sems.at[0]),
-        pltpu.make_async_copy(cas_far, cas_ref, sems.at[1]),
-    ]
+    parity = band_at % 2
+    rel = index_buf[...] - parity * HALF_NA
+    fields = [weight_buf[offset] for offset in range(4)]
+    for node in range(HALF_NA):
+        theta_out[node] = node_sum(rel, fields, node)
+    rows = pl.ds(parity, 64, stride=2)
+    rel = index_buf[rows, :]
+    fields = [slope_buf[offset, rows, :] for offset in range(4)]
+    for node in range(NA):
+        slope_out[node] = node_sum(rel, fields, node)
+
+
+def load_kernel(own_ref, phi_far, cas_far, phi_ref, cas_ref, phi_sems, cas_sem):
+    copies = [pltpu.make_async_copy(cas_far, cas_ref, cas_sem)]
     copies += [
         pltpu.make_async_copy(phi_far.at[step], phi_ref.at[step], phi_sems.at[step])
         for step in range(NEAR)
@@ -170,24 +212,19 @@
     own, other = own_ref[...], other_ref[...]
     first = lax.axis_index("band") % 2 == 0
     density = jnp.concatenate([jnp.where(first, own, other), jnp.where(first, other, own)], axis=0)
-    cas = cas_ref[...]
-    lane = lax.broadcasted_iota(jnp.int32, (N, N), 1)
+    wide, row = cas_ref[: 2 * N], cas_ref[2 * N :]
     theta = density[None] * coefficient_ref[...]
-    along_z = rows_times(theta.reshape(HALF_NA * N, N), cas)
+    along_z = rows_times(theta.reshape(HALF_NA * N, N), wide)
     for pair in range(ROWS):
-        waves = []
+        items = []
         for node in (2 * pair, 2 * pair + 1):
-            waves.append(times_block(cas, along_z[node * N : (node + 1) * N]))
-        even, odd = waves
-        out_ref[pl.ds(pair, N, stride=2 * ROWS), :] = jnp.where(
-            lane < POINTS, even, pltpu.roll(odd, POINTS, 1)
-        )
-        out_ref[pl.ds(ROWS + pair, N, stride=2 * ROWS), :] = jnp.where(
-            lane < POINTS, pltpu.roll(even, POINTS, 1), odd
-        )
-
-
-def mix_kernel(data_ref, cas_ref, phi_ref, far_ref, out_ref, spec_ref, mixed_ref, late_ref, sems):
+            waves = times_block(row, along_z[node * N : (node + 1) * N])
+            items += [waves[slot * 32 : slot * 32 + 32] for slot in range(4)]
+        for block, item in enumerate(turned_groups(items)):
+            out_ref[pl.ds(block * ROWS + pair, 32, stride=8 * ROWS), :] = item
+
+
+def mix_kernel(data_ref, cas_ref, twist_ref, phi_ref, far_ref, out_ref, spec_ref, mixed_ref, late_ref, sems):
     cas = cas_ref[...]
     late = [
         pltpu.make_async_copy(far_ref.at[NEAR + step], late_ref.at[step], sems.at[step])
@@ -233,35 +270,50 @@
     for copy in late:
         copy.wait()
     lax.fori_loop(0, GROUPS - NEAR, far, 0)
-    for half in range(2):
-        for pair in range(ROWS):
-            start = (half * ROWS + pair) * N
-            block = times_block_turned(cas, mixed_ref[start : start + N, :])
+    wave_set = lax.axis_index("band") * 2 + lax.axis_index("grid") // 8
+    twist = [twist_ref[pl.ds(wave_set * 4 + factor, 1), :] for factor in range(4)]
+    for pair in range(ROWS):
+        even, odd = [], []
+        for node in range(4 * pair, 4 * pair + 4):
+            start = node * POINTS
+            slots = [mixed_ref[start + 16 * slot : start + 16 * slot + 16, :] for slot in range(4)]
+            even += [slots[0] + slots[1], slots[2] + slots[3]]
+            near, other = slots[0] - slots[1], slots[2] - slots[3]
+            odd += [twist[0] * near + twist[1] * other, twist[2] * near + twist[3] * other]
+        for half, rows in enumerate((even, odd)):
+            block = times_block_turned(cas, jnp.concatenate(rows, axis=0))
             for at in range(8):
                 out_ref[lines(half, pair, at), :] = block[at * 16 : at * 16 + 16]
 
 
-def inverse_kernel(data_ref, coefficient_ref, cas_ref, keep_ref, send_ref, sum_ref):
-    parity = lax.axis_index("band") % 2
-    cas = cas_ref[...]
-    lane = lax.broadcasted_iota(jnp.int32, (N, N), 1)
+def inverse_kernel(data_ref, coefficient_ref, cas_ref, half_ref, out_ref):
+    cas, row = cas_ref[...], half_ref[...]
     along_y = []
     for pair in range(ROWS):
-        lower = data_ref[pl.ds(pair, N, stride=2 * ROWS), :]
-        upper = data_ref[pl.ds(ROWS + pair, N, stride=2 * ROWS), :]
-        along_y.append(
-            times_block(cas, jnp.where(lane < POINTS, lower, pltpu.roll(upper, POINTS, 1)))
+        items = turned_groups(
+            [data_ref[pl.ds(block * ROWS + pair, 32, stride=8 * ROWS), :] for block in range(8)]
         )
-        along_y.append(
-            times_block(cas, jnp.where(lane < POINTS, pltpu.roll(lower, POINTS, 1), upper))
+        for at in range(4):
+            waves = jnp.concatenate([items[2 * at], items[2 * at + 1]], axis=0)
+            along_y.append(times_block(row, waves))
+    fields = rows_times(jnp.concatenate(along_y, axis=0), cas)
+    total = fields[:64] * coefficient_ref[0]
+    for node in range(1, NA):
+        total = total + fields[node * 64 : (node + 1) * 64] * coefficient_ref[node]
+    out_ref[...] = total * (1.0 / float(N) ** 3)
+
+
+def weave_kernel(data_ref, out_ref, plane_ref, sems):
+    copies = []
+    for plane in range(8):
+        for parity in range(2):
+            plane_ref[plane, pl.ds(parity, 64, stride=2), :] = data_ref[2 * plane + parity]
+        copies.append(
+            pltpu.make_async_copy(plane_ref.at[plane], out_ref.at[plane], sems.at[plane])
         )
-    fields = rows_times(jnp.concatenate(along_y, axis=0), cas)
-    total = fields[:N] * coefficient_ref[0]
-    for node in range(1, HALF_NA):
-        total = total + fields[node * N : (node + 1) * N] * coefficient_ref[node]
-    sum_ref[...] = total * (1.0 / float(N) ** 3)
-    keep_ref[...] = sum_ref[pl.ds(parity * 64, 64), :]
-    send_ref[...] = sum_ref[pl.ds(64 - parity * 64, 64), :]
+        copies[-1].start()
+    for copy in copies:
+        copy.wait()
 
 
 def vmem():
@@ -279,6 +331,7 @@
 def per_device(partial_density, node_index, node_weight, node_slope, kernel_table):
     table = cas_table()
     cas = split_constant(table)
+    cas_two = jnp.concatenate([cas, split_row(table[wave_order()])], axis=0)
     x_order = np.arange(N).reshape(16, 8).T.reshape(-1)
     cas_x = split_constant(table[x_order])
     partner = [(i, i ^ 1) for i in range(16)]
@@ -305,7 +358,7 @@
 
     theta, slope = pl.pallas_call(
         fields_kernel,
-        out_shape=[pltpu.HBM((HALF_NA, N, N), f32)] * 2,
+        out_shape=[pltpu.VMEM((HALF_NA, N, N), f32), pltpu.VMEM((NA, 64, N), f32)],
         in_specs=[anywhere()] * 3,
         out_specs=[vmem()] * 2,
         scratch_shapes=[
@@ -320,22 +373,21 @@
     )(far(node_index), far(node_weight), far(node_slope))
     parts = lax.all_to_all(partial_density.reshape(16, 64, N), "band", 0, 0, tiled=True)
     own = jnp.sum(parts, axis=0)
-    own, phi_far, slope, theta_far = lax.optimization_barrier((own, phi_far, slope, theta))
+    own, phi_far, slope, theta = lax.optimization_barrier((own, phi_far, slope, theta))
     other = lax.ppermute(own, "band", partner)
-    phi, theta, cas_near = pl.pallas_call(
+    phi, cas_near = pl.pallas_call(
         load_kernel,
         out_shape=[
             pltpu.VMEM((NEAR, PAIRS, 8, N), f32),
-            pltpu.VMEM(theta_far.shape, f32),
-            pltpu.VMEM(cas.shape, cas.dtype),
+            pltpu.VMEM(cas_two.shape, cas_two.dtype),
         ],
-        in_specs=[anywhere()] * 4,
-        out_specs=[vmem()] * 3,
-        scratch_shapes=[pltpu.SemaphoreType.DMA((NEAR,)), pltpu.SemaphoreType.DMA((2,))],
+        in_specs=[anywhere()] * 3,
+        out_specs=[vmem()] * 2,
+        scratch_shapes=[pltpu.SemaphoreType.DMA((NEAR,)), pltpu.SemaphoreType.DMA],
         compiler_params=pltpu.CompilerParams(vmem_limit_bytes=2 << 20),
         cost_estimate=pl.CostEstimate(flops=10**9, bytes_accessed=8 << 20, transcendentals=0),
         name="load",
-    )(own, far(phi_far), far(theta_far), far(cas))
+    )(own, far(phi_far), far(cas_two))
     lines = pl.pallas_call(
         forward_kernel,
         out_shape=jax.ShapeDtypeStruct((256 * ROWS, N), f32),
@@ -349,7 +401,7 @@
     lines = pl.pallas_call(
         mix_kernel,
         out_shape=jax.ShapeDtypeStruct((256 * ROWS, N), f32),
-        in_specs=[vmem(), vmem(), vmem(), anywhere()],
+        in_specs=[vmem()] * 4 + [anywhere()],
         out_specs=vmem(),
         scratch_shapes=[
             pltpu.VMEM((NA * POINTS, N), f32),
@@ -359,23 +411,29 @@
         ],
         compiler_params=pltpu.CompilerParams(vmem_limit_bytes=24 << 20),
         name="mix",
-    )(lines, cas_x, phi, far(phi_far))
+    )(lines, cas_x, twist_table(), phi, far(phi_far))
     lines = lax.all_to_all(lines.reshape(256, 1, ROWS * N), axes, 0, 0, tiled=True)
     lines = lines.reshape(256 * ROWS, N)
-    keep, send = pl.pallas_call(
+    share = pl.pallas_call(
         inverse_kernel,
-        out_shape=[jax.ShapeDtypeStruct((64, N), f32), jax.ShapeDtypeStruct((64, N), f32)],
-        in_specs=[vmem()] * 3,
-        out_specs=[vmem(), vmem()],
-        scratch_shapes=[pltpu.VMEM((N, N), f32)],
+        out_shape=jax.ShapeDtypeStruct((64, N), f32),
+        in_specs=[vmem()] * 4,
+        out_specs=vmem(),
         compiler_params=pltpu.CompilerParams(vmem_limit_bytes=12 << 20),
         name="inverse",
-    )(lines, slope, cas)
-    share = keep + lax.ppermute(send, "band", partner)
+    )(lines, slope, cas, split_row(half_table()))
     gathered = lax.all_to_all(
         jnp.broadcast_to(share[None], (16, 64, N)), "band", 0, 0, tiled=True
     )
-    return gathered.reshape(8, N, N)
+    return pl.pallas_call(
+        weave_kernel,
+        out_shape=pltpu.HBM((8, N, N), f32),
+        in_specs=[vmem()],
+        out_specs=anywhere(),
+        scratch_shapes=[pltpu.VMEM((8, N, N), f32), pltpu.SemaphoreType.DMA((8,))],
+        compiler_params=pltpu.CompilerParams(vmem_limit_bytes=4 << 20),
+        name="weave",
+    )(gathered)
 
 
 def solution(mesh):

time: 120 us -> 118 us (0.983)
  waiting for transfers between devices: 10.3 us -> 8.03 us
  blocking collectives: 80 us -> 81.5 us
    ppermute x1 -> x0, waiting for transfers between devices: 3.15 us -> none  [per_device(): share = keep + lax.ppermute(send, 'band', partner)]
    all_to_all x1, blocking collectives: 20 us -> 21.5 us  [per_device(): lax.all_to_all(jnp.broadcast_to(share[None], (16, 64, N)), 'band', 0, 0,...]
    pallas_call x2 -> x3, Pallas kernels: 2.99 us -> 3.29 us  [the longest x1 1.42 us: per_device(): pl.pallas_call(fields_kernel, out_shape=[pltpu.VMEM((HALF_NA, N, N), f32)...]
  transfers between devices with their start and end apart: 3 -> 2, of which waited for: 2 -> 1; matrix products, arithmetic and copies ran while one was open for 0% -> 0% of each run, Pallas kernels for 10% -> 9%
where the time goes in v4:
time: 118 us
  blocking collectives  81.5 us (69%)
  Pallas kernels  15.8 us (13%)
  starting transfers between devices  11.3 us (10%)
  waiting for transfers between devices  8.03 us (7%)
    all_to_all x2, blocking collectives, per_device(): lax.all_to_all(lines.reshape(256, 1, ROWS * N), axes, 0, 0, tiled=True)  60.1 us
    all_to_all x1, blocking collectives, per_device(): lax.all_to_all(jnp.broadcast_to(share[None], (16, 64, N)), 'band', 0, 0,...  21.5 us
    all_to_all x1, starting transfers between devices, per_device(): lax.all_to_all(partial_density.reshape(16, 64, N), 'band', 0, 0, tiled=True)  10.1 us
    all_to_all x1, waiting for transfers between devices, per_device(): lax.all_to_all(partial_density.reshape(16, 64, N), 'band', 0, 0, tiled=True)  8.03 us
    pallas_call x1, Pallas kernels, per_device(): pl.pallas_call(phi_kernel, out_shape=pltpu.HBM((GROUPS, PAIRS, 8, N), f32...  6.74 us
    pallas_call x1, Pallas kernels, per_device(): pl.pallas_call(load_kernel, out_shape=[pltpu.VMEM((NEAR, PAIRS, 8, N), f3...  2.84 us
  transfers between devices with their start and end apart: 2, of which 1 were waited for; matrix products, arithmetic and copies ran while one was open for 0% of the time, Pallas kernels for 9%

profile of v4, /device:TPU:2, one launch (start us, length us, event | category | flops | bytes accessed | tf_op | source)
XLA Modules:
  0.0 117.8 jit_solution(16488478083612621091)
XLA Ops:
  0.0 10.1 %all-to-all-start = ((f32[16,64,128]{2,1,0:T(8,128)}), f32[16,64,128]{2,1,0:T(8,128)S(1)}, u32[]{:S(2)}, u32[]{:S(2)}) async-start(f32[16,64,128]{2,1,0:T(8,128)} %bitcast.9), calls=%async_computation | async-start | bytes 1048576 | tf_op jit(solution)/shard_map/all_to_all | solution.py:374
  10.1 1.4 %fields.1 = (f32[10,128,128]{2,1,0:T(8,128)S(1)}, f32[20,64,128]{2,1,0:T(8,128)S(1)}) custom-call(s32[8,128,128]{2,1,0:T(8,128)} %index_ref.1, f32[4,8,128,128]{3,2,1,0:T(8,128)} %weight_ref.1, f32[4,8,128,128]{3,2,1,0:T(8,128)} %slope_ref.1), custom_call_target="tpu_custom_call" | custom-call | flops 100000000 | bytes 2097152 | tf_op jit(solution)/shard_map/fields/pallas_call | solution.py:359
  11.6 0.0 copy-start.4
  11.6 0.9 copy-done.4
  12.5 6.7 %phi.1.phi_far.far_ref = f32[8,210,8,128]{3,2,1,0:T(8,128)} custom-call(f32[20,20,114]{2,1,0:T(8,128)S(1)} %copy-done.4), custom_call_target="tpu_custom_call" | custom-call | flops 4000000000 | bytes 8388608 | tf_op jit(solution)/shard_map/phi/pallas_call | solution.py:341
  19.3 0.0 copy-start
  19.3 0.0 copy-start.2
  19.3 8.0 %all-to-all-done = f32[16,64,128]{2,1,0:T(8,128)S(1)} async-done(((f32[16,64,128]{2,1,0:T(8,128)}), f32[16,64,128]{2,1,0:T(8,128)S(1)}, u32[]{:S(2)}, u32[]{:S(2)}) %all-to-all-start) | async-done | bytes 524320 | tf_op jit(solution)/shard_map/all_to_all | solution.py:374
  27.3 1.2 collective-permute-start
  28.5 2.8 %load.1 = (f32[7,210,8,128]{3,2,1,0:T(8,128)S(1)}, bf16[384,256]{1,0:T(8,128)(2,1)S(1)}) custom-call(f32[64,128]{1,0:T(8,128)S(1)} %reduce_sum.9.own_ref, f32[8,210,8,128]{3,2,1,0:T(8,128)} %phi.1.phi_far.far_ref, bf16[384,256]{1,0:T(8,128)(2,1)} %constant.31.cas_far), custom_call_target="tpu_custom_call" | custom-call | flops 1000000000 | bytes 8388608 | tf_op jit(solution)/shard_map/load/pallas_call | solution.py:378
  31.3 0.0 collective-permute-done.other_ref
  31.4 1.0 forward.1
  32.3 31.1 %all_to_all.20 = f32[256,1,640]{2,1,0:T(1,128)S(1)} all-to-all(f32[256,1,640]{2,1,0:T(1,128)S(1)} %bitcast.5), channel_id=1, replica_groups=mesh['band'=16,'grid'=16] {'band','grid'}, dimensions={0} | all-to-all | bytes 1310720 | tf_op jit(solution)/shard_map/all_to_all | solution.py:399
  63.4 0.0 copy-done
  63.4 0.0 copy-done.2
  63.4 0.0 copy-start.1
  63.4 0.0 copy-start.3
  63.4 2.0 %mix.1 = f32[1280,128]{1,0:T(8,128)S(1)} custom-call(f32[1280,128]{1,0:T(8,128)S(1)} %bitcast.7, bf16[256,256]{1,0:T(8,128)(2,1)S(1)} %copy-done, f32[128,128]{1,0:T(8,128)S(1)} %copy-done.2, f32[7,210,8,128]{3,2,1,0:T(8,128)S(1)} %get-tuple-element.19.phi_ref, f32[8,210,8,128]{3,2,1,0:T(8,128)} %phi.1.phi_far.far_ref), custom_call_target="tpu_custom_call" | custom-call | tf_op jit(solution)/shard_map/mix/pallas_call | solution.py:401
  65.4 29.0 %all_to_all.21 = f32[256,1,640]{2,1,0:T(1,128)S(1)} all-to-all(f32[256,1,640]{2,1,0:T(1,128)S(1)} %bitcast.8), channel_id=1, replica_groups=mesh['band'=16,'grid'=16] {'band','grid'}, dimensions={0} | all-to-all | bytes 1310720 | tf_op jit(solution)/shard_map/all_to_all | solution.py:415
  94.4 0.0 copy-done.1
  94.4 0.0 copy-done.3
  94.4 1.0 inverse.1
  95.5 21.5 %all_to_all.22.data_ref = f32[16,64,128]{2,1,0:T(8,128)S(1)} all-to-all(f32[16,64,128]{2,1,0:T(8,128)S(1)} %broadcast_in_dim.2), channel_id=1, replica_groups=mesh['band'=16,'grid'=16] {'band'}, dimensions={0} | all-to-all | bytes 1048576 | tf_op jit(solution)/shard_map/all_to_all | solution.py:425
  117.0 0.9 weave.1
  (2 shorter events, 0.1 us)
Async XLA Ops:
  0.0 27.3 %all-to-all-start = ((f32[16,64,128]{2,1,0:T(8,128)}), f32[16,64,128]{2,1,0:T(8,128)S(1)}, u32[]{:S(2)}, u32[]{:S(2)}) async-start(f32[16,64,128]{2,1,0:T(8,128)} %bitcast.9), calls=%async_computation | async-start | bytes 1048576 | tf_op jit(solution)/shard_map/all_to_all | solution.py:374
  11.6 0.9 copy-start.4
  19.3 44.1 %copy-start = (bf16[256,256]{1,0:T(8,128)(2,1)S(1)}, bf16[256,256]{1,0:T(8,128)(2,1)}, u32[]{:S(2)}) copy-start(bf16[256,256]{1,0:T(8,128)(2,1)} %constant.37.cas_ref) | copy-start | bytes 393220
  19.3 44.1 %copy-start.2 = (f32[128,128]{1,0:T(8,128)S(1)}, f32[128,128]{1,0:T(8,128)}, u32[]{:S(2)}) copy-start(f32[128,128]{1,0:T(8,128)} %constant.15.clone.twist_ref) | copy-start | bytes 196612
  27.3 4.0 %collective-permute-start = (f32[64,128]{1,0:T(8,128)S(1)}, f32[64,128]{1,0:T(8,128)S(1)}, u32[]{:S(2)}, u32[]{:S(2)}) collective-permute-start(f32[64,128]{1,0:T(8,128)S(1)} %reduce_sum.9.own_ref), channel_id=1, source_target_pairs={{0,16},{16,0},{32,48},{48,32},{64,80},{80,64},{96,112},{112,96},{1... | collective-permute-start | bytes 98312 | tf_op jit(solution)/shard_map/ppermute | solution.py:377
  63.4 31.0 %copy-start.1 = (bf16[256,256]{1,0:T(8,128)(2,1)S(1)}, bf16[256,256]{1,0:T(8,128)(2,1)}, u32[]{:S(2)}) copy-start(bf16[256,256]{1,0:T(8,128)(2,1)} %constant.38.cas_ref) | copy-start | bytes 393220
  63.4 31.0 %copy-start.3 = (bf16[64,128]{1,0:T(8,128)(2,1)S(1)}, bf16[64,128]{1,0:T(8,128)(2,1)}, u32[]{:S(2)}) copy-start(bf16[64,128]{1,0:T(8,128)(2,1)} %constant.43.half_ref) | copy-start | bytes 49156

commit v5 on v4

--- a/solution.py
+++ b/solution.py
@@ -8,13 +8,12 @@
 
 N = 128
 NA = 20
-HALF_NA = 10
 PAIRS = NA * (NA + 1) // 2
 PAIR_ROWS = 216
 POINTS = 64
 ROWS = 5
-GROUPS = POINTS // 8
-NEAR = 7
+GROUPS = 6
+PHI_POINTS = 8 * GROUPS
 
 
 def cas_table():
@@ -113,7 +112,7 @@
     return jnp.where(positions < N // 2, positions, positions - N)
 
 
-def phi_kernel(table_ref, out_ref, flat_ref, shell_ref, fraction_ref, stage_ref, group_ref, sems):
+def phi_kernel(table_ref, near_ref, out_ref, flat_ref, shell_ref, fraction_ref, stage_ref, group_ref, sems):
     flat_ref[...] = jnp.zeros_like(flat_ref)
     start = 0
     for node in range(NA):
@@ -123,12 +122,12 @@
     table = split_value(flat_ref[...])
     band_at, grid_at = lax.axis_index("band"), lax.axis_index("grid")
     wave_set = band_at * 2 + grid_at // 8
-    point = lax.broadcasted_iota(jnp.int32, (POINTS, N), 0)
+    point = lax.broadcasted_iota(jnp.int32, (PHI_POINTS, N), 0)
     slot = point // 16
     other = jnp.where(wave_set == 0, 32, 64 - wave_set)
     freq_y = frequency(jnp.where(slot < 2, wave_set, other) + slot % 2 * 64)
     freq_z = frequency(point % 16 + grid_at % 8 * 16)
-    freq_x = frequency(lax.broadcasted_iota(jnp.int32, (POINTS, N), 1))
+    freq_x = frequency(lax.broadcasted_iota(jnp.int32, (PHI_POINTS, N), 1))
     square = freq_x * freq_x + freq_z * freq_z + freq_y * freq_y
     root = jnp.sqrt(square.astype(jnp.float32))
     shell = root.astype(jnp.int32)
@@ -162,6 +161,11 @@
         for item in range(PAIRS):
             group_ref[step % 2, item] = stage_ref[pl.ds(item, 8, stride=PAIR_ROWS), :]
         put(step).start()
+
+        @pl.when(step < 2)
+        def _():
+            near_ref[step] = group_ref[step % 2]
+
         return carry
 
     lax.fori_loop(0, GROUPS, group, 0)
@@ -184,63 +188,96 @@
         copy.start()
     for copy in copies:
         copy.wait()
-    parity = band_at % 2
-    rel = index_buf[...] - parity * HALF_NA
-    fields = [weight_buf[offset] for offset in range(4)]
-    for node in range(HALF_NA):
-        theta_out[node] = node_sum(rel, fields, node)
-    rows = pl.ds(parity, 64, stride=2)
+    rows = pl.ds(band_at % 2, 64, stride=2)
     rel = index_buf[rows, :]
-    fields = [slope_buf[offset, rows, :] for offset in range(4)]
-    for node in range(NA):
-        slope_out[node] = node_sum(rel, fields, node)
-
-
-def load_kernel(own_ref, phi_far, cas_far, phi_ref, cas_ref, phi_sems, cas_sem):
-    copies = [pltpu.make_async_copy(cas_far, cas_ref, cas_sem)]
-    copies += [
-        pltpu.make_async_copy(phi_far.at[step], phi_ref.at[step], phi_sems.at[step])
-        for step in range(NEAR)
-    ]
-    for copy in copies:
-        copy.start()
-    for copy in copies:
-        copy.wait()
-
-
-def forward_kernel(own_ref, other_ref, coefficient_ref, cas_ref, out_ref):
-    own, other = own_ref[...], other_ref[...]
-    first = lax.axis_index("band") % 2 == 0
-    density = jnp.concatenate([jnp.where(first, own, other), jnp.where(first, other, own)], axis=0)
-    wide, row = cas_ref[: 2 * N], cas_ref[2 * N :]
+    for buf, out_ref in ((weight_buf, theta_out), (slope_buf, slope_out)):
+        fields = [buf[offset, rows, :] for offset in range(4)]
+        for node in range(NA):
+            out_ref[node] = node_sum(rel, fields, node)
+
+
+def sort_kernel(far_ref, out_ref, plane_ref, sorted_ref, in_sems, out_sems):
+    def get(plane):
+        return pltpu.make_async_copy(far_ref.at[plane], plane_ref.at[plane], in_sems.at[plane])
+
+    def put(plane):
+        return pltpu.make_async_copy(
+            sorted_ref.at[pl.ds(2 * plane, 2)], out_ref.at[pl.ds(2 * plane, 2)], out_sems.at[plane]
+        )
+
+    for plane in range(8):
+        get(plane).start()
+    for plane in range(8):
+        get(plane).wait()
+        for parity in range(2):
+            sorted_ref[2 * plane + parity] = plane_ref[plane, pl.ds(parity, 64, stride=2), :]
+        put(plane).start()
+    for plane in range(8):
+        put(plane).wait()
+
+
+def forward_kernel(parts_ref, coefficient_ref, cas_ref, half_ref, far_ref, out_ref, near_ref, sem):
+    copy = pltpu.make_async_copy(far_ref.at[2], near_ref, sem)
+    copy.start()
+    density = parts_ref[0]
+    for part in range(1, 16):
+        density = density + parts_ref[part]
+    row = half_ref[...]
     theta = density[None] * coefficient_ref[...]
-    along_z = rows_times(theta.reshape(HALF_NA * N, N), wide)
+    along_z = rows_times(theta.reshape(NA * 64, N), cas_ref[...])
     for pair in range(ROWS):
         items = []
-        for node in (2 * pair, 2 * pair + 1):
-            waves = times_block(row, along_z[node * N : (node + 1) * N])
-            items += [waves[slot * 32 : slot * 32 + 32] for slot in range(4)]
+        for node in range(4 * pair, 4 * pair + 4):
+            waves = times_block(row, along_z[node * 64 : (node + 1) * 64])
+            items += [waves[:32], waves[32:]]
         for block, item in enumerate(turned_groups(items)):
             out_ref[pl.ds(block * ROWS + pair, 32, stride=8 * ROWS), :] = item
-
-
-def mix_kernel(data_ref, cas_ref, twist_ref, phi_ref, far_ref, out_ref, spec_ref, mixed_ref, late_ref, sems):
+    copy.wait()
+
+
+def mix_kernel(
+    data_ref, cas_ref, twist_ref, first_ref, second_ref, far_ref, out_ref,
+    spec_ref, mixed_ref, late_ref, sems,
+):
     cas = cas_ref[...]
+    wave_set = lax.axis_index("band") * 2 + lax.axis_index("grid") // 8
+    paired = wave_set != 0
     late = [
-        pltpu.make_async_copy(far_ref.at[NEAR + step], late_ref.at[step], sems.at[step])
-        for step in range(GROUPS - NEAR)
+        pltpu.make_async_copy(far_ref.at[3 + step], late_ref.at[step], sems.at[step])
+        for step in range(3)
     ]
-    for copy in late:
-        copy.start()
+    late[0].start()
+
+    @pl.when(jnp.logical_not(paired))
+    def _():
+        late[1].start()
+        late[2].start()
+
+    twist = [twist_ref[pl.ds(wave_set * 4 + factor, 1), :] for factor in range(4)]
 
     def lines(half, pair, at):
         return pl.ds((at * 2 + half) * 16 * ROWS + pair, 16, stride=ROWS)
 
-    for half in range(2):
-        for pair in range(ROWS):
-            block = jnp.concatenate([data_ref[lines(half, pair, at), :] for at in range(8)], axis=0)
-            start = (half * ROWS + pair) * N
-            spec_ref[start : start + N, :] = rows_times(block.T, cas)
+    for pair in range(ROWS):
+        even, odd = (
+            rows_times(
+                jnp.concatenate([data_ref[lines(half, pair, at), :] for at in range(8)], axis=0).T,
+                cas,
+            )
+            for half in range(2)
+        )
+        for at in range(4):
+            start = (4 * pair + at) * POINTS
+            near, other = odd[at * 32 : at * 32 + 16], odd[at * 32 + 16 : at * 32 + 32]
+            turned = (
+                twist[0] * near + twist[1] * other,
+                twist[2] * near + twist[3] * other,
+            )
+            for residue in range(2):
+                first = even[at * 32 + 16 * residue : at * 32 + 16 * residue + 16]
+                base = start + 32 * residue
+                spec_ref[base : base + 16, :] = first + turned[residue]
+                spec_ref[base + 16 : base + 32, :] = first - turned[residue]
 
     def group(step, phi_at):
         spec = [spec_ref[pl.ds(node * POINTS + step * 8, 8), :] for node in range(NA)]
@@ -258,20 +295,31 @@
         for b in range(NA):
             mixed_ref[pl.ds(b * POINTS + step * 8, 8), :] = total[b]
 
-    def near(step, carry):
-        group(step, phi_ref.at[step])
-        return carry
-
-    def far(step, carry):
-        group(NEAR + step, late_ref.at[step])
-        return carry
-
-    lax.fori_loop(0, NEAR, near, 0)
-    for copy in late:
-        copy.wait()
-    lax.fori_loop(0, GROUPS - NEAR, far, 0)
-    wave_set = lax.axis_index("band") * 2 + lax.axis_index("grid") // 8
-    twist = [twist_ref[pl.ds(wave_set * 4 + factor, 1), :] for factor in range(4)]
+    def each(start, count, gap, phi_of):
+        def body(turn, carry):
+            group(start + gap * turn, phi_of(turn))
+            return carry
+
+        lax.fori_loop(0, count, body, 0)
+
+    each(0, 2, 1, lambda turn: first_ref.at[turn])
+    group(2, second_ref)
+
+    @pl.when(paired)
+    def _():
+        each(6, 2, 1, lambda turn: first_ref.at[turn])
+        group(4, second_ref)
+        late[0].wait()
+        each(3, 2, 2, lambda turn: late_ref.at[0])
+
+    @pl.when(jnp.logical_not(paired))
+    def _():
+        late[0].wait()
+        group(3, late_ref.at[0])
+        for step in (1, 2):
+            late[step].wait()
+            each(3 + step, 2, 2, lambda turn, step=step: late_ref.at[step])
+
     for pair in range(ROWS):
         even, odd = [], []
         for node in range(4 * pair, 4 * pair + 4):
@@ -331,22 +379,24 @@
 def per_device(partial_density, node_index, node_weight, node_slope, kernel_table):
     table = cas_table()
     cas = split_constant(table)
-    cas_two = jnp.concatenate([cas, split_row(table[wave_order()])], axis=0)
+    half = half_table()
     x_order = np.arange(N).reshape(16, 8).T.reshape(-1)
     cas_x = split_constant(table[x_order])
-    partner = [(i, i ^ 1) for i in range(16)]
     axes = ("band", "grid")
     f32 = jnp.float32
 
-    phi_far = pl.pallas_call(
+    phi_first, phi_far = pl.pallas_call(
         phi_kernel,
-        out_shape=pltpu.HBM((GROUPS, PAIRS, 8, N), f32),
+        out_shape=[
+            pltpu.VMEM((2, PAIRS, 8, N), f32),
+            pltpu.HBM((GROUPS, PAIRS, 8, N), f32),
+        ],
         in_specs=[vmem()],
-        out_specs=anywhere(),
+        out_specs=[vmem(), anywhere()],
         scratch_shapes=[
             pltpu.VMEM((PAIR_ROWS, N), f32),
-            pltpu.VMEM((POINTS, N), jnp.int32),
-            pltpu.VMEM((POINTS, N), f32),
+            pltpu.VMEM((PHI_POINTS, N), jnp.int32),
+            pltpu.VMEM((PHI_POINTS, N), f32),
             pltpu.VMEM((8 * PAIR_ROWS, N), f32),
             pltpu.VMEM((2, PAIRS, 8, N), f32),
             pltpu.SemaphoreType.DMA((2,)),
@@ -358,7 +408,7 @@
 
     theta, slope = pl.pallas_call(
         fields_kernel,
-        out_shape=[pltpu.VMEM((HALF_NA, N, N), f32), pltpu.VMEM((NA, 64, N), f32)],
+        out_shape=[pltpu.VMEM((NA, 64, N), f32), pltpu.HBM((NA, 64, N), f32)],
         in_specs=[anywhere()] * 3,
         out_specs=[vmem()] * 2,
         scratch_shapes=[
@@ -371,47 +421,52 @@
         cost_estimate=pl.CostEstimate(flops=10**8, bytes_accessed=2 << 20, transcendentals=0),
         name="fields",
     )(far(node_index), far(node_weight), far(node_slope))
-    parts = lax.all_to_all(partial_density.reshape(16, 64, N), "band", 0, 0, tiled=True)
-    own = jnp.sum(parts, axis=0)
-    own, phi_far, slope, theta = lax.optimization_barrier((own, phi_far, slope, theta))
-    other = lax.ppermute(own, "band", partner)
-    phi, cas_near = pl.pallas_call(
-        load_kernel,
+    rows = pl.pallas_call(
+        sort_kernel,
+        out_shape=pltpu.HBM((16, 64, N), f32),
+        in_specs=[anywhere()],
+        out_specs=anywhere(),
+        scratch_shapes=[
+            pltpu.VMEM((8, N, N), f32),
+            pltpu.VMEM((16, 64, N), f32),
+            pltpu.SemaphoreType.DMA((8,)),
+            pltpu.SemaphoreType.DMA((8,)),
+        ],
+        compiler_params=pltpu.CompilerParams(vmem_limit_bytes=4 << 20),
+        name="sort_rows",
+    )(far(partial_density[0]))
+    parts = lax.all_to_all(rows, "band", 0, 0, tiled=True)
+    parts, phi_first, phi_far, slope, theta = lax.optimization_barrier(
+        (parts, phi_first, phi_far, slope, theta)
+    )
+    lines, phi_second = pl.pallas_call(
+        forward_kernel,
         out_shape=[
-            pltpu.VMEM((NEAR, PAIRS, 8, N), f32),
-            pltpu.VMEM(cas_two.shape, cas_two.dtype),
+            jax.ShapeDtypeStruct((256 * ROWS, N), f32),
+            pltpu.VMEM((PAIRS, 8, N), f32),
         ],
-        in_specs=[anywhere()] * 3,
+        in_specs=[vmem()] * 4 + [anywhere()],
         out_specs=[vmem()] * 2,
-        scratch_shapes=[pltpu.SemaphoreType.DMA((NEAR,)), pltpu.SemaphoreType.DMA],
-        compiler_params=pltpu.CompilerParams(vmem_limit_bytes=2 << 20),
-        cost_estimate=pl.CostEstimate(flops=10**9, bytes_accessed=8 << 20, transcendentals=0),
-        name="load",
-    )(own, far(phi_far), far(cas_two))
-    lines = pl.pallas_call(
-        forward_kernel,
-        out_shape=jax.ShapeDtypeStruct((256 * ROWS, N), f32),
-        in_specs=[vmem()] * 4,
-        out_specs=vmem(),
+        scratch_shapes=[pltpu.SemaphoreType.DMA],
         compiler_params=pltpu.CompilerParams(vmem_limit_bytes=12 << 20),
         name="forward",
-    )(own, other, theta, cas_near)
+    )(parts, theta, cas, split_row(half.T), far(phi_far))
     lines = lax.all_to_all(lines.reshape(256, 1, ROWS * N), axes, 0, 0, tiled=True)
     lines = lines.reshape(256 * ROWS, N)
     lines = pl.pallas_call(
         mix_kernel,
         out_shape=jax.ShapeDtypeStruct((256 * ROWS, N), f32),
-        in_specs=[vmem()] * 4 + [anywhere()],
+        in_specs=[vmem()] * 5 + [anywhere()],
         out_specs=vmem(),
         scratch_shapes=[
             pltpu.VMEM((NA * POINTS, N), f32),
             pltpu.VMEM((NA * POINTS, N), f32),
-            pltpu.VMEM((GROUPS - NEAR, PAIRS, 8, N), f32),
-            pltpu.SemaphoreType.DMA((GROUPS - NEAR,)),
+            pltpu.VMEM((3, PAIRS, 8, N), f32),
+            pltpu.SemaphoreType.DMA((3,)),
         ],
         compiler_params=pltpu.CompilerParams(vmem_limit_bytes=24 << 20),
         name="mix",
-    )(lines, cas_x, twist_table(), phi, far(phi_far))
+    )(lines, cas_x, twist_table(), phi_first, phi_second, far(phi_far))
     lines = lax.all_to_all(lines.reshape(256, 1, ROWS * N), axes, 0, 0, tiled=True)
     lines = lines.reshape(256 * ROWS, N)
     share = pl.pallas_call(
@@ -421,7 +476,7 @@
         out_specs=vmem(),
         compiler_params=pltpu.CompilerParams(vmem_limit_bytes=12 << 20),
         name="inverse",
-    )(lines, slope, cas, split_row(half_table()))
+    )(lines, slope, cas, split_row(half))
     gathered = lax.all_to_all(
         jnp.broadcast_to(share[None], (16, 64, N)), "band", 0, 0, tiled=True
     )

time: 118 us -> 117 us (level)
  waiting for transfers between devices: 8.03 us -> 9.51 us
  starting transfers between devices: 11.3 us -> 10.1 us
    all_to_all x1, waiting for transfers between devices: 8.03 us -> 9.51 us  [per_device(): parts = lax.all_to_all(rows, 'band', 0, 0, tiled=True)]
    pallas_call x4, Pallas kernels: 12 us -> 10.6 us  [the longest x1 5.42 us: per_device(): pl.pallas_call(phi_kernel, out_shape=[pltpu.VMEM((2, PAIRS, 8, N), f32),...]
  transfers between devices with their start and end apart: 2 -> 1, of which waited for: 1 -> 1; matrix products, arithmetic and copies ran while one was open for 0% -> 0% of each run, Pallas kernels for 9% -> 7%
where the time goes in v5:
time: 117 us; the launch traced here: 116 us
  blocking collectives  81.1 us (69%)
  Pallas kernels  15.3 us (13%)
  starting transfers between devices  10.1 us (9%)
  waiting for transfers between devices  9.51 us (8%)
    all_to_all x2, blocking collectives, per_device(): lax.all_to_all(lines.reshape(256, 1, ROWS * N), axes, 0, 0, tiled=True)  59.6 us
    all_to_all x1, blocking collectives, per_device(): lax.all_to_all(jnp.broadcast_to(share[None], (16, 64, N)), 'band', 0, 0,...  21.5 us
    all_to_all x1, starting transfers between devices, per_device(): parts = lax.all_to_all(rows, 'band', 0, 0, tiled=True)  10.1 us
    all_to_all x1, waiting for transfers between devices, per_device(): parts = lax.all_to_all(rows, 'band', 0, 0, tiled=True)  9.51 us
    pallas_call x1, Pallas kernels, per_device(): pl.pallas_call(phi_kernel, out_shape=[pltpu.VMEM((2, PAIRS, 8, N), f32),...  5.42 us
    pallas_call x1, Pallas kernels, per_device(): pl.pallas_call(mix_kernel, out_shape=jax.ShapeDtypeStruct((256 * ROWS, N)...  2.76 us
  transfers between devices with their start and end apart: 1, of which 1 were waited for; matrix products, arithmetic and copies ran while one was open for 0% of the time, Pallas kernels for 7%

profile of v5, /device:TPU:2, one launch (start us, length us, event | category | flops | bytes accessed | tf_op | source)
XLA Modules:
  0.0 116.2 jit_solution(18105152494481328433)
XLA Ops:
  0.0 1.8 %sort_rows.1 = f32[16,64,128]{2,1,0:T(8,128)} custom-call(f32[8,128,128]{2,1,0:T(8,128)} %bitcast.9), custom_call_target="tpu_custom_call" | custom-call | tf_op jit(solution)/shard_map/sort_rows/pallas_call | solution.py:424
  1.8 10.1 %all-to-all-start = ((f32[16,64,128]{2,1,0:T(8,128)}), f32[16,64,128]{2,1,0:T(8,128)S(1)}, u32[]{:S(2)}, u32[]{:S(2)}) async-start(f32[16,64,128]{2,1,0:T(8,128)} %sort_rows.1), calls=%async_computation | async-start | bytes 1048576 | tf_op jit(solution)/shard_map/all_to_all | solution.py:438
  12.0 0.0 copy-start.6
  12.0 2.2 %fields.1 = (f32[20,64,128]{2,1,0:T(8,128)S(1)}, f32[20,64,128]{2,1,0:T(8,128)}) custom-call(s32[8,128,128]{2,1,0:T(8,128)} %index_ref.1, f32[4,8,128,128]{3,2,1,0:T(8,128)} %weight_ref.1, f32[4,8,128,128]{3,2,1,0:T(8,128)} %slope_ref.1), custom_call_target="tpu_custom_call" | custom-call | flops 100000000 | bytes 2097152 | tf_op jit(solution)/shard_map/fields/pallas_call | solution.py:409
  14.2 0.0 copy-done.6
  14.2 0.0 copy-start.1
  14.2 0.0 copy-start.5
  14.2 5.4 %phi.1 = (f32[2,210,8,128]{3,2,1,0:T(8,128)S(1)}, f32[6,210,8,128]{3,2,1,0:T(8,128)}) custom-call(f32[20,20,114]{2,1,0:T(8,128)S(1)} %copy-done.6), custom_call_target="tpu_custom_call" | custom-call | flops 4000000000 | bytes 8388608 | tf_op jit(solution)/shard_map/phi/pallas_call | solution.py:388
  19.6 9.5 %all-to-all-done.parts_ref = f32[16,64,128]{2,1,0:T(8,128)S(1)} async-done(((f32[16,64,128]{2,1,0:T(8,128)}), f32[16,64,128]{2,1,0:T(8,128)S(1)}, u32[]{:S(2)}, u32[]{:S(2)}) %all-to-all-start) | async-done | bytes 524320 | tf_op jit(solution)/shard_map/all_to_all | solution.py:438
  29.2 0.0 copy-done.1
  29.2 0.0 copy-done.5
  29.2 0.0 copy-start.2
  29.2 0.0 copy-start.3
  29.2 1.2 %forward.1 = (f32[1280,128]{1,0:T(8,128)S(1)}, f32[210,8,128]{2,1,0:T(8,128)S(1)}) custom-call(f32[16,64,128]{2,1,0:T(8,128)S(1)} %all-to-all-done.parts_ref, f32[20,64,128]{2,1,0:T(8,128)S(1)} %get-tuple-element.21.coefficient_ref, bf16[256,256]{1,0:T(8,128)(2,1)S(1)} %copy-done.1, bf16[64,128]{1,0:T(8,128)(2,1)S(1)} %copy-done.5, ...), custom_call_target="tpu_custom_call" | custom-call | tf_op jit(solution)/shard_map/forward/pallas_call | solution.py:442
  30.4 31.0 %all_to_all.20 = f32[256,1,640]{2,1,0:T(1,128)S(1)} all-to-all(f32[256,1,640]{2,1,0:T(1,128)S(1)} %bitcast.8), channel_id=1, replica_groups=mesh['band'=16,'grid'=16] {'band','grid'}, dimensions={0} | all-to-all | bytes 1310720 | tf_op jit(solution)/shard_map/all_to_all | solution.py:454
  61.4 0.0 copy-done.2
  61.4 0.0 copy-done.3
  61.4 0.0 copy-start
  61.4 0.0 copy-start.4
  61.4 2.8 %mix.1 = f32[1280,128]{1,0:T(8,128)S(1)} custom-call(f32[1280,128]{1,0:T(8,128)S(1)} %bitcast.6, bf16[256,256]{1,0:T(8,128)(2,1)S(1)} %copy-done.2, f32[128,128]{1,0:T(8,128)S(1)} %copy-done.3, f32[2,210,8,128]{3,2,1,0:T(8,128)S(1)} %get-tuple-element.24.first_ref, f32[210,8,128]{2,1,0:T(8,128)S(1)} %get-tuple-element.25.second_ref, ...), custom_call_target="tpu_custom_call" | custom-call | tf_op jit(solution)/shard_map/mix/pallas_call | solution.py:456
  64.2 28.6 %all_to_all.21 = f32[256,1,640]{2,1,0:T(1,128)S(1)} all-to-all(f32[256,1,640]{2,1,0:T(1,128)S(1)} %bitcast.7), channel_id=1, replica_groups=mesh['band'=16,'grid'=16] {'band','grid'}, dimensions={0} | all-to-all | bytes 1310720 | tf_op jit(solution)/shard_map/all_to_all | solution.py:470
  92.8 0.0 copy-done
  92.8 0.0 copy-done.4
  92.8 1.0 inverse.1
  93.9 21.5 %all_to_all.22.data_ref = f32[16,64,128]{2,1,0:T(8,128)S(1)} all-to-all(f32[16,64,128]{2,1,0:T(8,128)S(1)} %broadcast_in_dim.2), channel_id=1, replica_groups=mesh['band'=16,'grid'=16] {'band'}, dimensions={0} | all-to-all | bytes 1048576 | tf_op jit(solution)/shard_map/all_to_all | solution.py:480
  115.3 0.9 weave.1
  (1 shorter events, 0.0 us)
Async XLA Ops:
  1.8 27.3 %all-to-all-start = ((f32[16,64,128]{2,1,0:T(8,128)}), f32[16,64,128]{2,1,0:T(8,128)S(1)}, u32[]{:S(2)}, u32[]{:S(2)}) async-start(f32[16,64,128]{2,1,0:T(8,128)} %sort_rows.1), calls=%async_computation | async-start | bytes 1048576 | tf_op jit(solution)/shard_map/all_to_all | solution.py:438
  12.0 2.2 %copy-start.6 = (f32[20,20,114]{2,1,0:T(8,128)S(1)}, f32[20,20,114]{2,1,0:T(8,128)}, u32[]{:S(2)}) copy-start(f32[20,20,114]{2,1,0:T(8,128)} %table_ref.1) | copy-start | bytes 547204
  14.2 15.0 %copy-start.1 = (bf16[256,256]{1,0:T(8,128)(2,1)S(1)}, bf16[256,256]{1,0:T(8,128)(2,1)}, u32[]{:S(2)}) copy-start(bf16[256,256]{1,0:T(8,128)(2,1)} %constant.24.cas_ref) | copy-start | bytes 393220
  14.2 15.0 %copy-start.5 = (bf16[64,128]{1,0:T(8,128)(2,1)S(1)}, bf16[64,128]{1,0:T(8,128)(2,1)}, u32[]{:S(2)}) copy-start(bf16[64,128]{1,0:T(8,128)(2,1)} %constant.29.half_ref) | copy-start | bytes 49156
  29.2 32.2 %copy-start.2 = (bf16[256,256]{1,0:T(8,128)(2,1)S(1)}, bf16[256,256]{1,0:T(8,128)(2,1)}, u32[]{:S(2)}) copy-start(bf16[256,256]{1,0:T(8,128)(2,1)} %constant.35.cas_ref) | copy-start | bytes 393220
  29.2 32.2 %copy-start.3 = (f32[128,128]{1,0:T(8,128)S(1)}, f32[128,128]{1,0:T(8,128)}, u32[]{:S(2)}) copy-start(f32[128,128]{1,0:T(8,128)} %constant.13.clone.twist_ref) | copy-start | bytes 196612
  61.4 31.4 %copy-start = (f32[20,64,128]{2,1,0:T(8,128)S(1)}, f32[20,64,128]{2,1,0:T(8,128)}, u32[]{:S(2)}) copy-start(f32[20,64,128]{2,1,0:T(8,128)} %get-tuple-element.26.coefficient_ref) | copy-start | bytes 1966084
  61.4 31.4 %copy-start.4 = (bf16[64,128]{1,0:T(8,128)(2,1)S(1)}, bf16[64,128]{1,0:T(8,128)(2,1)}, u32[]{:S(2)}) copy-start(bf16[64,128]{1,0:T(8,128)(2,1)} %constant.40.half_ref) | copy-start | bytes 49156

commit v6 on v5

--- a/solution.py
+++ b/solution.py
@@ -79,26 +79,19 @@
     return halves_added(jnp.dot(row, parts, preferred_element_type=jnp.float32))
 
 
-def times_block_turned(wide, value):
-    parts = jnp.concatenate(split_value(value), axis=0)
-    parts = jnp.concatenate([parts, parts], axis=1)
-    dims = (((1,), (1,)), ((), ()))
-    return halves_added(
-        lax.dot_general(wide[:N], parts, dims, preferred_element_type=jnp.float32)
-    )
+def shifted_groups(items, group):
+    for bit in (1, 2, 4):
+        moved = group // bit % 2 == 1
+        items = [jnp.where(moved, items[(at + bit) % 8], items[at]) for at in range(8)]
+    return items
 
 
 def turned_groups(items):
-    items = list(items)
     group = lax.broadcasted_iota(jnp.int32, items[0].shape, 1) // 16
-    for bit in (1, 2, 4):
-        upper = group // bit % 2 == 1
-        for at in range(8):
-            if at & bit == 0:
-                first, second = items[at], items[at | bit]
-                items[at] = jnp.where(upper, pltpu.roll(second, bit * 16, 1), first)
-                items[at | bit] = jnp.where(upper, second, pltpu.roll(first, N - bit * 16, 1))
-    return items
+    items = shifted_groups(items, group)
+    items = items[:1] + [pltpu.roll(items[at], at * 16, 1) for at in range(1, 8)]
+    items = shifted_groups(items, group)
+    return [items[-at % 8] for at in range(8)]
 
 
 def node_sum(rel, fields, node):
@@ -216,9 +209,19 @@
         put(plane).wait()
 
 
-def forward_kernel(parts_ref, coefficient_ref, cas_ref, half_ref, far_ref, out_ref, near_ref, sem):
-    copy = pltpu.make_async_copy(far_ref.at[2], near_ref, sem)
-    copy.start()
+def forward_kernel(parts_ref, coefficient_ref, cas_ref, half_ref, far_ref, out_ref, near_ref, sems):
+    paired = lax.axis_index("band") * 2 + lax.axis_index("grid") // 8 != 0
+    copies = [
+        pltpu.make_async_copy(far_ref.at[2 + step], near_ref.at[step], sems.at[step])
+        for step in range(4)
+    ]
+    copies[0].start()
+
+    @pl.when(jnp.logical_not(paired))
+    def _():
+        for copy in copies[1:]:
+            copy.start()
+
     density = parts_ref[0]
     for part in range(1, 16):
         density = density + parts_ref[part]
@@ -232,26 +235,26 @@
             items += [waves[:32], waves[32:]]
         for block, item in enumerate(turned_groups(items)):
             out_ref[pl.ds(block * ROWS + pair, 32, stride=8 * ROWS), :] = item
-    copy.wait()
+    copies[0].wait()
+
+    @pl.when(jnp.logical_not(paired))
+    def _():
+        for copy in copies[1:]:
+            copy.wait()
 
 
 def mix_kernel(
     data_ref, cas_ref, twist_ref, first_ref, second_ref, far_ref, out_ref,
-    spec_ref, mixed_ref, late_ref, sems,
+    spec_ref, mixed_ref, late_ref, sem,
 ):
     cas = cas_ref[...]
     wave_set = lax.axis_index("band") * 2 + lax.axis_index("grid") // 8
     paired = wave_set != 0
-    late = [
-        pltpu.make_async_copy(far_ref.at[3 + step], late_ref.at[step], sems.at[step])
-        for step in range(3)
-    ]
-    late[0].start()
-
-    @pl.when(jnp.logical_not(paired))
+    late = pltpu.make_async_copy(far_ref.at[3], late_ref, sem)
+
+    @pl.when(paired)
     def _():
-        late[1].start()
-        late[2].start()
+        late.start()
 
     twist = [twist_ref[pl.ds(wave_set * 4 + factor, 1), :] for factor in range(4)]
 
@@ -303,22 +306,19 @@
         lax.fori_loop(0, count, body, 0)
 
     each(0, 2, 1, lambda turn: first_ref.at[turn])
-    group(2, second_ref)
+    group(2, second_ref.at[0])
 
     @pl.when(paired)
     def _():
         each(6, 2, 1, lambda turn: first_ref.at[turn])
-        group(4, second_ref)
-        late[0].wait()
-        each(3, 2, 2, lambda turn: late_ref.at[0])
+        group(4, second_ref.at[0])
+        late.wait()
+        each(3, 2, 2, lambda turn: late_ref)
 
     @pl.when(jnp.logical_not(paired))
     def _():
-        late[0].wait()
-        group(3, late_ref.at[0])
-        for step in (1, 2):
-            late[step].wait()
-            each(3 + step, 2, 2, lambda turn, step=step: late_ref.at[step])
+        group(3, second_ref.at[1])
+        each(4, 4, 1, lambda turn: second_ref.at[2 + turn % 2])
 
     for pair in range(ROWS):
         even, odd = [], []
@@ -329,7 +329,7 @@
             near, other = slots[0] - slots[1], slots[2] - slots[3]
             odd += [twist[0] * near + twist[1] * other, twist[2] * near + twist[3] * other]
         for half, rows in enumerate((even, odd)):
-            block = times_block_turned(cas, jnp.concatenate(rows, axis=0))
+            block = times_block(cas[:N], jnp.concatenate(rows, axis=0).T)
             for at in range(8):
                 out_ref[lines(half, pair, at), :] = block[at * 16 : at * 16 + 16]
 
@@ -443,11 +443,11 @@
         forward_kernel,
         out_shape=[
             jax.ShapeDtypeStruct((256 * ROWS, N), f32),
-            pltpu.VMEM((PAIRS, 8, N), f32),
+            pltpu.VMEM((4, PAIRS, 8, N), f32),
         ],
         in_specs=[vmem()] * 4 + [anywhere()],
         out_specs=[vmem()] * 2,
-        scratch_shapes=[pltpu.SemaphoreType.DMA],
+        scratch_shapes=[pltpu.SemaphoreType.DMA((4,))],
         compiler_params=pltpu.CompilerParams(vmem_limit_bytes=12 << 20),
         name="forward",
     )(parts, theta, cas, split_row(half.T), far(phi_far))
@@ -461,8 +461,8 @@
         scratch_shapes=[
             pltpu.VMEM((NA * POINTS, N), f32),
             pltpu.VMEM((NA * POINTS, N), f32),
-            pltpu.VMEM((3, PAIRS, 8, N), f32),
-            pltpu.SemaphoreType.DMA((3,)),
+            pltpu.VMEM((PAIRS, 8, N), f32),
+            pltpu.SemaphoreType.DMA,
         ],
         compiler_params=pltpu.CompilerParams(vmem_limit_bytes=24 << 20),
         name="mix",

time: 117 us -> 116 us (level)
    pallas_call x1, Pallas kernels: 1.21 us -> 2.45 us  [per_device(): pl.pallas_call(forward_kernel, out_shape=[jax.ShapeDtypeStruct((256 * ROW...]
where the time goes in v6:
time: 116 us
  blocking collectives  80.5 us (69%)
  Pallas kernels  15.2 us (13%)
  starting transfers between devices  10.1 us (9%)
  waiting for transfers between devices  9.51 us (8%)
    all_to_all x2, blocking collectives, per_device(): lax.all_to_all(lines.reshape(256, 1, ROWS * N), axes, 0, 0, tiled=True)  59.1 us
    all_to_all x1, blocking collectives, per_device(): lax.all_to_all(jnp.broadcast_to(share[None], (16, 64, N)), 'band', 0, 0,...  21.4 us
    all_to_all x1, starting transfers between devices, per_device(): parts = lax.all_to_all(rows, 'band', 0, 0, tiled=True)  10.1 us
    all_to_all x1, waiting for transfers between devices, per_device(): parts = lax.all_to_all(rows, 'band', 0, 0, tiled=True)  9.51 us
    pallas_call x1, Pallas kernels, per_device(): pl.pallas_call(phi_kernel, out_shape=[pltpu.VMEM((2, PAIRS, 8, N), f32),...  5.42 us
    pallas_call x1, Pallas kernels, per_device(): pl.pallas_call(forward_kernel, out_shape=[jax.ShapeDtypeStruct((256 * ROW...  2.45 us
  transfers between devices with their start and end apart: 1, of which 1 were waited for; matrix products, arithmetic and copies ran while one was open for 0% of the time, Pallas kernels for 7%

profile of v6, /device:TPU:2, one launch (start us, length us, event | category | flops | bytes accessed | tf_op | source)
XLA Modules:
  0.0 115.6 jit_solution(15995661472165171879)
XLA Ops:
  0.0 1.8 %sort_rows.1 = f32[16,64,128]{2,1,0:T(8,128)} custom-call(f32[8,128,128]{2,1,0:T(8,128)} %bitcast.9), custom_call_target="tpu_custom_call" | custom-call | tf_op jit(solution)/shard_map/sort_rows/pallas_call | solution.py:424
  1.8 10.1 %all-to-all-start = ((f32[16,64,128]{2,1,0:T(8,128)}), f32[16,64,128]{2,1,0:T(8,128)S(1)}, u32[]{:S(2)}, u32[]{:S(2)}) async-start(f32[16,64,128]{2,1,0:T(8,128)} %sort_rows.1), calls=%async_computation | async-start | bytes 1048576 | tf_op jit(solution)/shard_map/all_to_all | solution.py:438
  12.0 0.0 copy-start.6
  12.0 2.2 %fields.1 = (f32[20,64,128]{2,1,0:T(8,128)S(1)}, f32[20,64,128]{2,1,0:T(8,128)}) custom-call(s32[8,128,128]{2,1,0:T(8,128)} %index_ref.1, f32[4,8,128,128]{3,2,1,0:T(8,128)} %weight_ref.1, f32[4,8,128,128]{3,2,1,0:T(8,128)} %slope_ref.1), custom_call_target="tpu_custom_call" | custom-call | flops 100000000 | bytes 2097152 | tf_op jit(solution)/shard_map/fields/pallas_call | solution.py:409
  14.2 0.0 copy-done.6
  14.2 0.0 copy-start.1
  14.2 0.0 copy-start.5
  14.2 5.4 %phi.1 = (f32[2,210,8,128]{3,2,1,0:T(8,128)S(1)}, f32[6,210,8,128]{3,2,1,0:T(8,128)}) custom-call(f32[20,20,114]{2,1,0:T(8,128)S(1)} %copy-done.6), custom_call_target="tpu_custom_call" | custom-call | flops 4000000000 | bytes 8388608 | tf_op jit(solution)/shard_map/phi/pallas_call | solution.py:388
  19.6 9.5 %all-to-all-done.parts_ref = f32[16,64,128]{2,1,0:T(8,128)S(1)} async-done(((f32[16,64,128]{2,1,0:T(8,128)}), f32[16,64,128]{2,1,0:T(8,128)S(1)}, u32[]{:S(2)}, u32[]{:S(2)}) %all-to-all-start) | async-done | bytes 524320 | tf_op jit(solution)/shard_map/all_to_all | solution.py:438
  29.2 0.0 copy-done.1
  29.2 0.0 copy-done.5
  29.2 0.0 copy-start.2
  29.2 0.0 copy-start.3
  29.2 2.5 %forward.1 = (f32[1280,128]{1,0:T(8,128)S(1)}, f32[4,210,8,128]{3,2,1,0:T(8,128)S(1)}) custom-call(f32[16,64,128]{2,1,0:T(8,128)S(1)} %all-to-all-done.parts_ref, f32[20,64,128]{2,1,0:T(8,128)S(1)} %get-tuple-element.21.coefficient_ref, bf16[256,256]{1,0:T(8,128)(2,1)S(1)} %copy-done.1, bf16[64,128]{1,0:T(8,128)(2,1)S(1)} %copy-done.5, ...), custom_call_target="tpu_custom_call" | custom-call | tf_op jit(solution)/shard_map/forward/pallas_call | solution.py:442
  31.6 29.8 %all_to_all.20 = f32[256,1,640]{2,1,0:T(1,128)S(1)} all-to-all(f32[256,1,640]{2,1,0:T(1,128)S(1)} %bitcast.8), channel_id=1, replica_groups=mesh['band'=16,'grid'=16] {'band','grid'}, dimensions={0} | all-to-all | bytes 1310720 | tf_op jit(solution)/shard_map/all_to_all | solution.py:454
  61.4 0.0 copy-done.2
  61.4 0.0 copy-done.3
  61.4 0.0 copy-start
  61.4 0.0 copy-start.4
  61.4 1.8 %mix.1 = f32[1280,128]{1,0:T(8,128)S(1)} custom-call(f32[1280,128]{1,0:T(8,128)S(1)} %bitcast.5, bf16[256,256]{1,0:T(8,128)(2,1)S(1)} %copy-done.2, f32[128,128]{1,0:T(8,128)S(1)} %copy-done.3, f32[2,210,8,128]{3,2,1,0:T(8,128)S(1)} %get-tuple-element.24.first_ref, f32[4,210,8,128]{3,2,1,0:T(8,128)S(1)} %get-tuple-element.25.second_ref, ...), custom_call_target="tpu_custom_call" | custom-call | tf_op jit(solution)/shard_map/mix/pallas_call | solution.py:456
  63.2 29.3 %all_to_all.21 = f32[256,1,640]{2,1,0:T(1,128)S(1)} all-to-all(f32[256,1,640]{2,1,0:T(1,128)S(1)} %bitcast.6), channel_id=1, replica_groups=mesh['band'=16,'grid'=16] {'band','grid'}, dimensions={0} | all-to-all | bytes 1310720 | tf_op jit(solution)/shard_map/all_to_all | solution.py:470
  92.5 0.0 copy-done
  92.5 0.0 copy-done.4
  92.5 0.7 inverse.1
  93.3 21.4 %all_to_all.22.data_ref = f32[16,64,128]{2,1,0:T(8,128)S(1)} all-to-all(f32[16,64,128]{2,1,0:T(8,128)S(1)} %broadcast_in_dim.2), channel_id=1, replica_groups=mesh['band'=16,'grid'=16] {'band'}, dimensions={0} | all-to-all | bytes 1048576 | tf_op jit(solution)/shard_map/all_to_all | solution.py:480
  114.7 0.9 weave.1
  (1 shorter events, 0.0 us)
Async XLA Ops:
  1.8 27.3 %all-to-all-start = ((f32[16,64,128]{2,1,0:T(8,128)}), f32[16,64,128]{2,1,0:T(8,128)S(1)}, u32[]{:S(2)}, u32[]{:S(2)}) async-start(f32[16,64,128]{2,1,0:T(8,128)} %sort_rows.1), calls=%async_computation | async-start | bytes 1048576 | tf_op jit(solution)/shard_map/all_to_all | solution.py:438
  12.0 2.2 %copy-start.6 = (f32[20,20,114]{2,1,0:T(8,128)S(1)}, f32[20,20,114]{2,1,0:T(8,128)}, u32[]{:S(2)}) copy-start(f32[20,20,114]{2,1,0:T(8,128)} %table_ref.1) | copy-start | bytes 547204
  14.2 15.0 %copy-start.1 = (bf16[256,256]{1,0:T(8,128)(2,1)S(1)}, bf16[256,256]{1,0:T(8,128)(2,1)}, u32[]{:S(2)}) copy-start(bf16[256,256]{1,0:T(8,128)(2,1)} %constant.24.cas_ref) | copy-start | bytes 393220
  14.2 15.0 %copy-start.5 = (bf16[64,128]{1,0:T(8,128)(2,1)S(1)}, bf16[64,128]{1,0:T(8,128)(2,1)}, u32[]{:S(2)}) copy-start(bf16[64,128]{1,0:T(8,128)(2,1)} %constant.29.half_ref) | copy-start | bytes 49156
  29.2 32.3 %copy-start.2 = (bf16[256,256]{1,0:T(8,128)(2,1)S(1)}, bf16[256,256]{1,0:T(8,128)(2,1)}, u32[]{:S(2)}) copy-start(bf16[256,256]{1,0:T(8,128)(2,1)} %constant.35.cas_ref) | copy-start | bytes 393220
  29.2 32.3 %copy-start.3 = (f32[128,128]{1,0:T(8,128)S(1)}, f32[128,128]{1,0:T(8,128)}, u32[]{:S(2)}) copy-start(f32[128,128]{1,0:T(8,128)} %constant.13.clone.twist_ref) | copy-start | bytes 196612
  61.4 31.1 %copy-start = (f32[20,64,128]{2,1,0:T(8,128)S(1)}, f32[20,64,128]{2,1,0:T(8,128)}, u32[]{:S(2)}) copy-start(f32[20,64,128]{2,1,0:T(8,128)} %get-tuple-element.26.coefficient_ref) | copy-start | bytes 1966084
  61.4 31.1 %copy-start.4 = (bf16[64,128]{1,0:T(8,128)(2,1)S(1)}, bf16[64,128]{1,0:T(8,128)(2,1)}, u32[]{:S(2)}) copy-start(bf16[64,128]{1,0:T(8,128)(2,1)} %constant.40.half_ref) | copy-start | bytes 49156

commit v7 on v6

--- a/solution.py
+++ b/solution.py
@@ -215,11 +215,10 @@
         pltpu.make_async_copy(far_ref.at[2 + step], near_ref.at[step], sems.at[step])
         for step in range(4)
     ]
-    copies[0].start()
 
     @pl.when(jnp.logical_not(paired))
     def _():
-        for copy in copies[1:]:
+        for copy in copies:
             copy.start()
 
     density = parts_ref[0]
@@ -235,26 +234,29 @@
             items += [waves[:32], waves[32:]]
         for block, item in enumerate(turned_groups(items)):
             out_ref[pl.ds(block * ROWS + pair, 32, stride=8 * ROWS), :] = item
-    copies[0].wait()
 
     @pl.when(jnp.logical_not(paired))
     def _():
-        for copy in copies[1:]:
+        for copy in copies:
             copy.wait()
 
 
 def mix_kernel(
     data_ref, cas_ref, twist_ref, first_ref, second_ref, far_ref, out_ref,
-    spec_ref, mixed_ref, late_ref, sem,
+    spec_ref, mixed_ref, late_ref, sems,
 ):
     cas = cas_ref[...]
     wave_set = lax.axis_index("band") * 2 + lax.axis_index("grid") // 8
     paired = wave_set != 0
-    late = pltpu.make_async_copy(far_ref.at[3], late_ref, sem)
+    late = [
+        pltpu.make_async_copy(far_ref.at[2 + step], late_ref.at[step], sems.at[step])
+        for step in range(2)
+    ]
 
     @pl.when(paired)
     def _():
-        late.start()
+        for copy in late:
+            copy.start()
 
     twist = [twist_ref[pl.ds(wave_set * 4 + factor, 1), :] for factor in range(4)]
 
@@ -306,18 +308,17 @@
         lax.fori_loop(0, count, body, 0)
 
     each(0, 2, 1, lambda turn: first_ref.at[turn])
-    group(2, second_ref.at[0])
 
     @pl.when(paired)
     def _():
         each(6, 2, 1, lambda turn: first_ref.at[turn])
-        group(4, second_ref.at[0])
-        late.wait()
-        each(3, 2, 2, lambda turn: late_ref)
+        for step in range(2):
+            late[step].wait()
+            each(2 + step, 2, 2, lambda turn, step=step: late_ref.at[step])
 
     @pl.when(jnp.logical_not(paired))
     def _():
-        group(3, second_ref.at[1])
+        each(2, 2, 1, lambda turn: second_ref.at[turn])
         each(4, 4, 1, lambda turn: second_ref.at[2 + turn % 2])
 
     for pair in range(ROWS):
@@ -461,8 +462,8 @@
         scratch_shapes=[
             pltpu.VMEM((NA * POINTS, N), f32),
             pltpu.VMEM((NA * POINTS, N), f32),
-            pltpu.VMEM((PAIRS, 8, N), f32),
-            pltpu.SemaphoreType.DMA,
+            pltpu.VMEM((2, PAIRS, 8, N), f32),
+            pltpu.SemaphoreType.DMA((2,)),
         ],
         compiler_params=pltpu.CompilerParams(vmem_limit_bytes=24 << 20),
         name="mix",

time: 116 us -> 116 us (level)
  no operation moved by 1% of the time
where the time goes in v7:
time: 116 us; the launch traced here: 115 us
  blocking collectives  80.1 us (69%)
  Pallas kernels  15.4 us (13%)
  starting transfers between devices  10.1 us (9%)
  waiting for transfers between devices  9.51 us (8%)
    all_to_all x2, blocking collectives, per_device(): lax.all_to_all(lines.reshape(256, 1, ROWS * N), axes, 0, 0, tiled=True)  58.7 us
    all_to_all x1, blocking collectives, per_device(): lax.all_to_all(jnp.broadcast_to(share[None], (16, 64, N)), 'band', 0, 0,...  21.5 us
    all_to_all x1, starting transfers between devices, per_device(): parts = lax.all_to_all(rows, 'band', 0, 0, tiled=True)  10.1 us
    all_to_all x1, waiting for transfers between devices, per_device(): parts = lax.all_to_all(rows, 'band', 0, 0, tiled=True)  9.51 us
    pallas_call x1, Pallas kernels, per_device(): pl.pallas_call(phi_kernel, out_shape=[pltpu.VMEM((2, PAIRS, 8, N), f32),...  5.42 us
    pallas_call x1, Pallas kernels, per_device(): pl.pallas_call(forward_kernel, out_shape=[jax.ShapeDtypeStruct((256 * ROW...  2.65 us
  transfers between devices with their start and end apart: 1, of which 1 were waited for; matrix products, arithmetic and copies ran while one was open for 0% of the time, Pallas kernels for 7%

profile of v7, /device:TPU:2, one launch (start us, length us, event | category | flops | bytes accessed | tf_op | source)
XLA Modules:
  0.0 115.4 jit_solution(741633676254217697)
XLA Ops:
  0.0 1.8 %sort_rows.1 = f32[16,64,128]{2,1,0:T(8,128)} custom-call(f32[8,128,128]{2,1,0:T(8,128)} %bitcast.9), custom_call_target="tpu_custom_call" | custom-call | tf_op jit(solution)/shard_map/sort_rows/pallas_call | solution.py:425
  1.8 10.1 %all-to-all-start = ((f32[16,64,128]{2,1,0:T(8,128)}), f32[16,64,128]{2,1,0:T(8,128)S(1)}, u32[]{:S(2)}, u32[]{:S(2)}) async-start(f32[16,64,128]{2,1,0:T(8,128)} %sort_rows.1), calls=%async_computation | async-start | bytes 1048576 | tf_op jit(solution)/shard_map/all_to_all | solution.py:439
  12.0 0.0 copy-start.6
  12.0 2.2 %fields.1 = (f32[20,64,128]{2,1,0:T(8,128)S(1)}, f32[20,64,128]{2,1,0:T(8,128)}) custom-call(s32[8,128,128]{2,1,0:T(8,128)} %index_ref.1, f32[4,8,128,128]{3,2,1,0:T(8,128)} %weight_ref.1, f32[4,8,128,128]{3,2,1,0:T(8,128)} %slope_ref.1), custom_call_target="tpu_custom_call" | custom-call | flops 100000000 | bytes 2097152 | tf_op jit(solution)/shard_map/fields/pallas_call | solution.py:410
  14.2 0.0 copy-done.6
  14.2 0.0 copy-start.1
  14.2 0.0 copy-start.5
  14.2 5.4 %phi.1 = (f32[2,210,8,128]{3,2,1,0:T(8,128)S(1)}, f32[6,210,8,128]{3,2,1,0:T(8,128)}) custom-call(f32[20,20,114]{2,1,0:T(8,128)S(1)} %copy-done.6), custom_call_target="tpu_custom_call" | custom-call | flops 4000000000 | bytes 8388608 | tf_op jit(solution)/shard_map/phi/pallas_call | solution.py:389
  19.6 9.5 %all-to-all-done.parts_ref = f32[16,64,128]{2,1,0:T(8,128)S(1)} async-done(((f32[16,64,128]{2,1,0:T(8,128)}), f32[16,64,128]{2,1,0:T(8,128)S(1)}, u32[]{:S(2)}, u32[]{:S(2)}) %all-to-all-start) | async-done | bytes 524320 | tf_op jit(solution)/shard_map/all_to_all | solution.py:439
  29.2 0.0 copy-done.1
  29.2 0.0 copy-done.5
  29.2 0.0 copy-start.2
  29.2 0.0 copy-start.3
  29.2 2.6 %forward.1 = (f32[1280,128]{1,0:T(8,128)S(1)}, f32[4,210,8,128]{3,2,1,0:T(8,128)S(1)}) custom-call(f32[16,64,128]{2,1,0:T(8,128)S(1)} %all-to-all-done.parts_ref, f32[20,64,128]{2,1,0:T(8,128)S(1)} %get-tuple-element.21.coefficient_ref, bf16[256,256]{1,0:T(8,128)(2,1)S(1)} %copy-done.1, bf16[64,128]{1,0:T(8,128)(2,1)S(1)} %copy-done.5, ...), custom_call_target="tpu_custom_call" | custom-call | tf_op jit(solution)/shard_map/forward/pallas_call | solution.py:443
  31.8 29.1 %all_to_all.20 = f32[256,1,640]{2,1,0:T(1,128)S(1)} all-to-all(f32[256,1,640]{2,1,0:T(1,128)S(1)} %bitcast.8), channel_id=1, replica_groups=mesh['band'=16,'grid'=16] {'band','grid'}, dimensions={0} | all-to-all | bytes 1310720 | tf_op jit(solution)/shard_map/all_to_all | solution.py:455
  61.0 0.0 copy-done.2
  61.0 0.0 copy-done.3
  61.0 0.0 copy-start
  61.0 0.0 copy-start.4
  61.0 1.8 %mix.1 = f32[1280,128]{1,0:T(8,128)S(1)} custom-call(f32[1280,128]{1,0:T(8,128)S(1)} %bitcast.5, bf16[256,256]{1,0:T(8,128)(2,1)S(1)} %copy-done.2, f32[128,128]{1,0:T(8,128)S(1)} %copy-done.3, f32[2,210,8,128]{3,2,1,0:T(8,128)S(1)} %get-tuple-element.24.first_ref, f32[4,210,8,128]{3,2,1,0:T(8,128)S(1)} %get-tuple-element.25.second_ref, ...), custom_call_target="tpu_custom_call" | custom-call | tf_op jit(solution)/shard_map/mix/pallas_call | solution.py:457
  62.8 29.5 %all_to_all.21 = f32[256,1,640]{2,1,0:T(1,128)S(1)} all-to-all(f32[256,1,640]{2,1,0:T(1,128)S(1)} %bitcast.6), channel_id=1, replica_groups=mesh['band'=16,'grid'=16] {'band','grid'}, dimensions={0} | all-to-all | bytes 1310720 | tf_op jit(solution)/shard_map/all_to_all | solution.py:471
  92.3 0.0 copy-done
  92.3 0.0 copy-done.4
  92.3 0.7 inverse.1
  93.1 21.5 %all_to_all.22.data_ref = f32[16,64,128]{2,1,0:T(8,128)S(1)} all-to-all(f32[16,64,128]{2,1,0:T(8,128)S(1)} %broadcast_in_dim.2), channel_id=1, replica_groups=mesh['band'=16,'grid'=16] {'band'}, dimensions={0} | all-to-all | bytes 1048576 | tf_op jit(solution)/shard_map/all_to_all | solution.py:481
  114.5 0.9 weave.1
  (1 shorter events, 0.0 us)
Async XLA Ops:
  1.8 27.3 %all-to-all-start = ((f32[16,64,128]{2,1,0:T(8,128)}), f32[16,64,128]{2,1,0:T(8,128)S(1)}, u32[]{:S(2)}, u32[]{:S(2)}) async-start(f32[16,64,128]{2,1,0:T(8,128)} %sort_rows.1), calls=%async_computation | async-start | bytes 1048576 | tf_op jit(solution)/shard_map/all_to_all | solution.py:439
  12.0 2.2 %copy-start.6 = (f32[20,20,114]{2,1,0:T(8,128)S(1)}, f32[20,20,114]{2,1,0:T(8,128)}, u32[]{:S(2)}) copy-start(f32[20,20,114]{2,1,0:T(8,128)} %table_ref.1) | copy-start | bytes 547204
  14.2 15.0 %copy-start.1 = (bf16[256,256]{1,0:T(8,128)(2,1)S(1)}, bf16[256,256]{1,0:T(8,128)(2,1)}, u32[]{:S(2)}) copy-start(bf16[256,256]{1,0:T(8,128)(2,1)} %constant.24.cas_ref) | copy-start | bytes 393220
  14.2 15.0 %copy-start.5 = (bf16[64,128]{1,0:T(8,128)(2,1)S(1)}, bf16[64,128]{1,0:T(8,128)(2,1)}, u32[]{:S(2)}) copy-start(bf16[64,128]{1,0:T(8,128)(2,1)} %constant.29.half_ref) | copy-start | bytes 49156
  29.2 31.8 %copy-start.2 = (bf16[256,256]{1,0:T(8,128)(2,1)S(1)}, bf16[256,256]{1,0:T(8,128)(2,1)}, u32[]{:S(2)}) copy-start(bf16[256,256]{1,0:T(8,128)(2,1)} %constant.35.cas_ref) | copy-start | bytes 393220
  29.2 31.8 %copy-start.3 = (f32[128,128]{1,0:T(8,128)S(1)}, f32[128,128]{1,0:T(8,128)}, u32[]{:S(2)}) copy-start(f32[128,128]{1,0:T(8,128)} %constant.13.clone.twist_ref) | copy-start | bytes 196612
  61.0 31.3 %copy-start = (f32[20,64,128]{2,1,0:T(8,128)S(1)}, f32[20,64,128]{2,1,0:T(8,128)}, u32[]{:S(2)}) copy-start(f32[20,64,128]{2,1,0:T(8,128)} %get-tuple-element.26.coefficient_ref) | copy-start | bytes 1966084
  61.0 31.3 %copy-start.4 = (bf16[64,128]{1,0:T(8,128)(2,1)S(1)}, bf16[64,128]{1,0:T(8,128)(2,1)}, u32[]{:S(2)}) copy-start(bf16[64,128]{1,0:T(8,128)(2,1)} %constant.40.half_ref) | copy-start | bytes 49156

commit v8 on v7

--- a/solution.py
+++ b/solution.py
@@ -213,7 +213,7 @@
     paired = lax.axis_index("band") * 2 + lax.axis_index("grid") // 8 != 0
     copies = [
         pltpu.make_async_copy(far_ref.at[2 + step], near_ref.at[step], sems.at[step])
-        for step in range(4)
+        for step in range(2)
     ]
 
     @pl.when(jnp.logical_not(paired))
@@ -248,15 +248,13 @@
     cas = cas_ref[...]
     wave_set = lax.axis_index("band") * 2 + lax.axis_index("grid") // 8
     paired = wave_set != 0
+    last = jnp.where(paired, 2, 4)
     late = [
-        pltpu.make_async_copy(far_ref.at[2 + step], late_ref.at[step], sems.at[step])
+        pltpu.make_async_copy(far_ref.at[last + step], late_ref.at[step], sems.at[step])
         for step in range(2)
     ]
-
-    @pl.when(paired)
-    def _():
-        for copy in late:
-            copy.start()
+    for copy in late:
+        copy.start()
 
     twist = [twist_ref[pl.ds(wave_set * 4 + factor, 1), :] for factor in range(4)]
 
@@ -312,14 +310,14 @@
     @pl.when(paired)
     def _():
         each(6, 2, 1, lambda turn: first_ref.at[turn])
-        for step in range(2):
-            late[step].wait()
-            each(2 + step, 2, 2, lambda turn, step=step: late_ref.at[step])
 
     @pl.when(jnp.logical_not(paired))
     def _():
         each(2, 2, 1, lambda turn: second_ref.at[turn])
-        each(4, 4, 1, lambda turn: second_ref.at[2 + turn % 2])
+
+    for step in range(2):
+        late[step].wait()
+        each(last + step, 2, 2, lambda turn, step=step: late_ref.at[step])
 
     for pair in range(ROWS):
         even, odd = [], []
@@ -444,11 +442,11 @@
         forward_kernel,
         out_shape=[
             jax.ShapeDtypeStruct((256 * ROWS, N), f32),
-            pltpu.VMEM((4, PAIRS, 8, N), f32),
+            pltpu.VMEM((2, PAIRS, 8, N), f32),
         ],
         in_specs=[vmem()] * 4 + [anywhere()],
         out_specs=[vmem()] * 2,
-        scratch_shapes=[pltpu.SemaphoreType.DMA((4,))],
+        scratch_shapes=[pltpu.SemaphoreType.DMA((2,))],
         compiler_params=pltpu.CompilerParams(vmem_limit_bytes=12 << 20),
         name="forward",
     )(parts, theta, cas, split_row(half.T), far(phi_far))

time: 116 us -> 116 us (level)
  no operation moved by 1% of the time
where the time goes in v8:
time: 116 us; the launch traced here: 115 us
  blocking collectives  80.1 us (69%)
  Pallas kernels  15.4 us (13%)
  starting transfers between devices  10.1 us (9%)
  waiting for transfers between devices  9.51 us (8%)
    all_to_all x2, blocking collectives, per_device(): lax.all_to_all(lines.reshape(256, 1, ROWS * N), axes, 0, 0, tiled=True)  58.6 us
    all_to_all x1, blocking collectives, per_device(): lax.all_to_all(jnp.broadcast_to(share[None], (16, 64, N)), 'band', 0, 0,...  21.5 us
    all_to_all x1, starting transfers between devices, per_device(): parts = lax.all_to_all(rows, 'band', 0, 0, tiled=True)  10.1 us
    all_to_all x1, waiting for transfers between devices, per_device(): parts = lax.all_to_all(rows, 'band', 0, 0, tiled=True)  9.51 us
    pallas_call x1, Pallas kernels, per_device(): pl.pallas_call(phi_kernel, out_shape=[pltpu.VMEM((2, PAIRS, 8, N), f32),...  5.42 us
    pallas_call x1, Pallas kernels, per_device(): pl.pallas_call(mix_kernel, out_shape=jax.ShapeDtypeStruct((256 * ROWS, N)...  2.35 us
  transfers between devices with their start and end apart: 1, of which 1 were waited for; matrix products, arithmetic and copies ran while one was open for 0% of the time, Pallas kernels for 7%

profile of v8, /device:TPU:2, one launch (start us, length us, event | category | flops | bytes accessed | tf_op | source)
XLA Modules:
  0.0 115.4 jit_solution(10939286431892005478)
XLA Ops:
  0.0 1.8 %sort_rows.1 = f32[16,64,128]{2,1,0:T(8,128)} custom-call(f32[8,128,128]{2,1,0:T(8,128)} %bitcast.9), custom_call_target="tpu_custom_call" | custom-call | tf_op jit(solution)/shard_map/sort_rows/pallas_call | solution.py:423
  1.8 10.1 %all-to-all-start = ((f32[16,64,128]{2,1,0:T(8,128)}), f32[16,64,128]{2,1,0:T(8,128)S(1)}, u32[]{:S(2)}, u32[]{:S(2)}) async-start(f32[16,64,128]{2,1,0:T(8,128)} %sort_rows.1), calls=%async_computation | async-start | bytes 1048576 | tf_op jit(solution)/shard_map/all_to_all | solution.py:437
  12.0 0.0 copy-start.6
  12.0 2.2 %fields.1 = (f32[20,64,128]{2,1,0:T(8,128)S(1)}, f32[20,64,128]{2,1,0:T(8,128)}) custom-call(s32[8,128,128]{2,1,0:T(8,128)} %index_ref.1, f32[4,8,128,128]{3,2,1,0:T(8,128)} %weight_ref.1, f32[4,8,128,128]{3,2,1,0:T(8,128)} %slope_ref.1), custom_call_target="tpu_custom_call" | custom-call | flops 100000000 | bytes 2097152 | tf_op jit(solution)/shard_map/fields/pallas_call | solution.py:408
  14.2 0.0 copy-done.6
  14.2 0.0 copy-start.1
  14.2 0.0 copy-start.5
  14.2 5.4 %phi.1 = (f32[2,210,8,128]{3,2,1,0:T(8,128)S(1)}, f32[6,210,8,128]{3,2,1,0:T(8,128)}) custom-call(f32[20,20,114]{2,1,0:T(8,128)S(1)} %copy-done.6), custom_call_target="tpu_custom_call" | custom-call | flops 4000000000 | bytes 8388608 | tf_op jit(solution)/shard_map/phi/pallas_call | solution.py:387
  19.6 9.5 %all-to-all-done.parts_ref = f32[16,64,128]{2,1,0:T(8,128)S(1)} async-done(((f32[16,64,128]{2,1,0:T(8,128)}), f32[16,64,128]{2,1,0:T(8,128)S(1)}, u32[]{:S(2)}, u32[]{:S(2)}) %all-to-all-start) | async-done | bytes 524320 | tf_op jit(solution)/shard_map/all_to_all | solution.py:437
  29.2 0.0 copy-done.1
  29.2 0.0 copy-done.5
  29.2 0.0 copy-start.2
  29.2 0.0 copy-start.3
  29.2 2.1 %forward.1 = (f32[1280,128]{1,0:T(8,128)S(1)}, f32[2,210,8,128]{3,2,1,0:T(8,128)S(1)}) custom-call(f32[16,64,128]{2,1,0:T(8,128)S(1)} %all-to-all-done.parts_ref, f32[20,64,128]{2,1,0:T(8,128)S(1)} %get-tuple-element.21.coefficient_ref, bf16[256,256]{1,0:T(8,128)(2,1)S(1)} %copy-done.1, bf16[64,128]{1,0:T(8,128)(2,1)S(1)} %copy-done.5, ...), custom_call_target="tpu_custom_call" | custom-call | tf_op jit(solution)/shard_map/forward/pallas_call | solution.py:441
  31.3 29.7 %all_to_all.20 = f32[256,1,640]{2,1,0:T(1,128)S(1)} all-to-all(f32[256,1,640]{2,1,0:T(1,128)S(1)} %bitcast.8), channel_id=1, replica_groups=mesh['band'=16,'grid'=16] {'band','grid'}, dimensions={0} | all-to-all | bytes 1310720 | tf_op jit(solution)/shard_map/all_to_all | solution.py:453
  61.0 0.0 copy-done.2
  61.0 0.0 copy-done.3
  61.0 0.0 copy-start
  61.0 0.0 copy-start.4
  61.0 2.4 %mix.1 = f32[1280,128]{1,0:T(8,128)S(1)} custom-call(f32[1280,128]{1,0:T(8,128)S(1)} %bitcast.5, bf16[256,256]{1,0:T(8,128)(2,1)S(1)} %copy-done.2, f32[128,128]{1,0:T(8,128)S(1)} %copy-done.3, f32[2,210,8,128]{3,2,1,0:T(8,128)S(1)} %get-tuple-element.24.first_ref, f32[2,210,8,128]{3,2,1,0:T(8,128)S(1)} %get-tuple-element.25.second_ref, ...), custom_call_target="tpu_custom_call" | custom-call | tf_op jit(solution)/shard_map/mix/pallas_call | solution.py:455
  63.3 29.0 %all_to_all.21 = f32[256,1,640]{2,1,0:T(1,128)S(1)} all-to-all(f32[256,1,640]{2,1,0:T(1,128)S(1)} %bitcast.6), channel_id=1, replica_groups=mesh['band'=16,'grid'=16] {'band','grid'}, dimensions={0} | all-to-all | bytes 1310720 | tf_op jit(solution)/shard_map/all_to_all | solution.py:469
  92.3 0.0 copy-done
  92.3 0.0 copy-done.4
  92.3 0.7 inverse.1
  93.0 21.5 %all_to_all.22.data_ref = f32[16,64,128]{2,1,0:T(8,128)S(1)} all-to-all(f32[16,64,128]{2,1,0:T(8,128)S(1)} %broadcast_in_dim.2), channel_id=1, replica_groups=mesh['band'=16,'grid'=16] {'band'}, dimensions={0} | all-to-all | bytes 1048576 | tf_op jit(solution)/shard_map/all_to_all | solution.py:479
  114.5 0.9 weave.1
  (1 shorter events, 0.0 us)
Async XLA Ops:
  1.8 27.3 %all-to-all-start = ((f32[16,64,128]{2,1,0:T(8,128)}), f32[16,64,128]{2,1,0:T(8,128)S(1)}, u32[]{:S(2)}, u32[]{:S(2)}) async-start(f32[16,64,128]{2,1,0:T(8,128)} %sort_rows.1), calls=%async_computation | async-start | bytes 1048576 | tf_op jit(solution)/shard_map/all_to_all | solution.py:437
  12.0 2.2 %copy-start.6 = (f32[20,20,114]{2,1,0:T(8,128)S(1)}, f32[20,20,114]{2,1,0:T(8,128)}, u32[]{:S(2)}) copy-start(f32[20,20,114]{2,1,0:T(8,128)} %table_ref.1) | copy-start | bytes 547204
  14.2 15.0 %copy-start.1 = (bf16[256,256]{1,0:T(8,128)(2,1)S(1)}, bf16[256,256]{1,0:T(8,128)(2,1)}, u32[]{:S(2)}) copy-start(bf16[256,256]{1,0:T(8,128)(2,1)} %constant.24.cas_ref) | copy-start | bytes 393220
  14.2 15.0 %copy-start.5 = (bf16[64,128]{1,0:T(8,128)(2,1)S(1)}, bf16[64,128]{1,0:T(8,128)(2,1)}, u32[]{:S(2)}) copy-start(bf16[64,128]{1,0:T(8,128)(2,1)} %constant.29.half_ref) | copy-start | bytes 49156
  29.2 31.8 %copy-start.2 = (bf16[256,256]{1,0:T(8,128)(2,1)S(1)}, bf16[256,256]{1,0:T(8,128)(2,1)}, u32[]{:S(2)}) copy-start(bf16[256,256]{1,0:T(8,128)(2,1)} %constant.35.cas_ref) | copy-start | bytes 393220
  29.2 31.8 %copy-start.3 = (f32[128,128]{1,0:T(8,128)S(1)}, f32[128,128]{1,0:T(8,128)}, u32[]{:S(2)}) copy-start(f32[128,128]{1,0:T(8,128)} %constant.13.clone.twist_ref) | copy-start | bytes 196612
  61.0 31.3 %copy-start = (f32[20,64,128]{2,1,0:T(8,128)S(1)}, f32[20,64,128]{2,1,0:T(8,128)}, u32[]{:S(2)}) copy-start(f32[20,64,128]{2,1,0:T(8,128)} %get-tuple-element.26.coefficient_ref) | copy-start | bytes 1966084
  61.0 31.3 %copy-start.4 = (bf16[64,128]{1,0:T(8,128)(2,1)S(1)}, bf16[64,128]{1,0:T(8,128)(2,1)}, u32[]{:S(2)}) copy-start(bf16[64,128]{1,0:T(8,128)(2,1)} %constant.40.half_ref) | copy-start | bytes 49156
